TPU v7x, 32 devices: a whole 2x2x4 slice. The times are simulated.
32 devices in a mesh: width: 4 (over x, core), tok: 8 (over z, y).
Axes of the slice: x: 2, y: 2, z: 4, core: 2. Of those that a mesh axis runs over, the one named last changes fastest.
Arguments:
- tokens_in: bfloat16 [8192, 768], P('tok'), may hold values from -6 to 6
- seq_lengths: int32 [8, 24], P('tok'), may hold values from 1 to 512, 992 in all within a row
- query_weight: bfloat16 [768, 768], P(('width', 'tok')), may hold values from -0.21875 to 0.21875
- key_weight: bfloat16 [768, 768], P(('width', 'tok')), may hold values from -0.21875 to 0.21875
- value_weight: bfloat16 [768, 768], P(('width', 'tok')), may hold values from -0.21875 to 0.21875
- output_weight: bfloat16 [768, 768], P(('width', 'tok')), may hold values from -0.625 to 0.625
- expand_weight: bfloat16 [3072, 768], P(('width', 'tok')), may hold values from -0.21875 to 0.21875
- shrink_weight: bfloat16 [3072, 768], P(('width', 'tok')), may hold values from -0.109375 to 0.109375
- query_bias: bfloat16 [768], P(('width', 'tok')), may hold values from -1.796875 to 1.796875
- value_bias: bfloat16 [768], P(('width', 'tok')), may hold values from -1.796875 to 1.796875
- output_bias: bfloat16 [768], P(('width', 'tok')), may hold values from -1.796875 to 1.796875
- expand_bias: bfloat16 [3072], P(('width', 'tok')), may hold values from -1.796875 to 1.796875
- shrink_bias: bfloat16 [768], P(('width', 'tok')), may hold values from -1.796875 to 1.796875
- first_gain: bfloat16 [768], P(('width', 'tok')), may hold values from 0.5 to 1.5
- first_shift: bfloat16 [768], P(('width', 'tok')), may hold values from -1.796875 to 1.796875
- second_gain: bfloat16 [768], P(('width', 'tok')), may hold values from 0.5 to 1.5
- second_shift: bfloat16 [768], P(('width', 'tok')), may hold values from -1.796875 to 1.796875
- out_grad: bfloat16 [4, 8192, 768], P('width', 'tok'), may hold values from -6 to 6
Outputs:
- layer_out: bfloat16 [4, 8192, 768], P('width', 'tok')
- input_grad: float32 [4, 8192, 768], P('width', 'tok')
- query_weight_grad: float32 [768, 768], P(('width', 'tok'))
- key_weight_grad: float32 [768, 768], P(('width', 'tok'))
- value_weight_grad: float32 [768, 768], P(('width', 'tok'))
- output_weight_grad: float32 [768, 768], P(('width', 'tok'))
- expand_weight_grad: float32 [3072, 768], P(('width', 'tok'))
- shrink_weight_grad: float32 [3072, 768], P(('width', 'tok'))
- query_bias_grad: float32 [768], P(('width', 'tok'))
- value_bias_grad: float32 [768], P(('width', 'tok'))
- output_bias_grad: float32 [768], P(('width', 'tok'))
- expand_bias_grad: float32 [3072], P(('width', 'tok'))
- shrink_bias_grad: float32 [768], P(('width', 'tok'))
- first_gain_grad: float32 [768], P(('width', 'tok'))
- first_shift_grad: float32 [768], P(('width', 'tok'))
- second_gain_grad: float32 [768], P(('width', 'tok'))
- second_shift_grad: float32 [768], P(('width', 'tok'))
Inputs may be any that keep to these rules, and one draw needn't show every extreme that they name: `seq_lengths`: each tok shard's 24 lengths sum to 992, and the longest of each shard is exactly 512; a shard's sequences lie end to end from its first slot, and its last 32 slots are padding.
All inputs are finite; a program needn't handle non-finite values.
Results may differ from a plain program's by a relative error of at most 0.017.
Values may be sent and summed in bfloat16 or wider, within the bound.
A program may use at most 320 MiB of HBM per device.

v0:
```python
from functools import partial
import math

import jax
import jax.numpy as jnp
from jax import lax
from jax.sharding import PartitionSpec as P

HEADS = 12
HEAD_DIM = 64


norm_eps = 1e-12


def shortened(value):

    def short(part):
        return part.astype(jnp.bfloat16) if part.dtype == jnp.float32 else part

    return jax.tree.map(short, value)


def dot_rows(left, right):
    return lax.dot_general(
        left, right, (((1,), (1,)), ((), ())), preferred_element_type=jnp.float32
    )


def dot_cols(left, right):
    return lax.dot_general(
        left, right, (((0,), (0,)), ((), ())), preferred_element_type=jnp.float32
    )


def dot_plain(left, right):
    return jnp.dot(left, right, preferred_element_type=jnp.float32)


def layer_norm(value, gain, shift):
    average = jnp.mean(value, axis=-1, keepdims=True)
    centred = value - average
    variance = jnp.mean(centred * centred, axis=-1, keepdims=True)
    return centred * lax.rsqrt(variance + norm_eps) * gain + shift


def gelu_exact(value):
    return jax.nn.gelu(value, approximate=False)


def column_sum(value):
    return jnp.sum(value.astype(jnp.float32), axis=0)


def widen(value, full_rows):
    padding = ((0, full_rows - value.shape[0]),) + ((0, 0),) * (value.ndim - 1)
    return jnp.pad(value, padding)


def masked_scores(query_rows, key_heads, segment, lower, block_rows, head_count):
    query_heads = query_rows[lower : lower + block_rows].reshape(block_rows, head_count, HEAD_DIM)
    scores = jnp.einsum("qhd,khd->hqk", query_heads, key_heads, preferred_element_type=jnp.float32)
    scores = scores * (1.0 / math.sqrt(HEAD_DIM))
    allowed = segment[lower : lower + block_rows][:, None] == segment[None, :]
    return (query_heads, jnp.where(allowed[None], scores, -1e30))


def attend(query_rows, key_rows, value_rows, segment, head_count):
    length = query_rows.shape[0]
    block_rows = min(512, length)
    key_heads = key_rows.reshape(length, head_count, HEAD_DIM)
    value_heads = value_rows.reshape(length, head_count, HEAD_DIM)
    contexts = []
    logsums = []
    for block_index in range(length // block_rows):
        lower = block_index * block_rows
        unused, scores = masked_scores(
            query_rows, key_heads, segment, lower, block_rows, head_count
        )
        row_peak = jnp.max(scores, axis=-1, keepdims=True)
        unscaled = jnp.exp(scores - row_peak)
        row_total = jnp.sum(unscaled, axis=-1, keepdims=True)
        prob_low = (unscaled / row_total).astype(jnp.bfloat16)
        context = jnp.einsum(
            "hqk,khd->qhd", prob_low, value_heads, preferred_element_type=jnp.float32
        )
        contexts.append(context.reshape(block_rows, head_count * HEAD_DIM).astype(jnp.bfloat16))
        logsums.append(row_peak + jnp.log(row_total))
    return (jnp.concatenate(contexts, axis=0), jnp.concatenate(logsums, axis=1))


def attend_back(query_rows, key_rows, value_rows, segment, logsums, context_grad, head_count):
    length = query_rows.shape[0]
    block_rows = min(512, length)
    score_scale = 1.0 / math.sqrt(HEAD_DIM)
    key_heads = key_rows.reshape(length, head_count, HEAD_DIM)
    value_heads = value_rows.reshape(length, head_count, HEAD_DIM)
    key_total = jnp.zeros((length, head_count, HEAD_DIM), jnp.float32)
    value_total = jnp.zeros((length, head_count, HEAD_DIM), jnp.float32)
    query_parts = []
    for block_index in range(length // block_rows):
        lower = block_index * block_rows
        query_heads, scores = masked_scores(
            query_rows, key_heads, segment, lower, block_rows, head_count
        )
        prob_full = jnp.exp(scores - logsums[:, lower : lower + block_rows])
        grad_heads = context_grad[lower : lower + block_rows].reshape(
            block_rows, head_count, HEAD_DIM
        )
        prob_grad = jnp.einsum(
            "qhd,khd->hqk", grad_heads, value_heads, preferred_element_type=jnp.float32
        )
        inner = jnp.sum(prob_full * prob_grad, axis=-1, keepdims=True)
        score_grad = (prob_full * (prob_grad - inner)).astype(jnp.bfloat16)
        query_part = jnp.einsum(
            "hqk,khd->qhd", score_grad, key_heads, preferred_element_type=jnp.float32
        )
        query_parts.append((query_part * score_scale).reshape(block_rows, head_count * HEAD_DIM))
        key_total = (
            key_total
            + jnp.einsum(
                "hqk,qhd->khd", score_grad, query_heads, preferred_element_type=jnp.float32
            )
            * score_scale
        )
        value_total = value_total + jnp.einsum(
            "hqk,qhd->khd",
            prob_full.astype(jnp.bfloat16),
            grad_heads,
            preferred_element_type=jnp.float32,
        )
    query_grad = jnp.concatenate(query_parts, axis=0).astype(jnp.bfloat16)
    key_grad = key_total.reshape(length, head_count * HEAD_DIM).astype(jnp.bfloat16)
    value_grad = value_total.reshape(length, head_count * HEAD_DIM).astype(jnp.bfloat16)
    return (query_grad, key_grad, value_grad)


def subnet_pass(subnet, groups, gathered, inputs, segment, cotangent):
    (
        query_weight,
        key_weight,
        value_weight,
        output_weight,
        expand_weight,
        shrink_weight,
        query_bias,
        value_bias,
        output_bias,
        expand_bias,
        shrink_bias,
        first_gain,
        first_shift,
        second_gain,
        second_shift,
    ) = gathered
    full_feat = query_weight.shape[0]
    full_units = expand_weight.shape[0]
    head_count = (subnet + 1) * HEADS // groups
    feat_used = head_count * HEAD_DIM
    units_used = (subnet + 1) * full_units // groups
    query_part = query_weight[:feat_used]
    key_part = key_weight[:feat_used]
    value_part = value_weight[:feat_used]
    output_part = output_weight[:feat_used]
    expand_part = expand_weight[:units_used]
    shrink_part = shrink_weight[:units_used]
    query_rows = (dot_rows(inputs, query_part) + query_bias[:feat_used].astype(jnp.float32)).astype(
        jnp.bfloat16
    )
    key_rows = dot_rows(inputs, key_part).astype(jnp.bfloat16)
    value_rows = (dot_rows(inputs, value_part) + value_bias[:feat_used].astype(jnp.float32)).astype(
        jnp.bfloat16
    )
    context, logsums = attend(query_rows, key_rows, value_rows, segment, head_count)
    attended = dot_plain(context, output_part) + output_bias.astype(jnp.float32)
    normed, first_pull = jax.vjp(
        layer_norm,
        inputs.astype(jnp.float32) + attended,
        first_gain.astype(jnp.float32),
        first_shift.astype(jnp.float32),
    )
    normed_low = normed.astype(jnp.bfloat16)
    upward = dot_rows(normed_low, expand_part) + expand_bias[:units_used].astype(jnp.float32)
    activated_full, gelu_pull = jax.vjp(gelu_exact, upward)
    activated = activated_full.astype(jnp.bfloat16)
    branch = dot_plain(activated, shrink_part) + shrink_bias.astype(jnp.float32)
    result, second_pull = jax.vjp(
        layer_norm,
        normed + branch,
        second_gain.astype(jnp.float32),
        second_shift.astype(jnp.float32),
    )
    sum2_grad, second_gain_grad, second_shift_grad = second_pull(cotangent.astype(jnp.float32))
    branch_grad = sum2_grad.astype(jnp.bfloat16)
    shrink_grad = dot_cols(activated, branch_grad)
    upward_grad = gelu_pull(dot_rows(branch_grad, shrink_part))[0].astype(jnp.bfloat16)
    expand_grad = dot_cols(upward_grad, normed_low)
    normed_grad = sum2_grad + dot_plain(upward_grad, expand_part)
    sum1_grad, first_gain_grad, first_shift_grad = first_pull(normed_grad)
    attended_grad = sum1_grad.astype(jnp.bfloat16)
    output_grad = dot_cols(context, attended_grad)
    context_grad = dot_rows(attended_grad, output_part).astype(jnp.bfloat16)
    query_grad, key_grad, value_grad = attend_back(
        query_rows, key_rows, value_rows, segment, logsums, context_grad, head_count
    )
    input_grad = (
        sum1_grad
        + dot_plain(query_grad, query_part)
        + dot_plain(key_grad, key_part)
        + dot_plain(value_grad, value_part)
    )
    return (
        result.astype(jnp.bfloat16),
        input_grad,
        widen(dot_cols(query_grad, inputs), full_feat),
        widen(dot_cols(key_grad, inputs), full_feat),
        widen(dot_cols(value_grad, inputs), full_feat),
        widen(output_grad, full_feat),
        widen(expand_grad, full_units),
        widen(shrink_grad, full_units),
        widen(column_sum(query_grad), full_feat),
        widen(column_sum(value_grad), full_feat),
        column_sum(attended_grad),
        widen(column_sum(upward_grad), full_units),
        column_sum(branch_grad),
        first_gain_grad,
        first_shift_grad,
        second_gain_grad,
        second_shift_grad,
    )


def scatter_final(items):
    return (
        lax.psum_scatter(
            items[0].astype(jnp.bfloat16), "width", scatter_dimension=0, tiled=True
        ).astype(jnp.float32),
        lax.psum_scatter(
            items[1].astype(jnp.bfloat16), "width", scatter_dimension=0, tiled=True
        ).astype(jnp.float32),
        lax.psum_scatter(
            items[2].astype(jnp.bfloat16), "width", scatter_dimension=0, tiled=True
        ).astype(jnp.float32),
        lax.psum_scatter(
            items[3].astype(jnp.bfloat16), "width", scatter_dimension=0, tiled=True
        ).astype(jnp.float32),
        lax.psum_scatter(
            items[4].astype(jnp.bfloat16), "width", scatter_dimension=0, tiled=True
        ).astype(jnp.float32),
        lax.psum_scatter(
            items[5].astype(jnp.bfloat16), "width", scatter_dimension=0, tiled=True
        ).astype(jnp.float32),
        lax.psum_scatter(
            items[6].astype(jnp.bfloat16), "width", scatter_dimension=0, tiled=True
        ).astype(jnp.float32),
        lax.psum_scatter(
            items[7].astype(jnp.bfloat16), "width", scatter_dimension=0, tiled=True
        ).astype(jnp.float32),
        lax.psum_scatter(
            items[8].astype(jnp.bfloat16), "width", scatter_dimension=0, tiled=True
        ).astype(jnp.float32),
        lax.psum_scatter(
            items[9].astype(jnp.bfloat16), "width", scatter_dimension=0, tiled=True
        ).astype(jnp.float32),
        lax.psum_scatter(
            items[10].astype(jnp.bfloat16), "width", scatter_dimension=0, tiled=True
        ).astype(jnp.float32),
        lax.psum_scatter(
            items[11].astype(jnp.bfloat16), "width", scatter_dimension=0, tiled=True
        ).astype(jnp.float32),
        lax.psum_scatter(
            items[12].astype(jnp.bfloat16), "width", scatter_dimension=0, tiled=True
        ).astype(jnp.float32),
        lax.psum_scatter(
            items[13].astype(jnp.bfloat16), "width", scatter_dimension=0, tiled=True
        ).astype(jnp.float32),
        lax.psum_scatter(
            items[14].astype(jnp.bfloat16), "width", scatter_dimension=0, tiled=True
        ).astype(jnp.float32),
    )


def regroup(array, groups, shards):
    rest = array.shape[1:]
    owned_rows = array.shape[0] // (groups * shards)
    split = array.reshape((groups, shards, owned_rows) + rest)
    return jnp.swapaxes(split, 0, 1).reshape(array.shape)


def fold_pieces(array, count):
    return jnp.sum(array.reshape((count, array.shape[0] // count) + array.shape[1:]), axis=0)


def local(
    tokens_in,
    seq_lengths,
    query_weight,
    key_weight,
    value_weight,
    output_weight,
    expand_weight,
    shrink_weight,
    query_bias,
    value_bias,
    output_bias,
    expand_bias,
    shrink_bias,
    first_gain,
    first_shift,
    second_gain,
    second_shift,
    out_grad,
):
    groups = lax.axis_size("width")
    shards = lax.axis_size("tok")
    gathered = (
        lax.all_gather(query_weight, ("width", "tok"), axis=0, tiled=True),
        lax.all_gather(key_weight, ("width", "tok"), axis=0, tiled=True),
        lax.all_gather(value_weight, ("width", "tok"), axis=0, tiled=True),
        lax.all_gather(output_weight, ("width", "tok"), axis=0, tiled=True),
        lax.all_gather(expand_weight, ("width", "tok"), axis=0, tiled=True),
        lax.all_gather(shrink_weight, ("width", "tok"), axis=0, tiled=True),
        lax.all_gather(query_bias, ("width", "tok"), axis=0, tiled=True),
        lax.all_gather(value_bias, ("width", "tok"), axis=0, tiled=True),
        lax.all_gather(output_bias, ("width", "tok"), axis=0, tiled=True),
        lax.all_gather(expand_bias, ("width", "tok"), axis=0, tiled=True),
        lax.all_gather(shrink_bias, ("width", "tok"), axis=0, tiled=True),
        lax.all_gather(first_gain, ("width", "tok"), axis=0, tiled=True),
        lax.all_gather(first_shift, ("width", "tok"), axis=0, tiled=True),
        lax.all_gather(second_gain, ("width", "tok"), axis=0, tiled=True),
        lax.all_gather(second_shift, ("width", "tok"), axis=0, tiled=True),
    )
    seq_ends = jnp.cumsum(seq_lengths[0])
    positions = jnp.arange(tokens_in.shape[0], dtype=jnp.int32)
    segment = jnp.sum((positions[:, None] >= seq_ends[None, :]).astype(jnp.int32), axis=1)
    branches = [partial(subnet_pass, subnet, groups) for subnet in range(groups)]
    results = lax.switch(
        lax.axis_index("width"), branches, tuple(gathered), tokens_in, segment, out_grad[0]
    )
    terms = results[2:]
    moved = [regroup(term, groups, shards) for term in terms]
    swapped = (
        lax.all_to_all(shortened(moved[0]), "tok", split_axis=0, concat_axis=0, tiled=True),
        lax.all_to_all(shortened(moved[1]), "tok", split_axis=0, concat_axis=0, tiled=True),
        lax.all_to_all(shortened(moved[2]), "tok", split_axis=0, concat_axis=0, tiled=True),
        lax.all_to_all(shortened(moved[3]), "tok", split_axis=0, concat_axis=0, tiled=True),
        lax.all_to_all(shortened(moved[4]), "tok", split_axis=0, concat_axis=0, tiled=True),
        lax.all_to_all(shortened(moved[5]), "tok", split_axis=0, concat_axis=0, tiled=True),
        lax.all_to_all(shortened(moved[6]), "tok", split_axis=0, concat_axis=0, tiled=True),
        lax.all_to_all(shortened(moved[7]), "tok", split_axis=0, concat_axis=0, tiled=True),
        lax.all_to_all(shortened(moved[8]), "tok", split_axis=0, concat_axis=0, tiled=True),
        lax.all_to_all(shortened(moved[9]), "tok", split_axis=0, concat_axis=0, tiled=True),
        lax.all_to_all(shortened(moved[10]), "tok", split_axis=0, concat_axis=0, tiled=True),
        lax.all_to_all(shortened(moved[11]), "tok", split_axis=0, concat_axis=0, tiled=True),
        lax.all_to_all(shortened(moved[12]), "tok", split_axis=0, concat_axis=0, tiled=True),
        lax.all_to_all(shortened(moved[13]), "tok", split_axis=0, concat_axis=0, tiled=True),
        lax.all_to_all(shortened(moved[14]), "tok", split_axis=0, concat_axis=0, tiled=True),
    )
    per_shard = [fold_pieces(piece, shards) for piece in swapped]
    owned = scatter_final(per_shard)
    return (results[0][None], results[1][None]) + tuple(owned)


def solution(mesh):
    placed = (
        P("tok", None),
        P("tok", None),
        P(("width", "tok"), None),
        P(("width", "tok"), None),
        P(("width", "tok"), None),
        P(("width", "tok"), None),
        P(("width", "tok"), None),
        P(("width", "tok"), None),
        P(("width", "tok")),
        P(("width", "tok")),
        P(("width", "tok")),
        P(("width", "tok")),
        P(("width", "tok")),
        P(("width", "tok")),
        P(("width", "tok")),
        P(("width", "tok")),
        P(("width", "tok")),
        P("width", "tok", None),
    )
    return jax.shard_map(
        local,
        mesh=mesh,
        in_specs=placed,
        out_specs=(
            P("width", "tok", None),
            P("width", "tok", None),
            P(("width", "tok"), None),
            P(("width", "tok"), None),
            P(("width", "tok"), None),
            P(("width", "tok"), None),
            P(("width", "tok"), None),
            P(("width", "tok"), None),
            P(("width", "tok")),
            P(("width", "tok")),
            P(("width", "tok")),
            P(("width", "tok")),
            P(("width", "tok")),
            P(("width", "tok")),
            P(("width", "tok")),
            P(("width", "tok")),
            P(("width", "tok")),
        ),
        check_vma=False,
    )
```

profile of v0, /device:TPU:0, one launch (start us, length us, event | category | flops | bytes accessed | tf_op | source)
XLA Modules:
  0.0 1187.5 jit_solution(11228019101677624167)
XLA Ops:
  16.9 42.4 %all-reduce.45 = (bf16[768]{0:T(1024)(128)(2,1)S(1)}, bf16[768]{0:T(1024)(128)(2,1)S(1)}, bf16[768]{0:T(1024)(128)(2,1)S(1)}, bf16[768]{0:T(1024)(128)(2,1)S(1)}...) all-reduce(bf16[768]{0:T(1024)(128)(2,1)S(1)} %dynamic-update-slice, ...), channel_id=1, replica_groups=mesh['width'=4,'tok'=8] {'width','tok'}, use_global_device_ids=true, to_apply=%add.27 | all-reduce | flops 9216 | bytes 36864
  59.3 8.8 all-gather.9.cloned.1.call-done
  68.1 55.7 %all-gather.7.cloned.1.call-done = bf16[768,768]{1,0:T(8,128)(2,1)} async-done(((bf16[24,768]{1,0:T(8,128)(2,1)}), bf16[768,768]{1,0:T(8,128)(2,1)}) %all-gather.7.cloned.1.call-update) | async-done | bytes 1179664 | tf_op jit(solution)/shard_map/all_gather | solution.py:318
  123.8 55.9 %all-gather.11.cloned.1.call-done = bf16[768,768]{1,0:T(8,128)(2,1)} async-done(((bf16[24,768]{1,0:T(8,128)(2,1)}), bf16[768,768]{1,0:T(8,128)(2,1)}) %all-gather.11.cloned.1.call-update) | async-done | bytes 1179664 | tf_op jit(solution)/shard_map/all_gather | solution.py:319
  179.7 55.8 %all-gather.13.cloned.1.call-done = bf16[768,768]{1,0:T(8,128)(2,1)} async-done(((bf16[24,768]{1,0:T(8,128)(2,1)}), bf16[768,768]{1,0:T(8,128)(2,1)}) %all-gather.13.cloned.1.call-update) | async-done | bytes 1179664 | tf_op jit(solution)/shard_map/all_gather | solution.py:320
  235.5 65.2 %all-gather.15.cloned.1.call-done = bf16[3072,768]{1,0:T(8,128)(2,1)} async-done(((bf16[96,768]{1,0:T(8,128)(2,1)}), bf16[3072,768]{1,0:T(8,128)(2,1)}) %all-gather.15.cloned.1.call-update) | async-done | bytes 4718608 | tf_op jit(solution)/shard_map/all_gather | solution.py:321
  300.7 64.6 %all-gather.17.cloned.1.call-done = bf16[3072,768]{1,0:T(8,128)(2,1)} async-done(((bf16[96,768]{1,0:T(8,128)(2,1)}), bf16[3072,768]{1,0:T(8,128)(2,1)}) %all-gather.17.cloned.1.call-update) | async-done | bytes 4718608 | tf_op jit(solution)/shard_map/all_gather | solution.py:322
  365.3 148.3 %conditional.2 = (bf16[768,768]{1,0:T(8,128)(2,1)}, bf16[768,768]{1,0:T(8,128)(2,1)}, bf16[768,768]{1,0:T(8,128)(2,1)}, bf16[768,768]{1,0:T(8,128)(2,1)}, bf16[3...) conditional(s32[]{:T(128)} %clamp.3, ...), branch_computations={%region_2.20_spmd, %region_20.38_spmd, %region_38.56_spmd, %region... | conditional | flops 53844111360 | bytes 1182552960
  397.8 10.1 multiply_convert_fusion.2
  408.0 3.8 fusion.266
  413.6 4.0 fusion.19
  423.2 4.1 multiply_reduce_fusion.2
  433.8 4.8 fusion.64
  439.2 3.5 convert_convert_fusion
  456.2 3.4 fusion.44
  515.1 3.8 all-to-all-start.7
  520.4 5.0 all-to-all-done.7
  525.3 3.3 all-to-all-start.6
  528.7 5.1 fusion.251
  535.0 5.5 all-to-all-start.13
  541.3 5.6 all-to-all-done.13
  546.9 3.3 all-to-all-start.11
  551.3 5.3 all-to-all-done.11
  560.7 5.6 all-to-all-done.14
  572.5 3.4 all-to-all-done.12
  581.7 4.0 all-to-all-done.8
  586.2 3.6 all-to-all-start
  592.2 15.4 %all-to-all-done = bf16[8,96,768]{2,1,0:T(8,128)(2,1)S(1)} async-done(((bf16[8,96,768]{2,1,0:T(8,128)(2,1)}), bf16[8,96,768]{2,1,0:T(8,128)(2,1)S(1)}, u32[]{:S(2)}, u32[]{:S(2)}) %all-to-all-start) | async-done | bytes 1179680 | tf_op jit(solution)/shard_map/all_to_all | solution.py:343
  607.6 3.6 all-to-all-start.1
  612.3 16.7 %all-to-all-done.1 = bf16[8,96,768]{2,1,0:T(8,128)(2,1)S(1)} async-done(((bf16[8,96,768]{2,1,0:T(8,128)(2,1)}), bf16[8,96,768]{2,1,0:T(8,128)(2,1)S(1)}, u32[]{:S(2)}, u32[]{:S(2)}) %all-to-all-start.1) | async-done | bytes 1179680 | tf_op jit(solution)/shard_map/all_to_all | solution.py:344
  628.9 3.6 all-to-all-start.2
  634.9 26.5 %all-to-all-done.2 = bf16[8,96,768]{2,1,0:T(8,128)(2,1)S(1)} async-done(((bf16[8,96,768]{2,1,0:T(8,128)(2,1)}), bf16[8,96,768]{2,1,0:T(8,128)(2,1)S(1)}, u32[]{:S(2)}, u32[]{:S(2)}) %all-to-all-start.2) | async-done | bytes 1179680 | tf_op jit(solution)/shard_map/all_to_all | solution.py:345
  661.4 4.5 all-to-all-start.3
  665.9 4.9 copy.117
  670.8 24.6 %all-to-all-done.3 = bf16[8,96,768]{2,1,0:T(8,128)(2,1)} async-done(((bf16[8,96,768]{2,1,0:T(8,128)(2,1)}), bf16[8,96,768]{2,1,0:T(8,128)(2,1)}, u32[]{:S(2)}, u32[]{:S(2)}) %all-to-all-start.3) | async-done | bytes 1179680 | tf_op jit(solution)/shard_map/all_to_all | solution.py:346
  695.4 4.6 all-to-all-start.4
  700.0 4.9 copy.118
  704.9 74.2 %all-to-all-done.4 = bf16[8,384,768]{2,1,0:T(8,128)(2,1)} async-done(((bf16[8,384,768]{2,1,0:T(8,128)(2,1)}), bf16[8,384,768]{2,1,0:T(8,128)(2,1)}, u32[]{:S(2)}, u32[]{:S(2)}) %all-to-all-start.4) | async-done | bytes 4718624 | tf_op jit(solution)/shard_map/all_to_all | solution.py:347
  779.1 16.0 %all-to-all-start.5 = ((bf16[8,384,768]{2,1,0:T(8,128)(2,1)}), bf16[8,384,768]{2,1,0:T(8,128)(2,1)}, u32[]{:S(2)}, u32[]{:S(2)}) async-start(bf16[8,384,768]{2,1,0:T(8,128)(2,1)} %bitcast.327), calls=%async_computation.10 | async-start | bytes 9437184 | tf_op jit(solution)/shard_map/all_to_all | solution.py:348
  800.0 4.0 reduce_sum.1063
  807.0 73.5 %all-to-all-done.5 = bf16[8,384,768]{2,1,0:T(8,128)(2,1)} async-done(((bf16[8,384,768]{2,1,0:T(8,128)(2,1)}), bf16[8,384,768]{2,1,0:T(8,128)(2,1)}, u32[]{:S(2)}, u32[]{:S(2)}) %all-to-all-start.5) | async-done | bytes 4718624 | tf_op jit(solution)/shard_map/all_to_all | solution.py:348
  890.9 4.0 reduce_sum.1064
  894.9 8.4 all-to-all-start.9
  903.3 6.2 add_bitcast_fusion
  909.7 10.8 all-to-all-done.9
  920.6 205.6 %all-reduce.46 = (bf16[96]{0:T(256)(128)(2,1)S(1)}, bf16[96]{0:T(256)(128)(2,1)S(1)}, bf16[96]{0:T(256)(128)(2,1)S(1)}, bf16[384]{0:T(512)(128)(2,1)S(1)}, bf16[...) all-reduce(bf16[96]{0:T(256)(128)(2,1)S(1)} %reduce_sum.1065, ...), channel_id=8, replica_groups=mesh['width'=4,'tok'=8] {'width'}, use_global_device_ids=true, to_apply=%region_87.88.clone | all-reduce | flops 1152 | bytes 4608
  1137.1 17.2 %reduce-scatter.15.cloned.1.call-done = bf16[96,768]{1,0:T(8,128)(2,1)} async-done(((bf16[384,768]{1,0:T(8,128)(2,1)}), bf16[96,768]{1,0:T(8,128)(2,1)}) %reduce-scatter.15.cloned.1.call-update) | async-done | bytes 147472 | tf_op jit(solution)/shard_map/reduce_scatter | solution.py:247
  1155.9 22.8 %reduce-scatter.17.cloned.1.call-done = bf16[96,768]{1,0:T(8,128)(2,1)} async-done(((bf16[384,768]{1,0:T(8,128)(2,1)}), bf16[96,768]{1,0:T(8,128)(2,1)}) %reduce-scatter.17.cloned.1.call-update) | async-done | bytes 147472 | tf_op jit(solution)/shard_map/reduce_scatter | solution.py:250
  (341 shorter events, 155.5 us)
Async XLA Ops:
  7.2 8.2 copy-start.162
  7.2 8.4 copy-start.163
  7.2 8.7 copy-start.164
  7.3 8.9 copy-start.165
  7.3 9.1 copy-start.166
  7.3 9.4 copy-start.167
  7.3 358.1 %copy-start.16 = (bf16[1024,768]{1,0:T(8,128)(2,1)S(1)}, bf16[1024,768]{1,0:T(8,128)(2,1)}, u32[]{:S(2)}) copy-start(bf16[1024,768]{1,0:T(8,128)(2,1)} %param.22) | copy-start | bytes 4718596
  7.3 60.8 %all-gather.9.cloned.1.call-start = ((), (), s32[]{:S(2)}) async-start(), calls=%async_computation.22 | async-start | bytes 1216512 | tf_op jit(solution)/shard_map/all_gather | solution.py:317
  8.0 115.8 %all-gather.7.cloned.1.call-start = ((), (), s32[]{:S(2)}) async-start(), calls=%async_computation.21 | async-start | bytes 1216512 | tf_op jit(solution)/shard_map/all_gather | solution.py:318
  8.8 171.0 %all-gather.11.cloned.1.call-start = ((), (), s32[]{:S(2)}) async-start(), calls=%async_computation.23 | async-start | bytes 1216512 | tf_op jit(solution)/shard_map/all_gather | solution.py:319
  9.5 226.0 %all-gather.13.cloned.1.call-start = ((), (), s32[]{:S(2)}) async-start(), calls=%async_computation.24 | async-start | bytes 1216512 | tf_op jit(solution)/shard_map/all_gather | solution.py:320
  10.1 290.6 %all-gather.15.cloned.1.call-start = ((), (), s32[]{:S(2)}) async-start(), calls=%async_computation.25 | async-start | bytes 4866048 | tf_op jit(solution)/shard_map/all_gather | solution.py:321
  10.7 354.7 %all-gather.17.cloned.1.call-start = ((), (), s32[]{:S(2)}) async-start(), calls=%async_computation.26 | async-start | bytes 4866048 | tf_op jit(solution)/shard_map/all_gather | solution.py:322
  365.5 12.3 %copy-start.17 = (bf16[1024,768]{1,0:T(8,128)(2,1)}, bf16[1024,768]{1,0:T(8,128)(2,1)S(1)}, u32[]{:S(2)}) copy-start(bf16[1024,768]{1,0:T(8,128)(2,1)S(1)} %get-tuple-element.838) | copy-start | bytes 4718596 | tf_op jit(solution)/shard_map/conditional
  393.3 29.9 %copy-start.14 = (f32[1024,768]{0,1:T(8,128)}, f32[1024,768]{0,1:T(8,128)S(1)}, u32[]{:S(2)}) copy-start(f32[1024,768]{0,1:T(8,128)S(1)} %get-tuple-element.1004) | copy-start | bytes 9437188 | tf_op jit(solution)/shard_map/conditional
  393.3 29.9 %copy-start.121 = (f32[1024]{0:T(1024)}, f32[1024]{0:T(1024)S(1)}, u32[]{:S(2)}) copy-start(f32[1024]{0:T(1024)S(1)} %broadcast_multiply_fusion.1) | copy-start | bytes 12292 | tf_op jit(solution)/shard_map/conditional
  393.8 14.2 %slice-start.31 = ((s8[4718592]{0:T(1024)(128)(4,1)}), s8[4194304]{0:T(1024)(128)(4,1)S(1)}, s32[]{:S(2)}) async-start(s8[4718592]{0:T(1024)(128)(4,1)} %bitcast.457), calls=%async_computation.64 | async-start | bytes 8388608 | tf_op jit(solution)/shard_map/conditional
  397.8 10.2 copy-start.156
  397.8 10.2 slice-start.32
  438.6 10.1 slice-start.21
  439.2 9.5 slice-start.22
  456.2 8.5 slice-start.19
  515.1 10.3 all-to-all-start.7
  525.3 9.7 all-to-all-start.6
  528.7 21.6 %copy-start.5 = (bf16[1024,768]{0,1:T(8,128)(2,1)S(1)}, bf16[1024,768]{0,1:T(8,128)(2,1)}, u32[]{:S(2)}) copy-start(bf16[1024,768]{0,1:T(8,128)(2,1)} %get-tuple-element.480) | copy-start | bytes 4718596
  535.0 11.9 %all-to-all-start.13 = ((bf16[8,96,1]{1,2,0:T(2,128)(2,1)}), bf16[8,96,1]{1,2,0:T(2,128)(2,1)S(1)}, u32[]{:S(2)}, u32[]{:S(2)}) async-start(bf16[8,96,1]{1,2,0:T(2,128)(2,1)} %convert_element_type.1150), calls=%async_computation.19 | async-start | bytes 8192 | tf_op jit(solution)/shard_map/all_to_all | solution.py:356
  546.9 9.7 all-to-all-start.11
  556.6 9.7 all-to-all-start.14
  566.3 19.4 %copy-start.137 = (bf16[8,96,1]{1,2,0:T(2,128)(2,1)}, bf16[8,96,1]{1,2,0:T(2,128)(2,1)S(1)}, u32[]{:S(2)}) copy-start(bf16[8,96,1]{1,2,0:T(2,128)(2,1)S(1)} %all-to-all-done.14) | copy-start | bytes 4612
  566.3 9.7 all-to-all-start.12
  576.0 9.7 copy-start.139
  576.0 9.7 all-to-all-start.8
  585.6 25.5 %copy-start.54 = (bf16[768,768]{1,0:T(8,128)(2,1)S(1)}, bf16[768,768]{1,0:T(8,128)(2,1)}, u32[]{:S(2)}) copy-start(bf16[768,768]{1,0:T(8,128)(2,1)} %get-tuple-element.467) | copy-start | bytes 3538948
  586.2 21.4 %all-to-all-start = ((bf16[8,96,768]{2,1,0:T(8,128)(2,1)}), bf16[8,96,768]{2,1,0:T(8,128)(2,1)S(1)}, u32[]{:S(2)}, u32[]{:S(2)}) async-start(bf16[8,96,768]{2,1,0:T(8,128)(2,1)} %bitcast.89), calls=%async_computation | async-start | bytes 2359296 | tf_op jit(solution)/shard_map/all_to_all | solution.py:343
  607.6 21.4 %all-to-all-start.1 = ((bf16[8,96,768]{2,1,0:T(8,128)(2,1)}), bf16[8,96,768]{2,1,0:T(8,128)(2,1)S(1)}, u32[]{:S(2)}, u32[]{:S(2)}) async-start(bf16[8,96,768]{2,1,0:T(8,128)(2,1)} %bitcast.363), calls=%async_computation.2 | async-start | bytes 2359296 | tf_op jit(solution)/shard_map/all_to_all | solution.py:344
  628.9 32.5 %all-to-all-start.2 = ((bf16[8,96,768]{2,1,0:T(8,128)(2,1)}), bf16[8,96,768]{2,1,0:T(8,128)(2,1)S(1)}, u32[]{:S(2)}, u32[]{:S(2)}) async-start(bf16[8,96,768]{2,1,0:T(8,128)(2,1)} %bitcast.364), calls=%async_computation.4 | async-start | bytes 2359296 | tf_op jit(solution)/shard_map/all_to_all | solution.py:345
  661.4 34.0 %all-to-all-start.3 = ((bf16[8,96,768]{2,1,0:T(8,128)(2,1)}), bf16[8,96,768]{2,1,0:T(8,128)(2,1)}, u32[]{:S(2)}, u32[]{:S(2)}) async-start(bf16[8,96,768]{2,1,0:T(8,128)(2,1)} %bitcast.365), calls=%async_computation.6 | async-start | bytes 2359296 | tf_op jit(solution)/shard_map/all_to_all | solution.py:346
  695.4 83.7 %all-to-all-start.4 = ((bf16[8,384,768]{2,1,0:T(8,128)(2,1)}), bf16[8,384,768]{2,1,0:T(8,128)(2,1)}, u32[]{:S(2)}, u32[]{:S(2)}) async-start(bf16[8,384,768]{2,1,0:T(8,128)(2,1)} %bitcast.328), calls=%async_computation.8 | async-start | bytes 9437184 | tf_op jit(solution)/shard_map/all_to_all | solution.py:347
  779.1 101.4 %all-to-all-start.5 = ((bf16[8,384,768]{2,1,0:T(8,128)(2,1)}), bf16[8,384,768]{2,1,0:T(8,128)(2,1)}, u32[]{:S(2)}, u32[]{:S(2)}) async-start(bf16[8,384,768]{2,1,0:T(8,128)(2,1)} %bitcast.327), calls=%async_computation.10 | async-start | bytes 9437184 | tf_op jit(solution)/shard_map/all_to_all | solution.py:348
  795.0 336.4 %reduce-scatter.7.cloned.1.call-start = ((), (), s32[]{:S(2)}) async-start(), calls=%async_computation.27 | async-start | bytes 184320 | tf_op jit(solution)/shard_map/reduce_scatter | solution.py:235
  796.0 336.9 %reduce-scatter.9.cloned.1.call-start = ((), (), s32[]{:S(2)}) async-start(), calls=%async_computation.28 | async-start | bytes 184320 | tf_op jit(solution)/shard_map/reduce_scatter | solution.py:238
  796.9 337.4 %reduce-scatter.11.cloned.1.call-start = ((), (), s32[]{:S(2)}) async-start(), calls=%async_computation.29 | async-start | bytes 184320 | tf_op jit(solution)/shard_map/reduce_scatter | solution.py:241
  797.8 337.9 %reduce-scatter.13.cloned.1.call-start = ((), (), s32[]{:S(2)}) async-start(), calls=%async_computation.30 | async-start | bytes 184320 | tf_op jit(solution)/shard_map/reduce_scatter | solution.py:244
  800.0 354.3 %reduce-scatter.15.cloned.1.call-start = ((), (), s32[]{:S(2)}) async-start(), calls=%async_computation.31 | async-start | bytes 737280 | tf_op jit(solution)/shard_map/reduce_scatter | solution.py:247
  804.0 79.8 %copy-start.177 = (u32[32]{0:T(128)S(1)}, u32[32]{0:T(128)}, u32[]{:S(2)}) copy-start(u32[32]{0:T(128)} %constant.630) | copy-start | bytes 388
  880.5 14.4 %all-to-all-start.10 = ((bf16[8,96,1]{1,2,0:T(2,128)(2,1)}), bf16[8,96,1]{1,2,0:T(2,128)(2,1)S(1)}, u32[]{:S(2)}, u32[]{:S(2)}) async-start(bf16[8,96,1]{1,2,0:T(2,128)(2,1)} %convert_element_type.1147), calls=%async_computation.16 | async-start | bytes 8192 | tf_op jit(solution)/shard_map/all_to_all | solution.py:353
  883.8 295.0 %reduce-scatter.17.cloned.1.call-start = ((), (), s32[]{:S(2)}) async-start(), calls=%async_computation.32 | async-start | bytes 737280 | tf_op jit(solution)/shard_map/reduce_scatter | solution.py:250
  894.9 25.6 %all-to-all-start.9 = ((bf16[8,2,192]{2,1,0:T(2,128)(2,1)}), bf16[8,2,192]{2,1,0:T(2,128)(2,1)S(1)}, u32[]{:S(2)}, u32[]{:S(2)}) async-start(bf16[8,2,192]{2,1,0:T(2,128)(2,1)} %reshape.1116), calls=%async_computation.15 | async-start | bytes 16384 | tf_op jit(solution)/shard_map/all_to_all | solution.py:352
  (50 other events, 186.9 us)
Sparse Core Ops, SparseCore 0:
  11.0 57.0 all-gather.8
  71.0 52.7 all-gather.6
  126.8 52.9 all-gather.10
  182.5 52.9 all-gather.12
  238.3 62.4 all-gather.14
  303.5 61.8 all-gather.16
  798.9 263.8 reduce-scatter.6
  1065.8 19.6 reduce-scatter.8
  1087.9 19.6 reduce-scatter.10
  1109.9 19.6 reduce-scatter.12
  1132.2 22.1 reduce-scatter.14
  1156.7 22.0 reduce-scatter.16
where the time goes:
time: 1190 us
  waiting for transfers between devices  621 us (52%)
  blocking collectives  248 us (21%)
  starting transfers between devices  73.8 us (6%)
  matrix products  71.1 us (6%)
  other arithmetic  70.8 us (6%)
  local copies, waits for them, and re-layouts  58.6 us (5%)
  loops' own time  28.5 us (2%)
  between operations  16.2 us (1%)
    unnamed x2, blocking collectives  248 us
    all_to_all x1, waiting for transfers between devices, local(): lax.all_to_all(shortened(moved[4]), 'tok', split_axis=0, concat_axis=0, t...  74.2 us
    all_to_all x1, waiting for transfers between devices, local(): lax.all_to_all(shortened(moved[5]), 'tok', split_axis=0, concat_axis=0, t...  73.5 us
    all_gather x1, waiting for transfers between devices, local(): lax.all_gather(expand_weight, ('width', 'tok'), axis=0, tiled=True)  65.2 us
    all_gather x1, waiting for transfers between devices, local(): lax.all_gather(shrink_weight, ('width', 'tok'), axis=0, tiled=True)  64.6 us
    all_gather x1, waiting for transfers between devices, local(): lax.all_gather(value_weight, ('width', 'tok'), axis=0, tiled=True)  55.9 us
    all_gather x1, waiting for transfers between devices, local(): lax.all_gather(output_weight, ('width', 'tok'), axis=0, tiled=True)  55.8 us
    all_gather x1, waiting for transfers between devices, local(): lax.all_gather(key_weight, ('width', 'tok'), axis=0, tiled=True)  55.7 us
  transfers between devices with their start and end apart: 27, of which 22 were waited for; matrix products, arithmetic and copies ran while one was open for 6% of the time, Pallas kernels for 0%

commit v1 on v0

v1 whole, which is shorter than its diff:
```python
import functools
import math

import jax
import jax.numpy as jnp
from jax import lax
from jax.experimental import pallas as pl
from jax.experimental.pallas import tpu as pltpu
from jax.sharding import PartitionSpec as P

HEADS = 12
HEAD_DIM = 64
norm_eps = 1e-12
BF = jnp.bfloat16
F32 = jnp.float32
BR = 128
BC = 256
RT = 256
MASKED = -1e30


def nt(left, right):
    return lax.dot_general(left, right, (((1,), (1,)), ((), ())), preferred_element_type=F32)


def tn(left, right):
    return lax.dot_general(left, right, (((0,), (0,)), ((), ())), preferred_element_type=F32)


def nn(left, right):
    return jnp.dot(left, right, preferred_element_type=F32)


def rows_at(index, size):
    return pl.ds(pl.multiple_of(index * size, size), size)


def head_of(shape, axis):
    return lax.broadcasted_iota(jnp.int32, shape, axis) // HEAD_DIM


def attn_fwd(scal, bounds, x_ref, wq_ref, wk_ref, wv_ref, bias_ref, segc_ref, segr_ref,
             ctx_ref, lse_ref, q_s, kt_s, v_s, s_s, m_s):
    heads = q_s.shape[1] // HEAD_DIM
    tokens = x_ref.shape[0]

    @pl.when(pl.program_id(0) <= scal[0])
    def _():
        wq, wk, wv = wq_ref[0], wk_ref[0], wv_ref[0]

        @pl.loop(0, tokens // RT)
        def _(i):
            r = rows_at(i, RT)
            xb = x_ref[r, :]
            q = (nt(xb, wq) + bias_ref[0, 0:1, :]).astype(BF).astype(F32)
            q_s[r, :] = (q * 0.125).astype(BF)
            v = (nt(xb, wv) + bias_ref[0, 1:2, :]).astype(BF)
            kt = nt(wk, xb).astype(BF)
            for h in range(heads):
                v_s[h, r, :] = jnp.where(head_of(v.shape, 1) == h, v, jnp.zeros_like(v))
                kt_s[h, :, r] = jnp.where(head_of(kt.shape, 0) == h, kt, jnp.zeros_like(kt))

        @pl.loop(0, tokens // BR)
        def _(i):
            r = rows_at(i, BR)
            qb = q_s[r, :]
            seg = segc_ref[r, :]
            seg = jnp.concatenate([seg] * (BC // 128), axis=1)
            lo, hi = bounds[0, i], bounds[1, i]
            m_s[...] = jnp.full_like(m_s, MASKED)

            @pl.loop(lo, hi)
            def _(j):
                c = rows_at(j, BC)
                keep = seg == segr_ref[0:1, c]
                for h in range(heads):
                    s = jnp.where(keep, nn(qb, kt_s[h, :, c]), MASKED)
                    s_s[h, :, c] = s
                    m_s[h] = jnp.maximum(m_s[h], s)

            tops = [jnp.max(m_s[h], axis=1, keepdims=True) for h in range(heads)]
            zero = jnp.zeros((BR, 1), F32)

            def second(j, carry):
                out, sums = carry
                c = rows_at(j, BC)
                new = []
                for h in range(heads):
                    e = jnp.exp(s_s[h, :, c] - tops[h])
                    out = out + nn(e.astype(BF), v_s[h, c, :])
                    new.append(sums[h] + jnp.sum(e, axis=1, keepdims=True))
                return out, tuple(new)

            out, sums = lax.fori_loop(
                lo, hi, second, (jnp.zeros((BR, q_s.shape[1]), F32), (zero,) * heads))
            lane = head_of(out.shape, 1)
            div = jnp.broadcast_to(sums[0], out.shape)
            col = lax.broadcasted_iota(jnp.int32, (BR, 128), 1)
            lse = jnp.broadcast_to(tops[0] + jnp.log(sums[0]), (BR, 128))
            for h in range(1, heads):
                div = jnp.where(lane == h, sums[h], div)
                lse = jnp.where(col == h, tops[h] + jnp.log(sums[h]), lse)
            ctx_ref[0, r, :] = (out / div).astype(BF)
            lse_ref[0, r, :] = lse


def attn_bwd(scal, bounds, x_ref, wq_ref, wk_ref, wv_ref, bias_ref, bcol_ref, segc_ref, segr_ref,
             ctx_ref, lse_ref, do_ref, dot_ref, s1g_ref,
             ig_ref, dwq_ref, dwk_ref, dwv_ref, db_ref,
             q_s, qt_s, k_s, kt_s, vt_s, dq_s, dkt_s, dvt_s, kt_f, vt_f):
    heads = q_s.shape[1] // HEAD_DIM
    tokens = x_ref.shape[0]

    @pl.when(pl.program_id(0) == 0)
    def _():
        ig_ref[...] = s1g_ref[...]

    @pl.when(pl.program_id(0) <= scal[0])
    def _():
        wq, wk, wv = wq_ref[0], wk_ref[0], wv_ref[0]
        qcol = bcol_ref[0, :, 0:1].astype(F32)
        vcol = bcol_ref[0, :, 1:2].astype(F32)

        @pl.loop(0, tokens // RT)
        def _(i):
            r = rows_at(i, RT)
            xb = x_ref[r, :]
            q = (nt(xb, wq) + bias_ref[0, 0:1, :]).astype(BF).astype(F32)
            q_s[r, :] = (q * 0.125).astype(BF)
            qt = (nt(wq, xb) + qcol).astype(BF).astype(F32)
            qt_s[:, r] = (qt * 0.125).astype(BF)
            k = nt(xb, wk).astype(BF)
            kt = nt(wk, xb).astype(BF)
            vt = (nt(wv, xb) + vcol).astype(BF)
            for h in range(heads):
                k_s[h, r, :] = jnp.where(head_of(k.shape, 1) == h, k, jnp.zeros_like(k))
                kt_s[h, :, r] = jnp.where(head_of(kt.shape, 0) == h, kt, jnp.zeros_like(kt))
                vt_s[h, :, r] = jnp.where(head_of(vt.shape, 0) == h, vt, jnp.zeros_like(vt))

        kt_f[...] = jnp.zeros_like(kt_f)
        vt_f[...] = jnp.zeros_like(vt_f)

        @pl.loop(0, tokens // BR)
        def _(i):
            r = rows_at(i, BR)
            qb = q_s[r, :]
            dob = do_ref[0, r, :]
            seg = segc_ref[r, :]
            seg = jnp.concatenate([seg] * (BC // 128), axis=1)
            prod = dob.astype(F32) * ctx_ref[0, r, :].astype(F32)
            lane = head_of(prod.shape, 1)
            inner = [jnp.sum(jnp.where(lane == h, prod, 0.0), axis=1, keepdims=True) for h in range(heads)]
            lses = [lse_ref[0, r, h : h + 1] for h in range(heads)]
            qts = [qt_s[h * HEAD_DIM : (h + 1) * HEAD_DIM, r] for h in range(heads)]
            dots = [dot_ref[0, h * HEAD_DIM : (h + 1) * HEAD_DIM, r] for h in range(heads)]

            def block(j, dq):
                c = rows_at(j, BC)
                keep = seg == segr_ref[0:1, c]
                for h in range(heads):
                    hs = slice(h * HEAD_DIM, (h + 1) * HEAD_DIM)
                    s = jnp.where(keep, nn(qb, kt_s[h, :, c]), MASKED)
                    p = jnp.exp(s - lses[h])
                    dp = nn(dob, vt_s[h, :, c])
                    ds = (p * (dp - inner[h])).astype(BF)
                    dq = dq + nn(ds, k_s[h, c, :])
                    kt_f[hs, c] += nn(qts[h], ds)
                    vt_f[hs, c] += nn(dots[h], p.astype(BF))
                return dq

            dq = lax.fori_loop(bounds[0, i], bounds[1, i], block, jnp.zeros(qb.shape, F32))
            dq_s[r, :] = (dq * 0.125).astype(BF)

        dkt_s[...] = kt_f[...].astype(BF)
        dvt_s[...] = vt_f[...].astype(BF)

        @pl.loop(0, tokens // RT)
        def _(i):
            r = rows_at(i, RT)
            ig_ref[r, :] += nn(dq_s[r, :], wq) + tn(dkt_s[:, r], wk) + tn(dvt_s[:, r], wv)

        x = x_ref[...]
        dwq_ref[0] = tn(dq_s[...], x).astype(BF)
        dwk_ref[0] = nn(dkt_s[...], x).astype(BF)
        dwv_ref[0] = nn(dvt_s[...], x).astype(BF)
        ones = jnp.ones((8, tokens), BF)
        db_ref[0, 0:8, :] = nn(ones, dq_s[...])
        db_ref[0, 8:16, :] = nt(ones, dvt_s[...])


def normal_parts(value):
    phi = jnp.exp(-0.5 * value * value) * (1.0 / math.sqrt(2.0 * math.pi))
    cum = 0.5 + 0.5 * lax.erf(value * math.sqrt(0.5))
    return cum, phi


def middle(scal, x_ref, ctx_ref, wo_ref, e_ref, s_ref, vec_ref, eb_ref, c_ref,
           lo_ref, s1g_ref, do_ref, dot_ref, dwo_ref, vg_ref, ebg_ref, de_hbm, ds_hbm,
           nl_s, n1_s, r1_s, br_s, act_s, gp_s, ug_s, bg_s, stage, sems):
    tokens, width = x_ref.shape
    used = scal[0] + 1
    tiles = tokens // RT
    ob, sb = vec_ref[2:3, :], vec_ref[3:4, :]
    g1, b1 = vec_ref[4:5, :], vec_ref[5:6, :]
    g2, b2 = vec_ref[6:7, :], vec_ref[7:8, :]

    def mean(v):
        return jnp.sum(v, axis=1, keepdims=True) * (1.0 / width)

    @pl.loop(0, tiles)
    def _(i):
        r = rows_at(i, RT)
        total = lax.fori_loop(
            0, used, lambda q, t: t + nn(ctx_ref[q, r, :], wo_ref[q]), jnp.zeros((RT, width), F32))
        v = x_ref[r, :].astype(F32) + (total + ob)
        v = v - mean(v)
        rstd = lax.rsqrt(mean(v * v) + norm_eps)
        n = v * rstd
        n1_s[r, :] = n
        r1_s[r, :] = jnp.broadcast_to(rstd, (RT, 128))
        normed = n * g1 + b1
        nl_s[r, :] = normed.astype(BF)
        br_s[r, :] = normed + sb

    @pl.loop(0, used)
    def _(q):
        @pl.loop(0, tiles)
        def _(i):
            r = rows_at(i, RT)
            u = nt(nl_s[r, :], e_ref[q]) + eb_ref[q, 0:1, :]
            cum, phi = normal_parts(u)
            act = (u * cum).astype(BF)
            act_s[q, r, :] = act
            gp_s[q, r, :] = (cum + u * phi).astype(BF)
            br_s[r, :] += nn(act, s_ref[q])

    zero = jnp.zeros((1, width), F32)

    def second_norm(i, sums):
        r = rows_at(i, RT)
        v = br_s[r, :]
        v = v - mean(v)
        rstd = lax.rsqrt(mean(v * v) + norm_eps)
        n = v * rstd
        lo_ref[r, :] = (n * g2 + b2).astype(BF)
        c = c_ref[r, :].astype(F32)
        m = c * g2
        g = rstd * (m - mean(m) - n * mean(m * n))
        s1g_ref[r, :] = g
        bg = g.astype(BF)
        bg_s[r, :] = bg
        return (sums[0] + jnp.sum(c * n, axis=0, keepdims=True),
                sums[1] + jnp.sum(c, axis=0, keepdims=True),
                sums[2] + jnp.sum(bg.astype(F32), axis=0, keepdims=True))

    g2g, b2g, sbg = lax.fori_loop(0, tiles, second_norm, (zero, zero, zero))
    vg_ref[6:7, :] = g2g
    vg_ref[7:8, :] = b2g
    vg_ref[3:4, :] = sbg

    def moved(kind, q, out_hbm):
        return pltpu.make_async_copy(stage.at[kind], out_hbm.at[q], sems.at[kind])

    @pl.loop(0, used)
    def _(q):
        def tile(i, total):
            r = rows_at(i, RT)
            d = nt(bg_s[r, :], s_ref[q]) * gp_s[q, r, :].astype(F32)
            ug = d.astype(BF)
            ug_s[r, :] = ug
            s1g_ref[r, :] += nn(ug, e_ref[q])
            return total + jnp.sum(ug.astype(F32), axis=0, keepdims=True)

        ebg_ref[q, 0:1, :] = lax.fori_loop(0, tiles, tile, zero)

        @pl.when(q > 0)
        def _():
            moved(0, q - 1, de_hbm).wait()
            moved(1, q - 1, ds_hbm).wait()

        for n in range(width // RT):
            cols = slice(n * RT, (n + 1) * RT)
            stage[0, cols, :] = tn(ug_s[:, cols], nl_s[...]).astype(BF)
            stage[1, cols, :] = tn(act_s[q, :, cols], bg_s[...]).astype(BF)
        moved(0, q, de_hbm).start()
        moved(1, q, ds_hbm).start()

    def first_norm(i, sums):
        r = rows_at(i, RT)
        g = s1g_ref[r, :]
        n = n1_s[r, :]
        m = g * g1
        out = r1_s[r, 0:1] * (m - mean(m) - n * mean(m * n))
        s1g_ref[r, :] = out
        ag = out.astype(BF)
        ug_s[r, :] = ag

        @pl.loop(0, used)
        def _(q):
            do_ref[q, r, :] = nt(ag, wo_ref[q]).astype(BF)
            dot_ref[q, :, r] = nt(wo_ref[q], ag).astype(BF)

        return (sums[0] + jnp.sum(g * n, axis=0, keepdims=True),
                sums[1] + jnp.sum(g, axis=0, keepdims=True),
                sums[2] + jnp.sum(ag.astype(F32), axis=0, keepdims=True))

    g1g, b1g, obg = lax.fori_loop(0, tiles, first_norm, (zero, zero, zero))
    vg_ref[4:5, :] = g1g
    vg_ref[5:6, :] = b1g
    vg_ref[2:3, :] = obg

    @pl.loop(0, used)
    def _(q):
        dwo_ref[q] = tn(ctx_ref[q], ug_s[...]).astype(BF)

    moved(0, used - 1, de_hbm).wait()
    moved(1, used - 1, ds_hbm).wait()


def run_middle(scal, x, ctx, wo, e, s, vec, eb, cot):
    groups, feat, width = wo.shape
    tokens = x.shape[0]
    vm = pl.BlockSpec(memory_space=pltpu.VMEM)
    sds = jax.ShapeDtypeStruct
    return pl.pallas_call(
        middle,
        name="middle",
        out_shape=(
            sds((tokens, width), BF), sds((tokens, width), F32),
            sds((groups, tokens, feat), BF), sds((groups, feat, tokens), BF),
            sds((groups, feat, width), BF), sds((8, width), F32), sds((groups, 8, width), F32),
            sds(e.shape, BF), sds(s.shape, BF)),
        in_specs=[pl.BlockSpec(memory_space=pltpu.SMEM)] + [vm] * 8,
        out_specs=(vm,) * 7 + (pl.BlockSpec(memory_space=pl.ANY),) * 2,
        scratch_shapes=[
            pltpu.VMEM((tokens, width), BF), pltpu.VMEM((tokens, width), F32),
            pltpu.VMEM((tokens, 128), F32), pltpu.VMEM((tokens, width), F32),
            pltpu.VMEM((groups, tokens, width), BF), pltpu.VMEM((groups, tokens, width), BF),
            pltpu.VMEM((tokens, width), BF), pltpu.VMEM((tokens, width), BF),
            pltpu.VMEM((2, width, width), BF), pltpu.SemaphoreType.DMA((2,))],
        compiler_params=pltpu.CompilerParams(vmem_limit_bytes=62 << 20),
    )(scal, x, ctx, wo, e, s, vec, eb, cot)


def attn_specs(tokens, width, feat):
    def at_quarter(*block):
        return pl.BlockSpec((1,) + block, lambda q, s, b: (jnp.minimum(q, s[0]), 0, 0))

    def whole(*block):
        return pl.BlockSpec(block, lambda q, s, b: (0, 0))

    return at_quarter, whole


def run_fwd(scal, bounds, x, wq, wk, wv, bias, segc, segr):
    groups, feat, width = wq.shape
    tokens = x.shape[0]
    heads = feat // HEAD_DIM
    at_quarter, whole = attn_specs(tokens, width, feat)
    sds = jax.ShapeDtypeStruct
    return pl.pallas_call(
        attn_fwd,
        name="attn_fwd",
        out_shape=(sds((groups, tokens, feat), BF), sds((groups, tokens, 128), F32)),
        grid_spec=pltpu.PrefetchScalarGridSpec(
            num_scalar_prefetch=2, grid=(groups,),
            in_specs=[whole(tokens, width)] + [at_quarter(feat, width)] * 3
            + [at_quarter(8, feat), whole(tokens, 128), whole(8, tokens)],
            out_specs=(at_quarter(tokens, feat), at_quarter(tokens, 128)),
            scratch_shapes=[
                pltpu.VMEM((tokens, feat), BF), pltpu.VMEM((heads, feat, tokens), BF),
                pltpu.VMEM((heads, tokens, feat), BF), pltpu.VMEM((heads, BR, tokens), F32),
                pltpu.VMEM((heads, BR, BC), F32)]),
        compiler_params=pltpu.CompilerParams(vmem_limit_bytes=60 << 20),
    )(scal, bounds, x, wq, wk, wv, bias, segc, segr)


def run_bwd(scal, bounds, x, wq, wk, wv, bias, bcol, segc, segr, ctx, lse, do, dot, s1g):
    groups, feat, width = wq.shape
    tokens = x.shape[0]
    heads = feat // HEAD_DIM
    at_quarter, whole = attn_specs(tokens, width, feat)
    sds = jax.ShapeDtypeStruct
    return pl.pallas_call(
        attn_bwd,
        name="attn_bwd",
        out_shape=(sds((tokens, width), F32),) + (sds((groups, feat, width), BF),) * 3
        + (sds((groups, 16, feat), F32),),
        grid_spec=pltpu.PrefetchScalarGridSpec(
            num_scalar_prefetch=2, grid=(groups,),
            in_specs=[whole(tokens, width)] + [at_quarter(feat, width)] * 3
            + [at_quarter(8, feat), at_quarter(feat, 128), whole(tokens, 128), whole(8, tokens),
               at_quarter(tokens, feat), at_quarter(tokens, 128), at_quarter(tokens, feat),
               at_quarter(feat, tokens), whole(tokens, width)],
            out_specs=(whole(tokens, width),) + (at_quarter(feat, width),) * 3 + (at_quarter(16, feat),),
            scratch_shapes=[
                pltpu.VMEM((tokens, feat), BF), pltpu.VMEM((feat, tokens), BF),
                pltpu.VMEM((heads, tokens, feat), BF), pltpu.VMEM((heads, feat, tokens), BF),
                pltpu.VMEM((heads, feat, tokens), BF), pltpu.VMEM((tokens, feat), BF),
                pltpu.VMEM((feat, tokens), BF), pltpu.VMEM((feat, tokens), BF),
                pltpu.VMEM((feat, tokens), F32), pltpu.VMEM((feat, tokens), F32)]),
        compiler_params=pltpu.CompilerParams(vmem_limit_bytes=60 << 20),
    )(scal, bounds, x, wq, wk, wv, bias, bcol, segc, segr, ctx, lse, do, dot, s1g)


def columns(array):
    return jnp.broadcast_to(array[:, :, None], array.shape + (128,)).astype(BF)


def gather_all(pack):
    return lax.all_gather(pack, ("width", "tok"), axis=0, tiled=False)


def scatter_all(terms):
    flat = terms.reshape((-1,) + terms.shape[2:])
    return lax.psum_scatter(flat, ("width", "tok"), scatter_dimension=0, tiled=True)[0]


def local(tokens_in, seq_lengths, *rest):
    weights, biases, out_grad = rest[:6], rest[6:15], rest[15]
    groups = lax.axis_size("width")
    shards = lax.axis_size("tok")
    level = lax.axis_index("width")
    tokens, width = tokens_in.shape
    owned = weights[0].shape[0]
    owned_ff = weights[4].shape[0]
    feat = owned * shards
    units = owned_ff * shards

    small = jnp.concatenate(biases)
    small = jnp.pad(small, (0, width - small.shape[0]))[None, :]
    small = jnp.pad(small, ((0, 7), (0, 0)))
    got = gather_all(jnp.concatenate(weights + (small,), axis=0))
    got = got.reshape((groups, shards) + got.shape[1:])

    def rows(lower, count):
        return got[:, :, lower : lower + count].reshape(groups, count * shards, width)

    wq, wk, wv, wo = (rows(n * owned, owned) for n in range(4))
    we, ws = rows(4 * owned, owned_ff), rows(4 * owned + owned_ff, owned_ff)
    row = got[:, :, 4 * owned + 2 * owned_ff]
    sizes = [b.shape[0] for b in biases]
    starts = [sum(sizes[:n]) for n in range(9)]
    vecs = [row[:, :, a : a + n].reshape(groups, n * shards) for a, n in zip(starts, sizes)]
    eb = jnp.pad(vecs[3][:, None, :].astype(F32), ((0, 0), (0, 7), (0, 0)))
    order = [vecs[0], vecs[1], vecs[2], vecs[4]] + vecs[5:]
    vec = jnp.stack([v.reshape(-1) for v in order]).astype(F32)
    bias = jnp.pad(jnp.stack([vecs[0], vecs[1]], axis=1).astype(F32), ((0, 0), (0, 6), (0, 0)))
    bcol = jnp.pad(jnp.stack([vecs[0], vecs[1]], axis=2), ((0, 0), (0, 0), (0, 126)))

    ends = jnp.cumsum(seq_lengths[0])
    positions = jnp.arange(tokens, dtype=jnp.int32)
    segment = jnp.sum((positions[:, None] >= ends[None, :]).astype(jnp.int32), axis=1)
    lows = jnp.sum((segment[None, :] < segment[::BR, None]).astype(jnp.int32), axis=1)
    highs = jnp.sum((segment[None, :] <= segment[BR - 1 :: BR, None]).astype(jnp.int32), axis=1)
    bounds = jnp.stack([lows // BC, (highs + BC - 1) // BC])
    segc = jnp.broadcast_to(segment[:, None], (tokens, 128))
    segr = jnp.broadcast_to(segment[None, :], (8, tokens))
    scal = level[None].astype(jnp.int32)

    ctx, lse = run_fwd(scal, bounds, tokens_in, wq, wk, wv, bias, segc, segr)
    result, s1g, do, dot, dwo, vg, ebg, de, ds = run_middle(
        scal, tokens_in, ctx, wo, we, ws, vec, eb, out_grad[0])
    input_grad, dwq, dwk, dwv, db = run_bwd(
        scal, bounds, tokens_in, wq, wk, wv, bias, bcol, segc, segr, ctx, lse, do, dot, s1g)

    mine = jnp.arange(groups) <= level

    def pieces(term):
        return term.reshape((groups, shards, -1) + term.shape[2:])

    def split(line):
        return line.reshape(groups, shards, -1)

    def only(term):
        return jnp.where(mine.reshape((groups,) + (1,) * (term.ndim - 1)), term, jnp.zeros_like(term))

    lines = [
        only(split(db[:, 0])), only(split(db[:, 8])), split(vg[2]), only(split(ebg[:, 0])),
        split(vg[3]), split(vg[4]), split(vg[5]), split(vg[6]), split(vg[7])]
    line = jnp.concatenate(lines, axis=2).astype(BF)
    line = jnp.pad(line, ((0, 0), (0, 0), (0, width - line.shape[2])))
    line = jnp.pad(line[:, :, None, :], ((0, 0), (0, 0), (0, 7), (0, 0)))
    terms = only(jnp.concatenate([pieces(t) for t in (dwq, dwk, dwv, dwo, de, ds)], axis=2))
    final = scatter_all(jnp.concatenate([terms, line], axis=2)).astype(F32)
    outs = [final[n * owned : (n + 1) * owned] for n in range(4)]
    outs += [final[4 * owned : 4 * owned + owned_ff], final[4 * owned + owned_ff : 4 * owned + 2 * owned_ff]]
    last = final[4 * owned + 2 * owned_ff]
    outs += [last[a : a + n] for a, n in zip(starts, sizes)]
    return (result[None], input_grad[None]) + tuple(outs)


def solution(mesh):
    both = ("width", "tok")
    placed = (P("tok", None), P("tok", None)) + (P(both, None),) * 6 + (P(both),) * 9
    return jax.shard_map(
        local,
        mesh=mesh,
        in_specs=placed + (P("width", "tok", None),),
        out_specs=(P("width", "tok", None), P("width", "tok", None))
        + (P(both, None),) * 6 + (P(both),) * 9,
        check_vma=False,
    )
```

time: 1190 us -> 569 us (0.48)
  blocking collectives: 248 us -> 0 us
  waiting for transfers between devices: 621 us -> 428 us
  starting transfers between devices: 73.8 us -> 0.08 us
  matrix products: 71.1 us -> 0 us
  Pallas kernels: 0 us -> 70.9 us
  other arithmetic: 70.8 us -> 11 us
  loops' own time: 28.5 us -> 0 us
  local copies, waits for them, and re-layouts: 58.6 us -> 43.6 us
    reduce_scatter x6 -> x1, waiting for transfers between devices: 40 us -> 323 us  [scatter_all(): lax.psum_scatter(flat, ('width', 'tok'), scatter_dimension=0, tiled=True)[0]]
    all_to_all x15 -> x0, waiting for transfers between devices: 271 us -> none  [the longest x1 74.2 us: local(): lax.all_to_all(shortened(moved[4]), 'tok', split_axis=0, concat_axis=0, t...]
    unnamed x2 -> x0, blocking collectives: 248 us -> none
    all_gather x6 -> x1, waiting for transfers between devices: 306 us -> 105 us  [gather_all(): return lax.all_gather(pack, ('width', 'tok'), axis=0, tiled=False)]
    all_to_all x15 -> x0, starting transfers between devices: 73.3 us -> none  [the longest x1 16 us: local(): lax.all_to_all(shortened(moved[5]), 'tok', split_axis=0, concat_axis=0, t...]
    dot_general x30 -> x0, matrix products: 71.1 us -> none  [the longest x6 21.5 us: dot_rows(): lax.dot_general(left, right, (((1,), (1,)), ((), ())), preferred_element_...]
    pallas_call x0 -> x3, Pallas kernels: none -> 70.9 us  [the longest x1 30.9 us: run_middle(): pl.pallas_call(middle, name='middle', out_shape=(sds((tokens, width), BF)...]
    reduce_sum x27 -> x2, other arithmetic: 30.6 us -> 0.31 us  [the longest x1 0.22 us: local(): jnp.sum((segment[None, :] < segment[::BR, None]).astype(jnp.int32), axis=1)]
  transfers between devices with their start and end apart: 27 -> 2, of which waited for: 22 -> 2; matrix products, arithmetic and copies ran while one was open for 6% -> 0% of each run, Pallas kernels for 0% -> 0%
where the time goes in v1:
time: 569 us; the launch traced here: 568 us
  waiting for transfers between devices  428 us (75%)
  Pallas kernels  70.9 us (12%)
  local copies, waits for them, and re-layouts  43.6 us (8%)
  between operations  14.4 us (3%)
  other arithmetic  11 us (2%)
    reduce_scatter x1, waiting for transfers between devices, scatter_all(): lax.psum_scatter(flat, ('width', 'tok'), scatter_dimension=0, tiled=True)[0]  323 us
    all_gather x1, waiting for transfers between devices, gather_all(): return lax.all_gather(pack, ('width', 'tok'), axis=0, tiled=False)  105 us
    pallas_call x1, Pallas kernels, run_middle(): pl.pallas_call(middle, name='middle', out_shape=(sds((tokens, width), BF)...  30.9 us
    pallas_call x1, Pallas kernels, run_bwd(): pl.pallas_call(attn_bwd, name='attn_bwd', out_shape=(sds((tokens, width),...  25.6 us
    pallas_call x1, Pallas kernels, run_fwd(): pl.pallas_call(attn_fwd, name='attn_fwd', out_shape=(sds((groups, tokens,...  14.4 us
    unnamed x23, local copies, waits for them, and re-layouts  13 us
    slice x2, local copies, waits for them, and re-layouts, rows(): return got[:, :, lower:lower + count].reshape(groups, count * shards, width)  12.6 us
  transfers between devices with their start and end apart: 2, of which 2 were waited for; matrix products, arithmetic and copies ran while one was open for 0% of the time, Pallas kernels for 0%

profile of v1, /device:TPU:0, one launch (start us, length us, event | category | flops | bytes accessed | tf_op | source)
XLA Modules:
  0.0 568.2 jit_solution(9763823032788523508)
XLA Ops:
  7.2 6.1 %concatenate.16 = bf16[288]{0:T(512)(128)(2,1)S(1)} concatenate(bf16[24]{0:T(256)(128)(2,1)} %param.26, bf16[24]{0:T(256)(128)(2,1)} %param.27, bf16[24]{0:T(256)(128)(2,1)} %param.28, bf16[96]{0:T(256)(128)(2,1)} %param.29, bf16[24]{0:T(256)(128)(2,1)} %param.30, bf16[24]{0:T(256)(128)(2,1)} %param.31, bf16[24]{0:T(256)(128)(2,1)} %param.32, bf16[24]{0:T(256)(128)(2,1)} %param.33, ...), dimensions={0} | concatenate | bytes 1152 | tf_op jit(solution)/shard_map/concatenate | solution.py:430
  13.4 0.8 constant_dynamic-update-slice_fusion.6
  14.1 0.8 constant_dynamic-update-slice_fusion.5
  14.9 0.8 constant_dynamic-update-slice_fusion.4
  15.7 0.8 constant_dynamic-update-slice_fusion.3
  16.4 0.9 constant_dynamic-update-slice_fusion.2
  17.4 0.9 constant_dynamic-update-slice_fusion.1
  18.3 0.8 copy-done.1
  19.2 0.7 copy.52
  19.9 0.1 reduce
  20.3 0.2 convert_reduce_fusion.2
  20.6 0.5 pad_add_fusion.bounds
  21.1 105.1 %all-gather.3.cloned.1.call-done = bf16[9472,768]{1,0:T(8,128)(2,1)} async-done(((bf16[296,768]{1,0:T(8,128)(2,1)}), bf16[9472,768]{1,0:T(8,128)(2,1)}) %all-gather.3.cloned.1.call-update) | async-done | bytes 14549008 | tf_op jit(solution)/shard_map/all_gather | solution.py:411
  126.2 1.0 slice.247
  127.5 0.1 stack_reshape_reshape.25
  127.8 0.1 stack_reshape_reshape.24
  128.0 4.6 fusion.7
  132.6 8.0 %fusion.6 = (bf16[4,8,96,768]{3,2,1,0:T(8,128)(2,1)}, bf16[4,8,96,768]{3,2,1,0:T(8,128)(2,1)}) fusion(bf16[4,8,296,768]{3,2,1,0:T(8,128)(2,1)} %bitcast.77), kind=kLoop, calls=%fused_computation.70 | loop fusion | bytes 18874368 | tf_op jit(solution)/shard_map/slice | solution.py:437
  140.7 0.1 stack_reshape_reshape.31
  140.8 0.1 stack_reshape_reshape.30
  140.9 0.1 stack_reshape_reshape.29
  141.3 0.6 convert_element_type.49.vec_ref
  142.0 0.7 pad_convert_fusion.eb_ref
  142.6 0.2 copy.57
  142.8 0.7 pad.38.bcol_ref
  143.5 0.6 fusion.5.bias_ref
  144.2 0.6 lt.6.segr_ref
  144.8 1.0 broadcast_in_dim.66.segc_ref
  145.8 14.4 %attn_fwd.1 = (bf16[4,1024,192]{2,1,0:T(8,128)(2,1)}, f32[4,1024,128]{2,1,0:T(8,128)}) custom-call(s32[1]{0:T(128)} %bitcast.scal, s32[2,8]{1,0:T(2,128)} %pad_add_fusion.bounds, bf16[1024,768]{1,0:T(8,128)(2,1)} %x_ref.5, bf16[4,192,768]{2,1,0:T(8,128)(2,1)} %bitcast.82, bf16[4,192,768]{2,1,0:T(8,128)(2,1)} %bitcast.80, bf16[4,192,768]{2,1,0:T(8,128)(2,1)} %bitcast.78, ...), custom_call_target="tpu_custom_call" | custom-call | tf_op jit(solution)/shard_map/attn_fwd/pallas_call | solution.py:361
  160.2 30.9 %middle.1 = (bf16[1024,768]{1,0:T(8,128)(2,1)}, f32[1024,768]{1,0:T(8,128)}, bf16[4,1024,192]{2,1,0:T(8,128)(2,1)}, bf16[4,192,1024]{2,1,0:T(8,128)(2,1)}, bf16[...) custom-call(s32[1]{0:T(128)} %bitcast.scal, ...), custom_call_target="tpu_custom_call" | custom-call | tf_op jit(solution)/shard_map/middle/pallas_call | solution.py:325
  191.1 25.6 %attn_bwd.1 = (f32[1024,768]{1,0:T(8,128)}, bf16[4,192,768]{2,1,0:T(8,128)(2,1)}, bf16[4,192,768]{2,1,0:T(8,128)(2,1)}, bf16[4,192,768]{2,1,0:T(8,128)(2,1)}, f32[4,16,192]{2,1,0:T(8,128)}) custom-call(s32[1]{0:T(128)} %bitcast.scal, s32[2,8]{1,0:T(2,128)} %pad_add_fusion.bounds, bf16[1024,768]{1,0:T(8,128)(2,1)} %x_ref.5, bf16[4,192,768]{2,1,0:T(8,128)(2,1)} %bitcast.83, ...), custom_call_target="tpu_custom_call" | custom-call | tf_op jit(solution)/shard_map/attn_bwd/pallas_call | solution.py:384
  216.8 0.8 slice_reduce_fusion.1
  217.7 0.9 slice_reduce_fusion
  219.6 0.1 concatenate.19
  219.8 1.6 constant_dynamic-update-slice_fusion.12
  221.4 1.4 constant_dynamic-update-slice_fusion.11
  222.8 1.4 constant_dynamic-update-slice_fusion.10
  224.3 0.1 constant_dynamic-update-slice_fusion.9
  224.4 2.7 constant_dynamic-update-slice_fusion.8
  227.1 0.4 constant_dynamic-update-slice_fusion.7
  227.5 1.4 broadcast_select_fusion
  229.0 5.3 fusion.1
  234.3 323.1 %reduce-scatter.2.cloned.1.call-done = bf16[1,296,768]{2,1,0:T(8,128)(2,1)} async-done(((bf16[32,296,768]{2,1,0:T(8,128)(2,1)}), bf16[1,296,768]{2,1,0:T(8,128)(2,1)}) %reduce-scatter.2.cloned.1.call-update) | async-done | bytes 454672 | tf_op jit(solution)/shard_map/reduce_scatter | solution.py:416
  557.5 1.1 convert_bitcast_fusion
  558.6 0.6 slice_bitcast_fusion.11
  559.2 0.6 slice_bitcast_fusion.6
  559.8 0.7 slice_bitcast_fusion.2
  560.5 0.8 slice_bitcast_fusion
  (51 shorter events, 2.5 us)
Async XLA Ops:
  7.2 119.0 %all-gather.3.cloned.1.call-start = ((), (), s32[]{:S(2)}) async-start(), calls=%async_computation.2 | async-start | bytes 15003648 | tf_op jit(solution)/shard_map/all_gather | solution.py:411
  18.3 0.8 copy-start.1
  19.1 538.4 %reduce-scatter.2.cloned.1.call-start = ((), (), s32[]{:S(2)}) async-start(), calls=%async_computation.1 | async-start | bytes 15003648 | tf_op jit(solution)/shard_map/reduce_scatter | solution.py:416
  191.1 27.7 %copy-start.2 = (f32[8,768]{1,0:T(8,128)S(1)}, f32[8,768]{1,0:T(8,128)}, u32[]{:S(2)}) copy-start(f32[8,768]{1,0:T(8,128)} %get-tuple-element.47) | copy-start | bytes 73732
  191.1 33.1 %copy-start = (bf16[4,192,768]{2,1,0:T(8,128)(2,1)S(1)}, bf16[4,192,768]{2,1,0:T(8,128)(2,1)}, u32[]{:S(2)}) copy-start(bf16[4,192,768]{2,1,0:T(8,128)(2,1)} %get-tuple-element.43) | copy-start | bytes 3538948
  191.1 36.0 %slice-start = ((s8[4718592]{0:T(1024)(128)(4,1)}), s8[524288]{0:T(1024)(128)(4,1)S(1)}, s32[]{:S(2)}) async-start(s8[4718592]{0:T(1024)(128)(4,1)} %bitcast.85), calls=%async_computation.3 | async-start | bytes 1048576
  219.8 7.3 %slice-start.1 = ((s8[4718592]{0:T(1024)(128)(4,1)}), s8[4194304]{0:T(1024)(128)(4,1)S(1)}, s32[]{:S(2)}) async-start(s8[4718592]{0:T(1024)(128)(4,1)} %bitcast.85), calls=%async_computation.4 | async-start | bytes 8388608
Sparse Core Ops, SparseCore 0:
  19.2 106.9 all-gather.2
  234.4 322.9 reduce-scatter.1

commit v2 on v1

--- a/solution.py
+++ b/solution.py
@@ -325,6 +325,7 @@
     return pl.pallas_call(
         middle,
         name="middle",
+        cost_estimate=pl.CostEstimate(flops=int(50e9), bytes_accessed=int(30e6), transcendentals=0),
         out_shape=(
             sds((tokens, width), BF), sds((tokens, width), F32),
             sds((groups, tokens, feat), BF), sds((groups, feat, tokens), BF),
@@ -361,6 +362,7 @@
     return pl.pallas_call(
         attn_fwd,
         name="attn_fwd",
+        cost_estimate=pl.CostEstimate(flops=int(40e9), bytes_accessed=int(30e6), transcendentals=0),
         out_shape=(sds((groups, tokens, feat), BF), sds((groups, tokens, 128), F32)),
         grid_spec=pltpu.PrefetchScalarGridSpec(
             num_scalar_prefetch=2, grid=(groups,),
@@ -384,6 +386,7 @@
     return pl.pallas_call(
         attn_bwd,
         name="attn_bwd",
+        cost_estimate=pl.CostEstimate(flops=int(90e9), bytes_accessed=int(30e6), transcendentals=0),
         out_shape=(sds((tokens, width), F32),) + (sds((groups, feat, width), BF),) * 3
         + (sds((groups, 16, feat), F32),),
         grid_spec=pltpu.PrefetchScalarGridSpec(
@@ -430,15 +433,18 @@
     small = jnp.concatenate(biases)
     small = jnp.pad(small, (0, width - small.shape[0]))[None, :]
     small = jnp.pad(small, ((0, 7), (0, 0)))
-    got = gather_all(jnp.concatenate(weights + (small,), axis=0))
+    got = gather_all(jnp.concatenate(weights[:3] + (small,), axis=0))
     got = got.reshape((groups, shards) + got.shape[1:])
-
-    def rows(lower, count):
-        return got[:, :, lower : lower + count].reshape(groups, count * shards, width)
-
-    wq, wk, wv, wo = (rows(n * owned, owned) for n in range(4))
-    we, ws = rows(4 * owned, owned_ff), rows(4 * owned + owned_ff, owned_ff)
-    row = got[:, :, 4 * owned + 2 * owned_ff]
+    late = gather_all(jnp.concatenate(weights[3:], axis=0))
+    late = late.reshape((groups, shards) + late.shape[1:])
+
+    def rows(source, lower, count):
+        return source[:, :, lower : lower + count].reshape(groups, count * shards, width)
+
+    wq, wk, wv = (rows(got, n * owned, owned) for n in range(3))
+    wo = rows(late, 0, owned)
+    we, ws = rows(late, owned, owned_ff), rows(late, owned + owned_ff, owned_ff)
+    row = got[:, :, 3 * owned]
     sizes = [b.shape[0] for b in biases]
     starts = [sum(sizes[:n]) for n in range(9)]
     vecs = [row[:, :, a : a + n].reshape(groups, n * shards) for a, n in zip(starts, sizes)]
@@ -461,19 +467,24 @@
     ctx, lse = run_fwd(scal, bounds, tokens_in, wq, wk, wv, bias, segc, segr)
     result, s1g, do, dot, dwo, vg, ebg, de, ds = run_middle(
         scal, tokens_in, ctx, wo, we, ws, vec, eb, out_grad[0])
+    mine = jnp.arange(groups) <= level
+
+    def pieces(term):
+        return term.reshape((groups, shards, -1) + term.shape[2:])
+
+    def split(line):
+        return line.reshape(groups, shards, -1)
+
+    def only(term):
+        return jnp.where(mine.reshape((groups,) + (1,) * (term.ndim - 1)), term, jnp.zeros_like(term))
+
+    def packed(*terms):
+        return only(jnp.concatenate([pieces(t) for t in terms], axis=2))
+
+    first, s1g = lax.optimization_barrier((packed(dwo, de, ds), s1g))
+    early = scatter_all(first)
     input_grad, dwq, dwk, dwv, db = run_bwd(
         scal, bounds, tokens_in, wq, wk, wv, bias, bcol, segc, segr, ctx, lse, do, dot, s1g)
-
-    mine = jnp.arange(groups) <= level
-
-    def pieces(term):
-        return term.reshape((groups, shards, -1) + term.shape[2:])
-
-    def split(line):
-        return line.reshape(groups, shards, -1)
-
-    def only(term):
-        return jnp.where(mine.reshape((groups,) + (1,) * (term.ndim - 1)), term, jnp.zeros_like(term))
 
     lines = [
         only(split(db[:, 0])), only(split(db[:, 8])), split(vg[2]), only(split(ebg[:, 0])),
@@ -481,11 +492,13 @@
     line = jnp.concatenate(lines, axis=2).astype(BF)
     line = jnp.pad(line, ((0, 0), (0, 0), (0, width - line.shape[2])))
     line = jnp.pad(line[:, :, None, :], ((0, 0), (0, 0), (0, 7), (0, 0)))
-    terms = only(jnp.concatenate([pieces(t) for t in (dwq, dwk, dwv, dwo, de, ds)], axis=2))
-    final = scatter_all(jnp.concatenate([terms, line], axis=2)).astype(F32)
-    outs = [final[n * owned : (n + 1) * owned] for n in range(4)]
-    outs += [final[4 * owned : 4 * owned + owned_ff], final[4 * owned + owned_ff : 4 * owned + 2 * owned_ff]]
-    last = final[4 * owned + 2 * owned_ff]
+    second = jnp.concatenate([packed(dwq, dwk, dwv), line], axis=2)
+    second, early = lax.optimization_barrier((second, early))
+    early = early.astype(F32)
+    final = scatter_all(second).astype(F32)
+    outs = [final[n * owned : (n + 1) * owned] for n in range(3)]
+    outs += [early[:owned], early[owned : owned + owned_ff], early[owned + owned_ff :]]
+    last = final[3 * owned]
     outs += [last[a : a + n] for a, n in zip(starts, sizes)]
     return (result[None], input_grad[None]) + tuple(outs)
 

time: 569 us -> 522 us (0.917)
  waiting for transfers between devices: 428 us -> 372 us
  other arithmetic: 11 us -> 22.8 us
  local copies, waits for them, and re-layouts: 43.6 us -> 33.4 us
  Pallas kernels: 70.9 us -> 78.2 us
    reduce_scatter x1 -> x2, waiting for transfers between devices: 323 us -> 250 us  [scatter_all(): lax.psum_scatter(flat, ('width', 'tok'), scatter_dimension=0, tiled=True)[0]]
    all_gather x1 -> x2, waiting for transfers between devices: 105 us -> 122 us  [gather_all(): return lax.all_gather(pack, ('width', 'tok'), axis=0, tiled=False)]
    unnamed x23 -> x6, local copies, waits for them, and re-layouts: 13 us -> 1.04 us
    select_n x1 -> x2, other arithmetic: 1.44 us -> 13.3 us  [only(): jnp.where(mine.reshape((groups,) + (1,) * (term.ndim - 1)), term, jnp.zer...]
    pallas_call x3, Pallas kernels: 70.9 us -> 78.2 us  [the longest x1 30.6 us: run_middle(): pl.pallas_call(middle, name='middle', cost_estimate=pl.CostEstimate(flops...]
    slice x5 -> x7, local copies, waits for them, and re-layouts: 15.2 us -> 17.4 us  [the longest x3 14.2 us: rows(): source[:, :, lower:lower + count].reshape(groups, count * shards, width)]
  transfers between devices with their start and end apart: 2 -> 4, of which waited for: 2 -> 4; matrix products, arithmetic and copies ran while one was open for 0% -> 5% of each run, Pallas kernels for 0% -> 9%
where the time goes in v2:
time: 522 us; the launch traced here: 521 us
  waiting for transfers between devices  372 us (71%)
  Pallas kernels  78.2 us (15%)
  local copies, waits for them, and re-layouts  33.4 us (6%)
  other arithmetic  22.8 us (4%)
  between operations  14 us (3%)
    reduce_scatter x2, waiting for transfers between devices, scatter_all(): lax.psum_scatter(flat, ('width', 'tok'), scatter_dimension=0, tiled=True)[0]  250 us
    all_gather x2, waiting for transfers between devices, gather_all(): return lax.all_gather(pack, ('width', 'tok'), axis=0, tiled=False)  122 us
    pallas_call x1, Pallas kernels, run_middle(): pl.pallas_call(middle, name='middle', cost_estimate=pl.CostEstimate(flops...  30.6 us
    pallas_call x1, Pallas kernels, run_bwd(): pl.pallas_call(attn_bwd, name='attn_bwd', cost_estimate=pl.CostEstimate(f...  30.1 us
    pallas_call x1, Pallas kernels, run_fwd(): pl.pallas_call(attn_fwd, name='attn_fwd', cost_estimate=pl.CostEstimate(f...  17.4 us
    slice x3, local copies, waits for them, and re-layouts, rows(): source[:, :, lower:lower + count].reshape(groups, count * shards, width)  14.2 us
    select_n x2, other arithmetic, only(): jnp.where(mine.reshape((groups,) + (1,) * (term.ndim - 1)), term, jnp.zer...  13.3 us
  transfers between devices with their start and end apart: 4, of which 4 were waited for; matrix products, arithmetic and copies ran while one was open for 5% of the time, Pallas kernels for 9%

profile of v2, /device:TPU:0, one launch (start us, length us, event | category | flops | bytes accessed | tf_op | source)
XLA Modules:
  0.0 520.9 jit_solution(5626010645899410051)
XLA Ops:
  7.2 6.1 %concatenate.22 = bf16[288]{0:T(512)(128)(2,1)S(1)} concatenate(bf16[24]{0:T(256)(128)(2,1)} %param.26, bf16[24]{0:T(256)(128)(2,1)} %param.27, bf16[24]{0:T(256)(128)(2,1)} %param.28, bf16[96]{0:T(256)(128)(2,1)} %param.29, bf16[24]{0:T(256)(128)(2,1)} %param.30, bf16[24]{0:T(256)(128)(2,1)} %param.31, bf16[24]{0:T(256)(128)(2,1)} %param.32, bf16[24]{0:T(256)(128)(2,1)} %param.33, ...), dimensions={0} | concatenate | bytes 1152 | tf_op jit(solution)/shard_map/concatenate | solution.py:433
  13.4 1.5 fusion.3
  14.9 1.7 pad_maximum_fusion
  16.7 0.7 copy.52
  17.5 0.1 reduce
  17.9 0.2 convert_reduce_fusion.2
  18.1 0.6 pad_add_fusion.bounds
  18.7 59.9 %all-gather.5.cloned.1.call-done = bf16[2560,768]{1,0:T(8,128)(2,1)} async-done(((bf16[80,768]{1,0:T(8,128)(2,1)}), bf16[2560,768]{1,0:T(8,128)(2,1)}) %all-gather.5.cloned.1.call-update) | async-done | bytes 3932176 | tf_op jit(solution)/shard_map/all_gather | solution.py:414
  78.6 1.0 slice.235
  79.9 0.1 stack_reshape_reshape.24
  80.1 0.1 stack_reshape_reshape.25
  80.3 0.1 stack_reshape_reshape.26
  80.4 0.1 stack_reshape_reshape.27
  80.5 0.1 stack_reshape_reshape.28
  80.6 0.1 stack_reshape_reshape.29
  80.7 0.1 stack_reshape_reshape.30
  80.8 0.1 stack_reshape_reshape.31
  80.9 0.6 convert_element_type.52.vec_ref
  81.6 0.6 fusion.7.bias_ref
  82.3 0.7 pad_convert_fusion.eb_ref
  82.9 3.8 fusion.9
  86.8 1.0 broadcast_in_dim.77.segc_ref
  87.7 0.6 lt.6.segr_ref
  88.3 17.4 %attn_fwd.1 = (bf16[4,1024,192]{2,1,0:T(8,128)(2,1)}, f32[4,1024,128]{2,1,0:T(8,128)}) custom-call(s32[1]{0:T(128)} %bitcast.scal, s32[2,8]{1,0:T(2,128)} %pad_add_fusion.bounds, bf16[1024,768]{1,0:T(8,128)(2,1)} %x_ref.5, bf16[4,192,768]{2,1,0:T(8,128)(2,1)} %bitcast.89, bf16[4,192,768]{2,1,0:T(8,128)(2,1)} %bitcast.87, bf16[4,192,768]{2,1,0:T(8,128)(2,1)} %bitcast.85, ...), custom_call_target="tpu_custom_call" | custom-call | flops 40000000000 | bytes 30000000 | tf_op jit(solution)/shard_map/attn_fwd/pallas_call | solution.py:362
  105.7 61.9 %all-gather.7.cloned.1.call-done = bf16[6912,768]{1,0:T(8,128)(2,1)} async-done(((bf16[216,768]{1,0:T(8,128)(2,1)}), bf16[6912,768]{1,0:T(8,128)(2,1)}) %all-gather.7.cloned.1.call-update) | async-done | bytes 10616848 | tf_op jit(solution)/shard_map/all_gather | solution.py:414
  167.7 8.0 %fusion.8 = (bf16[4,8,96,768]{3,2,1,0:T(8,128)(2,1)}, bf16[4,8,96,768]{3,2,1,0:T(8,128)(2,1)}) fusion(bf16[4,8,216,768]{3,2,1,0:T(8,128)(2,1)} %bitcast.71), kind=kLoop, calls=%fused_computation.59 | loop fusion | bytes 18874368 | tf_op jit(solution)/shard_map/slice | solution.py:442
  175.6 2.4 slice.238
  178.0 30.6 %middle.1 = (bf16[1024,768]{1,0:T(8,128)(2,1)}, f32[1024,768]{1,0:T(8,128)}, bf16[4,1024,192]{2,1,0:T(8,128)(2,1)}, bf16[4,192,1024]{2,1,0:T(8,128)(2,1)}, bf16[...) custom-call(s32[1]{0:T(128)} %bitcast.scal, ...), custom_call_target="tpu_custom_call" | custom-call | flops 49999998976 | bytes 30000000 | tf_op jit(solution)/shard_map/middle/pallas_call | solution.py:325
  208.7 10.9 %maximum_select_fusion = bf16[4,8,216,768]{3,2,1,0:T(8,128)(2,1)} fusion(bf16[4,8,96,768]{3,2,1,0:T(8,128)(2,1)} %bitcast.76, bf16[4,8,96,768]{3,2,1,0:T(8,128)(2,1)} %bitcast.75, bf16[4,8,24,768]{3,2,1,0:T(8,128)(2,1)} %bitcast.81, pred[4]{0:T(512)(128)(4,1)S(1)} %iota_compare_fusion.4), kind=kLoop, calls=%fused_computation | loop fusion | flops 37158912 | bytes 21233668 | tf_op jit(solution)/shard_map/jit(_where)/select_n | solution.py:479
  219.6 0.2 reduce-scatter.5.cloned.1.call-start
  220.0 0.2 copy.57
  220.2 0.7 pad.38.bcol_ref
  220.9 30.1 %attn_bwd.1 = (f32[1024,768]{1,0:T(8,128)}, bf16[4,192,768]{2,1,0:T(8,128)(2,1)}, bf16[4,192,768]{2,1,0:T(8,128)(2,1)}, bf16[4,192,768]{2,1,0:T(8,128)(2,1)}, f32[4,16,192]{2,1,0:T(8,128)}) custom-call(s32[1]{0:T(128)} %bitcast.scal, s32[2,8]{1,0:T(2,128)} %pad_add_fusion.bounds, bf16[1024,768]{1,0:T(8,128)(2,1)} %x_ref.5, bf16[4,192,768]{2,1,0:T(8,128)(2,1)} %bitcast.90, ...), custom_call_target="tpu_custom_call" | custom-call | flops 89999998976 | bytes 30000000 | tf_op jit(solution)/shard_map/attn_bwd/pallas_call | solution.py:386
  251.1 0.8 slice_reduce_fusion.1
  252.3 0.1 reshape_squeeze.37
  252.8 0.9 slice_reduce_fusion
  253.9 0.1 concatenate.27
  254.1 2.4 maximum_select_fusion.1
  256.6 2.2 fusion.1
  258.8 143.9 %reduce-scatter.3.cloned.1.call-done = bf16[1,216,768]{2,1,0:T(8,128)(2,1)} async-done(((bf16[32,216,768]{2,1,0:T(8,128)(2,1)}), bf16[1,216,768]{2,1,0:T(8,128)(2,1)}) %reduce-scatter.3.cloned.1.call-update) | async-done | bytes 331792 | tf_op jit(solution)/shard_map/reduce_scatter | solution.py:419
  402.6 0.9 copy-done
  403.6 0.6 slice.257
  404.2 0.8 fusion.10
  405.1 106.5 %reduce-scatter.5.cloned.1.call-done = bf16[1,80,768]{2,1,0:T(8,128)(2,1)} async-done(((bf16[32,80,768]{2,1,0:T(8,128)(2,1)}), bf16[1,80,768]{2,1,0:T(8,128)(2,1)}) %reduce-scatter.5.cloned.1.call-update) | async-done | bytes 122896 | tf_op jit(solution)/shard_map/reduce_scatter | solution.py:419
  511.6 0.9 convert_bitcast_fusion
  512.5 0.6 slice_bitcast_fusion.3
  513.1 0.6 slice_bitcast_fusion.8
  513.7 0.7 slice_bitcast_fusion
  (42 shorter events, 2.2 us)
Async XLA Ops:
  7.2 71.5 %all-gather.5.cloned.1.call-start = ((), (), s32[]{:S(2)}) async-start(), calls=%async_computation.4 | async-start | bytes 4055040 | tf_op jit(solution)/shard_map/all_gather | solution.py:414
  14.8 152.8 %all-gather.7.cloned.1.call-start = ((), (), s32[]{:S(2)}) async-start(), calls=%async_computation.5 | async-start | bytes 10948608 | tf_op jit(solution)/shard_map/all_gather | solution.py:414
  16.6 386.0 %reduce-scatter.3.cloned.1.call-start = ((), (), s32[]{:S(2)}) async-start(), calls=%async_computation.2 | async-start | bytes 10948608 | tf_op jit(solution)/shard_map/reduce_scatter | solution.py:419
  219.6 292.0 %reduce-scatter.5.cloned.1.call-start = ((), (), s32[]{:S(2)}) async-start(), calls=%async_computation.3 | async-start | bytes 4055040 | tf_op jit(solution)/shard_map/reduce_scatter | solution.py:419
  220.9 31.1 %copy-start.1 = (f32[8,768]{1,0:T(8,128)S(1)}, f32[8,768]{1,0:T(8,128)}, u32[]{:S(2)}) copy-start(f32[8,768]{1,0:T(8,128)} %get-tuple-element.52) | copy-start | bytes 73732
  402.6 1.0 copy-start
Sparse Core Ops, SparseCore 0:
  15.0 63.6 all-gather.4
  82.1 85.4 all-gather.6
  219.7 182.8 reduce-scatter.2
  407.9 103.6 reduce-scatter.4

commit v3 on v2

--- a/solution.py
+++ b/solution.py
@@ -406,6 +406,175 @@
     )(scal, bounds, x, wq, wk, wv, bias, bcol, segc, segr, ctx, lse, do, dot, s1g)
 
 
+PART = 16
+
+
+def peer_copy(src, dst, send, recv, **where):
+    return pltpu.make_async_remote_copy(
+        src_ref=src, dst_ref=dst, send_sem=send, recv_sem=recv,
+        device_id=where, device_id_type=pl.DeviceIdType.MESH)
+
+
+def greet(w, t):
+    barrier = pltpu.get_barrier_semaphore()
+    mesh_id = pl.DeviceIdType.MESH
+    pl.semaphore_signal(barrier, inc=1, device_id={"width": w ^ 1, "tok": t}, device_id_type=mesh_id)
+    pl.semaphore_signal(barrier, inc=1, device_id={"width": w ^ 2, "tok": t}, device_id_type=mesh_id)
+    pl.semaphore_signal(barrier, inc=1, device_id={"width": w, "tok": t ^ 1}, device_id_type=mesh_id)
+    for k in range(1, 4):
+        other = lax.rem(t + 2 * k, 8)
+        pl.semaphore_signal(barrier, inc=1, device_id={"width": w, "tok": other}, device_id_type=mesh_id)
+    pl.semaphore_wait(barrier, 6)
+
+
+def reduce_kernel(g_ref, out_ref, ra, sx, rx, acc, ry, sy, rz,
+                  sa_sem, ra_sem, sx_sem, rx_sem, sy_sem, ry_sem, sz_sem, rz_sem):
+    w = lax.axis_index("width")
+    t = lax.axis_index("tok")
+    y = lax.rem(t, 2)
+    z = lax.div(t, 2)
+    parts = g_ref.shape[3] // PART
+    greet(w, t)
+
+    def rows(p):
+        return pl.ds(pl.multiple_of(p * PART, PART), PART)
+
+    def near(p, slot, quarter):
+        return peer_copy(g_ref.at[quarter, :, :, rows(p), :], ra.at[slot, :, :, rows(p), :],
+                         sa_sem.at[slot, p], ra_sem.at[slot, p], width=w ^ 1, tok=t)
+
+    def across(p):
+        return peer_copy(sx.at[:, :, rows(p), :], rx.at[:, :, rows(p), :],
+                         sx_sem.at[p], rx_sem.at[p], width=w ^ 2, tok=t)
+
+    def beside(p):
+        return peer_copy(acc.at[:, 1 - y, rows(p), :], ry.at[:, rows(p), :],
+                         sy_sem.at[p], ry_sem.at[p], width=w, tok=t ^ 1)
+
+    def along(p, k):
+        there = lax.rem(z + k, 4)
+        return peer_copy(sy.at[there, rows(p), :], rz.at[k - 1, rows(p), :],
+                         sz_sem.at[k - 1, p], rz_sem.at[k - 1, p], width=w, tok=2 * there + y)
+
+    @pl.loop(0, parts)
+    def _(p):
+        @pl.when(w == 3)
+        def _():
+            near(p, 0, 0).start()
+
+        @pl.when(w == 2)
+        def _():
+            near(p, 0, 1).start()
+
+    @pl.loop(0, parts)
+    def _(p):
+        @pl.when(w == 3)
+        def _():
+            near(p, 1, 2).start()
+
+        @pl.when(w == 1)
+        def _():
+            near(p, 0, 0).start()
+
+    @pl.loop(0, parts)
+    def _(p):
+        @pl.when(w >= 2)
+        def _():
+            near(p, 0, 0).wait_recv()
+            far = w - 2
+            sx[:, :, rows(p), :] = (g_ref[far, :, :, rows(p), :].astype(F32)
+                                    + ra[0, :, :, rows(p), :].astype(F32)).astype(BF)
+            across(p).start()
+
+    @pl.loop(0, parts)
+    def _(p):
+        total = g_ref[w, :, :, rows(p), :].astype(F32)
+        acc[:, :, rows(p), :] = total.astype(BF)
+
+        @pl.when(w == 2)
+        def _():
+            near(p, 1, 2).wait_recv()
+            acc[:, :, rows(p), :] = (g_ref[w, :, :, rows(p), :].astype(F32)
+                                     + ra[1, :, :, rows(p), :].astype(F32)).astype(BF)
+
+        @pl.when(w == 1)
+        def _():
+            across(p).wait_recv()
+            acc[:, :, rows(p), :] = (g_ref[w, :, :, rows(p), :].astype(F32)
+                                     + rx[:, :, rows(p), :].astype(F32)).astype(BF)
+
+        @pl.when(w == 0)
+        def _():
+            near(p, 0, 0).wait_recv()
+            across(p).wait_recv()
+            acc[:, :, rows(p), :] = (g_ref[w, :, :, rows(p), :].astype(F32)
+                                     + ra[0, :, :, rows(p), :].astype(F32)
+                                     + rx[:, :, rows(p), :].astype(F32)).astype(BF)
+
+        beside(p).start()
+
+    @pl.loop(0, parts)
+    def _(p):
+        beside(p).wait_recv()
+        sy[:, rows(p), :] = (acc[:, y, rows(p), :].astype(F32) + ry[:, rows(p), :].astype(F32)).astype(BF)
+        for k in range(1, 4):
+            along(p, k).start()
+
+    @pl.loop(0, parts)
+    def _(p):
+        total = sy[z, rows(p), :].astype(F32)
+        for k in range(1, 4):
+            along(p, k).wait_recv()
+            total = total + rz[k - 1, rows(p), :].astype(F32)
+        out_ref[rows(p), :] = total
+
+    @pl.loop(0, parts)
+    def _(p):
+        @pl.when(w == 3)
+        def _():
+            near(p, 0, 0).wait_send()
+            near(p, 1, 2).wait_send()
+
+        @pl.when(w == 2)
+        def _():
+            near(p, 0, 1).wait_send()
+
+        @pl.when(w == 1)
+        def _():
+            near(p, 0, 0).wait_send()
+
+        @pl.when(w >= 2)
+        def _():
+            across(p).wait_send()
+
+        beside(p).wait_send()
+        for k in range(1, 4):
+            along(p, k).wait_send()
+
+
+def reduce_fast(terms):
+    groups, shards, count, width = terms.shape
+    parts = count // PART
+    vm = pl.BlockSpec(memory_space=pltpu.VMEM)
+    dma = pltpu.SemaphoreType.DMA
+    column = (4, 2, count, width)
+    return pl.pallas_call(
+        reduce_kernel,
+        name="reduce_fast",
+        out_shape=jax.ShapeDtypeStruct((count, width), F32),
+        in_specs=[vm],
+        out_specs=vm,
+        scratch_shapes=[
+            pltpu.VMEM((2,) + column, BF), pltpu.VMEM(column, BF), pltpu.VMEM(column, BF),
+            pltpu.VMEM(column, BF), pltpu.VMEM((4, count, width), BF), pltpu.VMEM((4, count, width), BF),
+            pltpu.VMEM((3, count, width), BF),
+            dma((2, parts)), dma((2, parts)), dma((parts,)), dma((parts,)),
+            dma((parts,)), dma((parts,)), dma((3, parts)), dma((3, parts))],
+        compiler_params=pltpu.CompilerParams(
+            collective_id=1, has_side_effects=True, vmem_limit_bytes=40 << 20),
+    )(terms.reshape((groups, 4, 2, count, width)))
+
+
 def columns(array):
     return jnp.broadcast_to(array[:, :, None], array.shape + (128,)).astype(BF)
 
@@ -481,25 +650,31 @@
     def packed(*terms):
         return only(jnp.concatenate([pieces(t) for t in terms], axis=2))
 
-    first, s1g = lax.optimization_barrier((packed(dwo, de, ds), s1g))
+    def lined(*lines):
+        line = jnp.concatenate(lines, axis=2).astype(BF)
+        line = jnp.pad(line, ((0, 0), (0, 0), (0, width - line.shape[2])))
+        return jnp.pad(line[:, :, None, :], ((0, 0), (0, 0), (0, 7), (0, 0)))
+
+    line = lined(only(split(ebg[:, 0])), *(split(vg[n]) for n in range(2, 8)))
+    first = jnp.concatenate([packed(dwo, de, ds), line], axis=2)
+    first, s1g = lax.optimization_barrier((first, s1g))
     early = scatter_all(first)
     input_grad, dwq, dwk, dwv, db = run_bwd(
         scal, bounds, tokens_in, wq, wk, wv, bias, bcol, segc, segr, ctx, lse, do, dot, s1g)
 
-    lines = [
-        only(split(db[:, 0])), only(split(db[:, 8])), split(vg[2]), only(split(ebg[:, 0])),
-        split(vg[3]), split(vg[4]), split(vg[5]), split(vg[6]), split(vg[7])]
-    line = jnp.concatenate(lines, axis=2).astype(BF)
-    line = jnp.pad(line, ((0, 0), (0, 0), (0, width - line.shape[2])))
-    line = jnp.pad(line[:, :, None, :], ((0, 0), (0, 0), (0, 7), (0, 0)))
+    line = lined(only(split(db[:, 0])), only(split(db[:, 8])))
     second = jnp.concatenate([packed(dwq, dwk, dwv), line], axis=2)
-    second, early = lax.optimization_barrier((second, early))
+    if groups == 4 and shards == 8 and owned % 8 == 0:
+        final = reduce_fast(second)
+    else:
+        final = scatter_all(second).astype(F32)
     early = early.astype(F32)
-    final = scatter_all(second).astype(F32)
     outs = [final[n * owned : (n + 1) * owned] for n in range(3)]
-    outs += [early[:owned], early[owned : owned + owned_ff], early[owned + owned_ff :]]
-    last = final[3 * owned]
-    outs += [last[a : a + n] for a, n in zip(starts, sizes)]
+    outs += [early[:owned], early[owned : owned + owned_ff], early[owned + owned_ff : owned + 2 * owned_ff]]
+    late = final[3 * owned]
+    soon = early[owned + 2 * owned_ff]
+    vecs = [soon[owned_ff + n * owned : owned_ff + (n + 1) * owned] for n in range(6)]
+    outs += [late[:owned], late[owned : 2 * owned], vecs[0], soon[:owned_ff]] + vecs[1:]
     return (result[None], input_grad[None]) + tuple(outs)
 
 

time: 522 us -> 431 us (0.83)
  waiting for transfers between devices: 372 us -> 129 us
  Pallas kernels: 78.2 us -> 230 us
    reduce_scatter x2 -> x1, waiting for transfers between devices: 250 us -> 6.45 us  [scatter_all(): lax.psum_scatter(flat, ('width', 'tok'), scatter_dimension=0, tiled=True)[0]]
    pallas_call x0 -> x1, Pallas kernels: none -> 154 us  [reduce_fast(): pl.pallas_call(reduce_kernel, name='reduce_fast', out_shape=jax.ShapeDtyp...]
    concatenate x0 -> x1, other arithmetic: none -> 5.36 us  [local(): first = jnp.concatenate([packed(dwo, de, ds), line], axis=2)]
  transfers between devices with their start and end apart: 4 -> 3, of which waited for: 4 -> 3; matrix products, arithmetic and copies ran while one was open for 5% -> 5% of each run, Pallas kernels for 9% -> 46%
where the time goes in v3:
time: 431 us; the launch traced here: 430 us
  Pallas kernels  230 us (53%)
  waiting for transfers between devices  129 us (30%)
  local copies, waits for them, and re-layouts  33 us (8%)
  other arithmetic  23.7 us (5%)
  between operations  14 us (3%)
    pallas_call x1, Pallas kernels, reduce_fast(): pl.pallas_call(reduce_kernel, name='reduce_fast', out_shape=jax.ShapeDtyp...  154 us
    all_gather x2, waiting for transfers between devices, gather_all(): return lax.all_gather(pack, ('width', 'tok'), axis=0, tiled=False)  123 us
    pallas_call x1, Pallas kernels, run_middle(): pl.pallas_call(middle, name='middle', cost_estimate=pl.CostEstimate(flops...  30.8 us
    pallas_call x1, Pallas kernels, run_bwd(): pl.pallas_call(attn_bwd, name='attn_bwd', cost_estimate=pl.CostEstimate(f...  28.5 us
    pallas_call x1, Pallas kernels, run_fwd(): pl.pallas_call(attn_fwd, name='attn_fwd', cost_estimate=pl.CostEstimate(f...  16.4 us
    slice x3, local copies, waits for them, and re-layouts, rows(): source[:, :, lower:lower + count].reshape(groups, count * shards, width)  14.2 us
    select_n x2, other arithmetic, only(): jnp.where(mine.reshape((groups,) + (1,) * (term.ndim - 1)), term, jnp.zer...  9.7 us
  transfers between devices with their start and end apart: 3, of which 3 were waited for; matrix products, arithmetic and copies ran while one was open for 5% of the time, Pallas kernels for 46%

profile of v3, /device:TPU:0, one launch (start us, length us, event | category | flops | bytes accessed | tf_op | source)
XLA Modules:
  0.0 429.7 jit_solution(16035895888989457906)
XLA Ops:
  7.2 6.1 %concatenate.29 = bf16[288]{0:T(512)(128)(2,1)S(1)} concatenate(bf16[24]{0:T(256)(128)(2,1)} %param.26, bf16[24]{0:T(256)(128)(2,1)} %param.27, bf16[24]{0:T(256)(128)(2,1)} %param.28, bf16[96]{0:T(256)(128)(2,1)} %param.29, bf16[24]{0:T(256)(128)(2,1)} %param.30, bf16[24]{0:T(256)(128)(2,1)} %param.31, bf16[24]{0:T(256)(128)(2,1)} %param.32, bf16[24]{0:T(256)(128)(2,1)} %param.33, ...), dimensions={0} | concatenate | bytes 1152 | tf_op jit(solution)/shard_map/concatenate | solution.py:602
  13.4 1.5 fusion.5
  14.9 1.7 pad_maximum_fusion
  16.7 0.7 copy.54
  17.5 0.1 reduce
  17.9 0.2 convert_reduce_fusion.2
  18.1 0.6 pad_add_fusion.bounds
  18.7 59.9 %all-gather.5.cloned.1.call-done = bf16[2560,768]{1,0:T(8,128)(2,1)} async-done(((bf16[80,768]{1,0:T(8,128)(2,1)}), bf16[2560,768]{1,0:T(8,128)(2,1)}) %all-gather.5.cloned.1.call-update) | async-done | bytes 3932176 | tf_op jit(solution)/shard_map/all_gather | solution.py:583
  78.6 1.0 slice.236
  79.9 0.1 stack_reshape_reshape.24
  80.1 0.1 stack_reshape_reshape.25
  80.3 0.1 stack_reshape_reshape.26
  80.4 0.1 stack_reshape_reshape.27
  80.5 0.1 stack_reshape_reshape.28
  80.6 0.1 stack_reshape_reshape.29
  80.7 0.1 stack_reshape_reshape.30
  80.8 0.1 stack_reshape_reshape.31
  80.9 0.6 convert_element_type.53.vec_ref
  81.6 0.6 fusion.13.bias_ref
  82.3 0.7 pad_convert_fusion.eb_ref
  82.9 3.8 fusion.15
  86.7 1.0 broadcast_in_dim.80.segc_ref
  87.7 0.6 lt.6.segr_ref
  88.3 16.4 %attn_fwd.1 = (bf16[4,1024,192]{2,1,0:T(8,128)(2,1)}, f32[4,1024,128]{2,1,0:T(8,128)}) custom-call(s32[1]{0:T(128)} %bitcast.scal, s32[2,8]{1,0:T(2,128)} %pad_add_fusion.bounds, bf16[1024,768]{1,0:T(8,128)(2,1)} %x_ref.5, bf16[4,192,768]{2,1,0:T(8,128)(2,1)} %bitcast.85, bf16[4,192,768]{2,1,0:T(8,128)(2,1)} %bitcast.83, bf16[4,192,768]{2,1,0:T(8,128)(2,1)} %bitcast.81, ...), custom_call_target="tpu_custom_call" | custom-call | flops 40000000000 | bytes 30000000 | tf_op jit(solution)/shard_map/attn_fwd/pallas_call | solution.py:362
  104.8 62.9 %all-gather.7.cloned.1.call-done = bf16[6912,768]{1,0:T(8,128)(2,1)} async-done(((bf16[216,768]{1,0:T(8,128)(2,1)}), bf16[6912,768]{1,0:T(8,128)(2,1)}) %all-gather.7.cloned.1.call-update) | async-done | bytes 10616848 | tf_op jit(solution)/shard_map/all_gather | solution.py:583
  167.7 8.0 %fusion.14 = (bf16[4,8,96,768]{3,2,1,0:T(8,128)(2,1)}, bf16[4,8,96,768]{3,2,1,0:T(8,128)(2,1)}) fusion(bf16[4,8,216,768]{3,2,1,0:T(8,128)(2,1)} %bitcast.72), kind=kLoop, calls=%fused_computation.67 | loop fusion | bytes 18874368 | tf_op jit(solution)/shard_map/slice | solution.py:611
  175.7 2.4 slice.239
  178.0 30.8 %middle.1 = (bf16[1024,768]{1,0:T(8,128)(2,1)}, f32[1024,768]{1,0:T(8,128)}, bf16[4,1024,192]{2,1,0:T(8,128)(2,1)}, bf16[4,192,1024]{2,1,0:T(8,128)(2,1)}, bf16[...) custom-call(s32[1]{0:T(128)} %bitcast.scal, ...), custom_call_target="tpu_custom_call" | custom-call | flops 49999998976 | bytes 30000000 | tf_op jit(solution)/shard_map/middle/pallas_call | solution.py:325
  208.9 0.7 convert.35
  210.3 0.9 slice_reduce_fusion
  211.4 0.1 concatenate.33
  211.6 7.3 %maximum_select_fusion = bf16[4,8,216,768]{3,2,1,0:T(8,128)(2,1)S(1)} fusion(bf16[4,8,96,768]{3,2,1,0:T(8,128)(2,1)} %bitcast.75, bf16[4,8,96,768]{3,2,1,0:T(8,128)(2,1)} %bitcast.74, bf16[4,8,24,768]{3,2,1,0:T(8,128)(2,1)} %bitcast.80, pred[4]{0:T(512)(128)(4,1)S(1)} %iota_compare_fusion.6), kind=kLoop, calls=%fused_computation.3 | loop fusion | flops 37158912 | bytes 21233668 | tf_op jit(solution)/shard_map/jit(_where)/select_n | solution.py:648
  218.9 5.4 %fusion.1 = bf16[4,8,224,768]{3,2,1,0:T(8,128)(2,1)} fusion(bf16[4,8,1,768]{3,2,1,0:T(2,128)(2,1)S(1)} %copy.63, bf16[4,8,216,768]{3,2,1,0:T(8,128)(2,1)S(1)} %maximum_select_fusion), kind=kLoop, calls=%fused_computation.2 | loop fusion | flops 33030144 | bytes 21676032 | tf_op jit(solution)/shard_map/concatenate | solution.py:659
  224.4 0.2 copy.59
  224.7 0.7 pad.45.bcol_ref
  225.4 28.5 %attn_bwd.1 = (f32[1024,768]{1,0:T(8,128)}, bf16[4,192,768]{2,1,0:T(8,128)(2,1)}, bf16[4,192,768]{2,1,0:T(8,128)(2,1)}, bf16[4,192,768]{2,1,0:T(8,128)(2,1)}, f32[4,16,192]{2,1,0:T(8,128)}) custom-call(s32[1]{0:T(128)} %bitcast.scal, s32[2,8]{1,0:T(2,128)} %pad_add_fusion.bounds, bf16[1024,768]{1,0:T(8,128)(2,1)} %x_ref.5, bf16[4,192,768]{2,1,0:T(8,128)(2,1)} %bitcast.86, ...), custom_call_target="tpu_custom_call" | custom-call | flops 89999998976 | bytes 30000000 | tf_op jit(solution)/shard_map/attn_bwd/pallas_call | solution.py:386
  253.9 0.8 slice_reduce_fusion.2
  255.1 2.4 maximum_select_fusion.1
  257.5 0.3 fusion.3
  257.9 153.9 %reduce_fast.1 = f32[80,768]{1,0:T(8,128)S(1)} custom-call(bf16[4,4,2,80,768]{4,3,2,1,0:T(8,128)(2,1)S(1)} %bitcast.70), custom_call_target="tpu_custom_call" | custom-call | tf_op jit(solution)/shard_map/reduce_fast/pallas_call | solution.py:561
  411.8 0.6 slice_bitcast_fusion.10
  412.4 0.7 fusion.16
  413.1 6.4 %reduce-scatter.2.cloned.1.call-done = bf16[1,224,768]{2,1,0:T(8,128)(2,1)} async-done(((bf16[32,224,768]{2,1,0:T(8,128)(2,1)}), bf16[1,224,768]{2,1,0:T(8,128)(2,1)}) %reduce-scatter.2.cloned.1.call-update) | async-done | bytes 344080 | tf_op jit(solution)/shard_map/reduce_scatter | solution.py:588
  419.5 1.1 convert_bitcast_fusion
  420.6 0.8 slice_bitcast_fusion
  421.4 0.6 slice_bitcast_fusion.2
  422.1 0.6 slice_bitcast_fusion.3
  422.7 0.5 slice_bitcast_fusion.8
  (40 shorter events, 2.5 us)
Async XLA Ops:
  7.2 71.5 %all-gather.5.cloned.1.call-start = ((), (), s32[]{:S(2)}) async-start(), calls=%async_computation.2 | async-start | bytes 4055040 | tf_op jit(solution)/shard_map/all_gather | solution.py:583
  14.8 152.8 %all-gather.7.cloned.1.call-start = ((), (), s32[]{:S(2)}) async-start(), calls=%async_computation.3 | async-start | bytes 10948608 | tf_op jit(solution)/shard_map/all_gather | solution.py:583
  16.6 402.9 %reduce-scatter.2.cloned.1.call-start = ((), (), s32[]{:S(2)}) async-start(), calls=%async_computation.1 | async-start | bytes 11354112 | tf_op jit(solution)/shard_map/reduce_scatter | solution.py:588
Sparse Core Ops, SparseCore 0:
  15.0 63.6 all-gather.4
  82.1 85.5 all-gather.6
  224.4 195.0 reduce-scatter.1

commit v4 on v3

--- a/solution.py
+++ b/solution.py
@@ -353,8 +353,15 @@
     return at_quarter, whole
 
 
-def run_fwd(scal, bounds, x, wq, wk, wv, bias, segc, segr):
-    groups, feat, width = wq.shape
+def weight_specs(groups, feat, width):
+    def one(kind):
+        return pl.BlockSpec((1, feat, width), lambda q, s, b: (kind * groups + jnp.minimum(q, s[0]), 0, 0))
+
+    return [one(kind) for kind in range(3)]
+
+
+def run_fwd(scal, bounds, x, wqkv, bias, segc, segr):
+    groups, feat, width = wqkv.shape[0] // 3, wqkv.shape[1], wqkv.shape[2]
     tokens = x.shape[0]
     heads = feat // HEAD_DIM
     at_quarter, whole = attn_specs(tokens, width, feat)
@@ -366,7 +373,7 @@
         out_shape=(sds((groups, tokens, feat), BF), sds((groups, tokens, 128), F32)),
         grid_spec=pltpu.PrefetchScalarGridSpec(
             num_scalar_prefetch=2, grid=(groups,),
-            in_specs=[whole(tokens, width)] + [at_quarter(feat, width)] * 3
+            in_specs=[whole(tokens, width)] + weight_specs(groups, feat, width)
             + [at_quarter(8, feat), whole(tokens, 128), whole(8, tokens)],
             out_specs=(at_quarter(tokens, feat), at_quarter(tokens, 128)),
             scratch_shapes=[
@@ -374,11 +381,11 @@
                 pltpu.VMEM((heads, tokens, feat), BF), pltpu.VMEM((heads, BR, tokens), F32),
                 pltpu.VMEM((heads, BR, BC), F32)]),
         compiler_params=pltpu.CompilerParams(vmem_limit_bytes=60 << 20),
-    )(scal, bounds, x, wq, wk, wv, bias, segc, segr)
-
-
-def run_bwd(scal, bounds, x, wq, wk, wv, bias, bcol, segc, segr, ctx, lse, do, dot, s1g):
-    groups, feat, width = wq.shape
+    )(scal, bounds, x, wqkv, wqkv, wqkv, bias, segc, segr)
+
+
+def run_bwd(scal, bounds, x, wqkv, bias, bcol, segc, segr, ctx, lse, do, dot, s1g):
+    groups, feat, width = wqkv.shape[0] // 3, wqkv.shape[1], wqkv.shape[2]
     tokens = x.shape[0]
     heads = feat // HEAD_DIM
     at_quarter, whole = attn_specs(tokens, width, feat)
@@ -391,7 +398,7 @@
         + (sds((groups, 16, feat), F32),),
         grid_spec=pltpu.PrefetchScalarGridSpec(
             num_scalar_prefetch=2, grid=(groups,),
-            in_specs=[whole(tokens, width)] + [at_quarter(feat, width)] * 3
+            in_specs=[whole(tokens, width)] + weight_specs(groups, feat, width)
             + [at_quarter(8, feat), at_quarter(feat, 128), whole(tokens, 128), whole(8, tokens),
                at_quarter(tokens, feat), at_quarter(tokens, 128), at_quarter(tokens, feat),
                at_quarter(feat, tokens), whole(tokens, width)],
@@ -403,7 +410,7 @@
                 pltpu.VMEM((feat, tokens), BF), pltpu.VMEM((feat, tokens), BF),
                 pltpu.VMEM((feat, tokens), F32), pltpu.VMEM((feat, tokens), F32)]),
         compiler_params=pltpu.CompilerParams(vmem_limit_bytes=60 << 20),
-    )(scal, bounds, x, wq, wk, wv, bias, bcol, segc, segr, ctx, lse, do, dot, s1g)
+    )(scal, bounds, x, wqkv, wqkv, wqkv, bias, bcol, segc, segr, ctx, lse, do, dot, s1g)
 
 
 PART = 16
@@ -575,6 +582,135 @@
     )(terms.reshape((groups, 4, 2, count, width)))
 
 
+def gather_kernel(own_ref, line_ref, all_ref, lines_ref, own_sem, recv_sem, z_sem, y_sem, core_sem, x_sem):
+    w = lax.axis_index("width")
+    t = lax.axis_index("tok")
+    y = lax.rem(t, 2)
+    z = lax.div(t, 2)
+    mine = (pltpu.make_async_copy(own_ref, all_ref.at[:, w, t], own_sem.at[0]),
+            pltpu.make_async_copy(line_ref, lines_ref.at[w, t], own_sem.at[1]))
+    for copy in mine:
+        copy.start()
+    greet(w, t)
+    for copy in mine:
+        copy.wait()
+
+    def both(q, s, sems, **where):
+        return (peer_copy(all_ref.at[:, q, s], all_ref.at[:, q, s], sems.at[0], recv_sem.at[0, q, s], **where),
+                peer_copy(lines_ref.at[q, s], lines_ref.at[q, s], sems.at[1], recv_sem.at[1, q, s], **where))
+
+    def along(k):
+        return both(w, t, z_sem.at[k - 1], width=w, tok=lax.rem(t + 2 * k, 8))
+
+    def beside(zz):
+        return both(w, 2 * zz + y, y_sem.at[zz], width=w, tok=t ^ 1)
+
+    def near(q, s):
+        return both(q, s, core_sem.at[q, s], width=w ^ 1, tok=t)
+
+    def across(s):
+        return both(w, s, x_sem.at[s], width=w ^ 2, tok=t)
+
+    def start(pair):
+        for copy in pair:
+            copy.start()
+
+    def arrived(q, s):
+        for copy in near(q, s):
+            copy.wait_recv()
+
+    def sent(pair):
+        for copy in pair:
+            copy.wait_send()
+
+    def outward(s):
+        @pl.when(w <= 1)
+        def _():
+            start(across(s))
+
+        @pl.when((w == 0) | (w == 2))
+        def _():
+            start(near(w, s))
+
+    for k in range(1, 4):
+        start(along(k))
+    start(beside(z))
+    outward(t)
+    for k in range(1, 4):
+        zz = lax.rem(z + k, 4)
+        arrived(w, 2 * zz + y)
+        start(beside(zz))
+        outward(2 * zz + y)
+
+    @pl.loop(0, 4)
+    def _(k):
+        s = 2 * lax.rem(z + k, 4) + (1 - y)
+        arrived(w, s)
+        outward(s)
+
+    @pl.loop(0, 8)
+    def _(k):
+        zz = lax.rem(z + lax.div(k, 2), 4)
+        s = 2 * zz + lax.rem(y + k, 2)
+
+        @pl.when(w >= 2)
+        def _():
+            arrived(w - 2, s)
+            start(near(w - 2, s))
+
+    @pl.loop(0, 8)
+    def _(s):
+        @pl.when((w == 1) | (w == 3))
+        def _():
+            arrived(w - 1, s)
+
+        @pl.when(w == 3)
+        def _():
+            arrived(0, s)
+
+        @pl.when(w == 2)
+        def _():
+            arrived(1, s)
+
+    for k in range(1, 4):
+        sent(along(k))
+
+    @pl.loop(0, 4)
+    def _(zz):
+        sent(beside(zz))
+
+    @pl.loop(0, 8)
+    def _(s):
+        @pl.when(w <= 1)
+        def _():
+            sent(across(s))
+
+        @pl.when((w == 0) | (w == 2))
+        def _():
+            sent(near(w, s))
+
+        @pl.when(w >= 2)
+        def _():
+            sent(near(w - 2, s))
+
+
+def gather_fast(own, line):
+    kinds, owned, width = own.shape
+    hbm = pl.BlockSpec(memory_space=pl.ANY)
+    dma = pltpu.SemaphoreType.DMA
+    return pl.pallas_call(
+        gather_kernel,
+        name="gather_fast",
+        out_shape=(jax.ShapeDtypeStruct((kinds, 4, 8, owned, width), BF),
+                   jax.ShapeDtypeStruct((4, 8) + line.shape, BF)),
+        in_specs=[hbm, hbm],
+        out_specs=(hbm, hbm),
+        scratch_shapes=[dma((2,)), dma((2, 4, 8)), dma((3, 2)), dma((4, 2)), dma((4, 8, 2)), dma((8, 2))],
+        compiler_params=pltpu.CompilerParams(collective_id=2, has_side_effects=True),
+        cost_estimate=pl.CostEstimate(flops=int(30e9), bytes_accessed=int(30e6), transcendentals=0),
+    )(own, line)
+
+
 def columns(array):
     return jnp.broadcast_to(array[:, :, None], array.shape + (128,)).astype(BF)
 
@@ -599,29 +735,40 @@
     feat = owned * shards
     units = owned_ff * shards
 
-    small = jnp.concatenate(biases)
-    small = jnp.pad(small, (0, width - small.shape[0]))[None, :]
-    small = jnp.pad(small, ((0, 7), (0, 0)))
-    got = gather_all(jnp.concatenate(weights[:3] + (small,), axis=0))
-    got = got.reshape((groups, shards) + got.shape[1:])
-    late = gather_all(jnp.concatenate(weights[3:], axis=0))
+    def flat(*vectors):
+        line = jnp.concatenate(vectors)
+        return jnp.pad(line, (0, width - line.shape[0]))[None, :]
+
+    late = gather_all(jnp.concatenate(weights[3:] + (flat(*biases[2:]),), axis=0))
     late = late.reshape((groups, shards) + late.shape[1:])
-
-    def rows(source, lower, count):
-        return source[:, :, lower : lower + count].reshape(groups, count * shards, width)
-
-    wq, wk, wv = (rows(got, n * owned, owned) for n in range(3))
-    wo = rows(late, 0, owned)
-    we, ws = rows(late, owned, owned_ff), rows(late, owned + owned_ff, owned_ff)
-    row = got[:, :, 3 * owned]
-    sizes = [b.shape[0] for b in biases]
-    starts = [sum(sizes[:n]) for n in range(9)]
+    soon = jnp.stack(weights[:3])
+    line = jnp.concatenate(biases[:2])
+    if groups == 4 and shards == 8 and owned % 8 == 0:
+        line = jnp.pad(line[None, :], ((0, 7), (0, 128 - line.shape[0])))
+        wqkv, line = gather_fast(soon, line)
+        line = line[:, :, 0, : 2 * owned]
+    else:
+        got = gather_all(jnp.concatenate([soon.reshape(3 * owned, width), flat(line)], axis=0))
+        wqkv = jnp.swapaxes(got[:, : 3 * owned].reshape(groups * shards, 3, owned, width), 0, 1)
+        line = got[:, 3 * owned, : 2 * owned].reshape(groups, shards, 2 * owned)
+    wqkv = wqkv.reshape(3 * groups, feat, width)
+
+    def rows(lower, count):
+        return late[:, :, lower : lower + count].reshape(groups, count * shards, width)
+
+    wo = rows(0, owned)
+    we, ws = rows(owned, owned_ff), rows(owned + owned_ff, owned_ff)
+    row = late[:, :, owned + 2 * owned_ff]
+    sizes = [b.shape[0] for b in biases[2:]]
+    starts = [sum(sizes[:n]) for n in range(7)]
     vecs = [row[:, :, a : a + n].reshape(groups, n * shards) for a, n in zip(starts, sizes)]
-    eb = jnp.pad(vecs[3][:, None, :].astype(F32), ((0, 0), (0, 7), (0, 0)))
-    order = [vecs[0], vecs[1], vecs[2], vecs[4]] + vecs[5:]
-    vec = jnp.stack([v.reshape(-1) for v in order]).astype(F32)
-    bias = jnp.pad(jnp.stack([vecs[0], vecs[1]], axis=1).astype(F32), ((0, 0), (0, 6), (0, 0)))
-    bcol = jnp.pad(jnp.stack([vecs[0], vecs[1]], axis=2), ((0, 0), (0, 0), (0, 126)))
+    qb = line[:, :, :owned].reshape(groups, feat)
+    vb = line[:, :, owned:].reshape(groups, feat)
+    eb = jnp.pad(vecs[1][:, None, :].astype(F32), ((0, 0), (0, 7), (0, 0)))
+    vec = jnp.stack([v.reshape(-1) for v in [vecs[0], vecs[2]] + vecs[3:]]).astype(F32)
+    vec = jnp.pad(vec, ((2, 0), (0, 0)))
+    bias = jnp.pad(jnp.stack([qb, vb], axis=1).astype(F32), ((0, 0), (0, 6), (0, 0)))
+    bcol = jnp.pad(jnp.stack([qb, vb], axis=2), ((0, 0), (0, 0), (0, 126)))
 
     ends = jnp.cumsum(seq_lengths[0])
     positions = jnp.arange(tokens, dtype=jnp.int32)
@@ -633,7 +780,7 @@
     segr = jnp.broadcast_to(segment[None, :], (8, tokens))
     scal = level[None].astype(jnp.int32)
 
-    ctx, lse = run_fwd(scal, bounds, tokens_in, wq, wk, wv, bias, segc, segr)
+    ctx, lse = run_fwd(scal, bounds, tokens_in, wqkv, bias, segc, segr)
     result, s1g, do, dot, dwo, vg, ebg, de, ds = run_middle(
         scal, tokens_in, ctx, wo, we, ws, vec, eb, out_grad[0])
     mine = jnp.arange(groups) <= level
@@ -660,7 +807,7 @@
     first, s1g = lax.optimization_barrier((first, s1g))
     early = scatter_all(first)
     input_grad, dwq, dwk, dwv, db = run_bwd(
-        scal, bounds, tokens_in, wq, wk, wv, bias, bcol, segc, segr, ctx, lse, do, dot, s1g)
+        scal, bounds, tokens_in, wqkv, bias, bcol, segc, segr, ctx, lse, do, dot, s1g)
 
     line = lined(only(split(db[:, 0])), only(split(db[:, 8])))
     second = jnp.concatenate([packed(dwq, dwk, dwv), line], axis=2)

time: 431 us -> 401 us (0.930)
  waiting for transfers between devices: 129 us -> 48 us
  Pallas kernels: 230 us -> 284 us
    all_gather x2 -> x1, waiting for transfers between devices: 123 us -> 38.4 us  [gather_all(): return lax.all_gather(pack, ('width', 'tok'), axis=0, tiled=False)]
    pallas_call x0 -> x1, Pallas kernels: none -> 38.5 us  [gather_fast(): pl.pallas_call(gather_kernel, name='gather_fast', out_shape=(jax.ShapeDty...]
    pallas_call x1, Pallas kernels: 154 us -> 167 us  [reduce_fast(): pl.pallas_call(reduce_kernel, name='reduce_fast', out_shape=jax.ShapeDtyp...]
    slice x4 -> x5, local copies, waits for them, and re-layouts: 15.2 us -> 12.3 us  [the longest x2 10.3 us: rows(): late[:, :, lower:lower + count].reshape(groups, count * shards, width)]
  transfers between devices with their start and end apart: 3 -> 2, of which waited for: 3 -> 2; matrix products, arithmetic and copies ran while one was open for 5% -> 4% of each run, Pallas kernels for 46% -> 63%
where the time goes in v4:
time: 401 us; the launch traced here: 400 us
  Pallas kernels  284 us (71%)
  waiting for transfers between devices  48 us (12%)
  local copies, waits for them, and re-layouts  29.1 us (7%)
  other arithmetic  24.4 us (6%)
  between operations  14.3 us (4%)
    pallas_call x1, Pallas kernels, reduce_fast(): pl.pallas_call(reduce_kernel, name='reduce_fast', out_shape=jax.ShapeDtyp...  167 us
    pallas_call x1, Pallas kernels, gather_fast(): pl.pallas_call(gather_kernel, name='gather_fast', out_shape=(jax.ShapeDty...  38.5 us
    all_gather x1, waiting for transfers between devices, gather_all(): return lax.all_gather(pack, ('width', 'tok'), axis=0, tiled=False)  38.4 us
    pallas_call x1, Pallas kernels, run_middle(): pl.pallas_call(middle, name='middle', cost_estimate=pl.CostEstimate(flops...  30.8 us
    pallas_call x1, Pallas kernels, run_bwd(): pl.pallas_call(attn_bwd, name='attn_bwd', cost_estimate=pl.CostEstimate(f...  30 us
    pallas_call x1, Pallas kernels, run_fwd(): pl.pallas_call(attn_fwd, name='attn_fwd', cost_estimate=pl.CostEstimate(f...  17.3 us
    slice x2, local copies, waits for them, and re-layouts, rows(): late[:, :, lower:lower + count].reshape(groups, count * shards, width)  10.3 us
    select_n x2, other arithmetic, only(): jnp.where(mine.reshape((groups,) + (1,) * (term.ndim - 1)), term, jnp.zer...  9.7 us
  transfers between devices with their start and end apart: 2, of which 2 were waited for; matrix products, arithmetic and copies ran while one was open for 4% of the time, Pallas kernels for 63%

profile of v4, /device:TPU:0, one launch (start us, length us, event | category | flops | bytes accessed | tf_op | source)
XLA Modules:
  0.0 399.7 jit_solution(8331036786083540964)
XLA Ops:
  7.2 4.8 %concatenate.30 = bf16[240]{0:T(256)(128)(2,1)S(1)} concatenate(bf16[24]{0:T(256)(128)(2,1)} %param.28, bf16[96]{0:T(256)(128)(2,1)} %param.29, bf16[24]{0:T(256)(128)(2,1)} %param.30, bf16[24]{0:T(256)(128)(2,1)} %param.31, bf16[24]{0:T(256)(128)(2,1)} %param.32, bf16[24]{0:T(256)(128)(2,1)} %param.33, bf16[24]{0:T(256)(128)(2,1)} %param.34), dimensions={0} | concatenate | bytes 960 | tf_op jit(solution)/shard_map/concatenate | solution.py:739
  12.0 1.7 maximum_bitcast_fusion
  13.8 0.7 copy.54
  14.6 0.1 reduce
  15.0 0.8 maximum_bitcast_fusion.1
  15.8 0.6 pad.45.line_ref
  16.3 1.5 pad_maximum_fusion.own_ref
  17.8 38.5 %gather_fast.1 = (bf16[3,4,8,24,768]{4,3,2,1,0:T(8,128)(2,1)}, bf16[4,8,8,128]{3,2,1,0:T(8,128)(2,1)}) custom-call(bf16[3,24,768]{2,1,0:T(8,128)(2,1)} %pad_maximum_fusion.own_ref, bf16[8,128]{1,0:T(8,128)(2,1)} %pad.45.line_ref), custom_call_target="tpu_custom_call" | custom-call | flops 30000001024 | bytes 30000000 | tf_op jit(solution)/shard_map/gather_fast/pallas_call | solution.py:701
  56.4 0.9 slice.175
  57.5 0.2 convert_reduce_fusion.2
  57.7 0.6 pad_add_fusion.bounds
  58.3 0.6 fusion.11.bias_ref
  58.9 1.0 broadcast_in_dim.83.segc_ref
  59.9 0.6 lt.6.segr_ref
  60.6 17.3 %attn_fwd.1 = (bf16[4,1024,192]{2,1,0:T(8,128)(2,1)}, f32[4,1024,128]{2,1,0:T(8,128)}) custom-call(s32[1]{0:T(128)} %bitcast.scal, s32[2,8]{1,0:T(2,128)} %pad_add_fusion.bounds, bf16[1024,768]{1,0:T(8,128)(2,1)} %x_ref.5, bf16[12,192,768]{2,1,0:T(8,128)(2,1)} %bitcast.99, bf16[12,192,768]{2,1,0:T(8,128)(2,1)} %bitcast.100, bf16[12,192,768]{2,1,0:T(8,128)(2,1)} %bitcast.101, ...), custom_call_target="tpu_custom_call" | custom-call | flops 40000000000 | bytes 30000000 | tf_op jit(solution)/shard_map/attn_fwd/pallas_call | solution.py:369
  77.9 38.4 %all-gather.4.cloned.1.call-done = bf16[32,217,768]{2,1,0:T(8,128)(2,1)} async-done(((bf16[1,217,768]{2,1,0:T(8,128)(2,1)}), bf16[32,217,768]{2,1,0:T(8,128)(2,1)}) %all-gather.4.cloned.1.call-update) | async-done | bytes 10666000 | tf_op jit(solution)/shard_map/all_gather | solution.py:719
  116.3 1.0 slice.230
  117.4 8.0 %fusion.12 = (bf16[4,8,96,768]{3,2,1,0:T(8,128)(2,1)}, bf16[4,8,96,768]{3,2,1,0:T(8,128)(2,1)}) fusion(bf16[4,8,217,768]{3,2,1,0:T(8,128)(2,1)} %bitcast.80), kind=kLoop, calls=%fused_computation.68 | loop fusion | bytes 18874368 | tf_op jit(solution)/shard_map/slice | solution.py:757
  125.5 2.4 slice.227
  128.0 0.1 stack_reshape_reshape.19
  128.1 0.1 stack_reshape_reshape.20
  128.2 0.1 stack_reshape_reshape.21
  128.3 0.1 stack_reshape_reshape.22
  128.4 0.1 stack_reshape_reshape.23
  128.5 0.6 pad_convert_fusion.1.vec_ref
  129.2 0.7 pad_convert_fusion.eb_ref
  129.9 30.8 %middle.1 = (bf16[1024,768]{1,0:T(8,128)(2,1)}, f32[1024,768]{1,0:T(8,128)}, bf16[4,1024,192]{2,1,0:T(8,128)(2,1)}, bf16[4,192,1024]{2,1,0:T(8,128)(2,1)}, bf16[...) custom-call(s32[1]{0:T(128)} %bitcast.scal, ...), custom_call_target="tpu_custom_call" | custom-call | flops 49999998976 | bytes 30000000 | tf_op jit(solution)/shard_map/middle/pallas_call | solution.py:325
  160.7 0.7 convert.37
  161.6 0.1 reshape_squeeze.35
  162.1 0.9 slice_reduce_fusion
  163.2 0.1 concatenate.33
  163.4 7.3 %maximum_select_fusion = bf16[4,8,216,768]{3,2,1,0:T(8,128)(2,1)S(1)} fusion(bf16[4,8,96,768]{3,2,1,0:T(8,128)(2,1)} %bitcast.83, bf16[4,8,96,768]{3,2,1,0:T(8,128)(2,1)} %bitcast.82, bf16[4,8,24,768]{3,2,1,0:T(8,128)(2,1)} %bitcast.86, pred[4]{0:T(512)(128)(4,1)S(1)} %iota_compare_fusion.5), kind=kLoop, calls=%fused_computation.3 | loop fusion | flops 37158912 | bytes 21233668 | tf_op jit(solution)/shard_map/jit(_where)/select_n | solution.py:795
  170.7 5.4 %fusion.1 = bf16[4,8,224,768]{3,2,1,0:T(8,128)(2,1)} fusion(bf16[4,8,1,768]{3,2,1,0:T(2,128)(2,1)S(1)} %copy.64, bf16[4,8,216,768]{3,2,1,0:T(8,128)(2,1)S(1)} %maximum_select_fusion), kind=kLoop, calls=%fused_computation.2 | loop fusion | flops 33030144 | bytes 21676032 | tf_op jit(solution)/shard_map/concatenate | solution.py:806
  176.3 0.2 copy.59
  176.5 0.7 pad.53.bcol_ref
  177.2 30.0 %attn_bwd.1 = (f32[1024,768]{1,0:T(8,128)}, bf16[4,192,768]{2,1,0:T(8,128)(2,1)}, bf16[4,192,768]{2,1,0:T(8,128)(2,1)}, bf16[4,192,768]{2,1,0:T(8,128)(2,1)}, f32[4,16,192]{2,1,0:T(8,128)}) custom-call(s32[1]{0:T(128)} %bitcast.scal, s32[2,8]{1,0:T(2,128)} %pad_add_fusion.bounds, bf16[1024,768]{1,0:T(8,128)(2,1)} %x_ref.5, bf16[12,192,768]{2,1,0:T(8,128)(2,1)} %bitcast.102, ...), custom_call_target="tpu_custom_call" | custom-call | flops 89999998976 | bytes 30000000 | tf_op jit(solution)/shard_map/attn_bwd/pallas_call | solution.py:393
  207.2 0.8 slice_reduce_fusion.2
  208.5 2.4 maximum_select_fusion.1
  210.9 0.3 fusion.3
  211.3 167.1 %reduce_fast.1 = f32[80,768]{1,0:T(8,128)S(1)} custom-call(bf16[4,4,2,80,768]{4,3,2,1,0:T(8,128)(2,1)S(1)} %bitcast.77), custom_call_target="tpu_custom_call" | custom-call | tf_op jit(solution)/shard_map/reduce_fast/pallas_call | solution.py:568
  378.4 0.6 slice_bitcast_fusion.10
  379.0 0.7 fusion.13
  379.7 9.6 %reduce-scatter.2.cloned.1.call-done = bf16[1,224,768]{2,1,0:T(8,128)(2,1)} async-done(((bf16[32,224,768]{2,1,0:T(8,128)(2,1)}), bf16[1,224,768]{2,1,0:T(8,128)(2,1)}) %reduce-scatter.2.cloned.1.call-update) | async-done | bytes 344080 | tf_op jit(solution)/shard_map/reduce_scatter | solution.py:724
  389.2 1.1 convert_bitcast_fusion
  390.3 0.8 slice_bitcast_fusion
  391.2 0.6 slice_bitcast_fusion.2
  391.8 0.6 slice_bitcast_fusion.3
  392.4 0.5 slice_bitcast_fusion.8
  (40 shorter events, 2.5 us)
Async XLA Ops:
  7.2 109.1 %all-gather.4.cloned.1.call-start = ((), (), s32[]{:S(2)}) async-start(), calls=%async_computation.2 | async-start | bytes 11354112 | tf_op jit(solution)/shard_map/all_gather | solution.py:719
  13.8 375.5 %reduce-scatter.2.cloned.1.call-start = ((), (), s32[]{:S(2)}) async-start(), calls=%async_computation.1 | async-start | bytes 11354112 | tf_op jit(solution)/shard_map/reduce_scatter | solution.py:724
Sparse Core Ops, SparseCore 0:
  13.9 102.3 all-gather.3
  176.2 212.9 reduce-scatter.1

commit v5 on v4

--- a/solution.py
+++ b/solution.py
@@ -39,69 +39,67 @@
     return lax.broadcasted_iota(jnp.int32, shape, axis) // HEAD_DIM
 
 
-def attn_fwd(scal, bounds, x_ref, wq_ref, wk_ref, wv_ref, bias_ref, segc_ref, segr_ref,
+def attn_fwd(bounds, x_ref, wq_ref, wk_ref, wv_ref, bias_ref, segc_ref, segr_ref,
              ctx_ref, lse_ref, q_s, kt_s, v_s, s_s, m_s):
     heads = q_s.shape[1] // HEAD_DIM
     tokens = x_ref.shape[0]
 
-    @pl.when(pl.program_id(0) <= scal[0])
-    def _():
-        wq, wk, wv = wq_ref[0], wk_ref[0], wv_ref[0]
-
-        @pl.loop(0, tokens // RT)
-        def _(i):
-            r = rows_at(i, RT)
-            xb = x_ref[r, :]
-            q = (nt(xb, wq) + bias_ref[0, 0:1, :]).astype(BF).astype(F32)
-            q_s[r, :] = (q * 0.125).astype(BF)
-            v = (nt(xb, wv) + bias_ref[0, 1:2, :]).astype(BF)
-            kt = nt(wk, xb).astype(BF)
+    wq, wk, wv = wq_ref[0], wk_ref[0], wv_ref[0]
+
+    @pl.loop(0, tokens // RT)
+    def _(i):
+        r = rows_at(i, RT)
+        xb = x_ref[r, :]
+        q = (nt(xb, wq) + bias_ref[0, 0:1, :]).astype(BF).astype(F32)
+        q_s[r, :] = (q * 0.125).astype(BF)
+        v = (nt(xb, wv) + bias_ref[0, 1:2, :]).astype(BF)
+        kt = nt(wk, xb).astype(BF)
+        for h in range(heads):
+            v_s[h, r, :] = jnp.where(head_of(v.shape, 1) == h, v, jnp.zeros_like(v))
+            kt_s[h, :, r] = jnp.where(head_of(kt.shape, 0) == h, kt, jnp.zeros_like(kt))
+
+    @pl.loop(0, tokens // BR)
+    def _(i):
+        r = rows_at(i, BR)
+        qb = q_s[r, :]
+        seg = segc_ref[r, :]
+        seg = jnp.concatenate([seg] * (BC // 128), axis=1)
+        lo, hi = bounds[0, i], bounds[1, i]
+        m_s[...] = jnp.full_like(m_s, MASKED)
+
+        @pl.loop(lo, hi)
+        def _(j):
+            c = rows_at(j, BC)
+            keep = seg == segr_ref[0:1, c]
             for h in range(heads):
-                v_s[h, r, :] = jnp.where(head_of(v.shape, 1) == h, v, jnp.zeros_like(v))
-                kt_s[h, :, r] = jnp.where(head_of(kt.shape, 0) == h, kt, jnp.zeros_like(kt))
-
-        @pl.loop(0, tokens // BR)
-        def _(i):
-            r = rows_at(i, BR)
-            qb = q_s[r, :]
-            seg = segc_ref[r, :]
-            seg = jnp.concatenate([seg] * (BC // 128), axis=1)
-            lo, hi = bounds[0, i], bounds[1, i]
-            m_s[...] = jnp.full_like(m_s, MASKED)
-
-            @pl.loop(lo, hi)
-            def _(j):
-                c = rows_at(j, BC)
-                keep = seg == segr_ref[0:1, c]
-                for h in range(heads):
-                    s = jnp.where(keep, nn(qb, kt_s[h, :, c]), MASKED)
-                    s_s[h, :, c] = s
-                    m_s[h] = jnp.maximum(m_s[h], s)
-
-            tops = [jnp.max(m_s[h], axis=1, keepdims=True) for h in range(heads)]
-            zero = jnp.zeros((BR, 1), F32)
-
-            def second(j, carry):
-                out, sums = carry
-                c = rows_at(j, BC)
-                new = []
-                for h in range(heads):
-                    e = jnp.exp(s_s[h, :, c] - tops[h])
-                    out = out + nn(e.astype(BF), v_s[h, c, :])
-                    new.append(sums[h] + jnp.sum(e, axis=1, keepdims=True))
-                return out, tuple(new)
-
-            out, sums = lax.fori_loop(
-                lo, hi, second, (jnp.zeros((BR, q_s.shape[1]), F32), (zero,) * heads))
-            lane = head_of(out.shape, 1)
-            div = jnp.broadcast_to(sums[0], out.shape)
-            col = lax.broadcasted_iota(jnp.int32, (BR, 128), 1)
-            lse = jnp.broadcast_to(tops[0] + jnp.log(sums[0]), (BR, 128))
-            for h in range(1, heads):
-                div = jnp.where(lane == h, sums[h], div)
-                lse = jnp.where(col == h, tops[h] + jnp.log(sums[h]), lse)
-            ctx_ref[0, r, :] = (out / div).astype(BF)
-            lse_ref[0, r, :] = lse
+                s = jnp.where(keep, nn(qb, kt_s[h, :, c]), MASKED)
+                s_s[h, :, c] = s
+                m_s[h] = jnp.maximum(m_s[h], s)
+
+        tops = [jnp.max(m_s[h], axis=1, keepdims=True) for h in range(heads)]
+        zero = jnp.zeros((BR, 1), F32)
+
+        def second(j, carry):
+            out, sums = carry
+            c = rows_at(j, BC)
+            new = []
+            for h in range(heads):
+                e = jnp.exp(s_s[h, :, c] - tops[h])
+                out = out + nn(e.astype(BF), v_s[h, c, :])
+                new.append(sums[h] + jnp.sum(e, axis=1, keepdims=True))
+            return out, tuple(new)
+
+        out, sums = lax.fori_loop(
+            lo, hi, second, (jnp.zeros((BR, q_s.shape[1]), F32), (zero,) * heads))
+        lane = head_of(out.shape, 1)
+        div = jnp.broadcast_to(sums[0], out.shape)
+        col = lax.broadcasted_iota(jnp.int32, (BR, 128), 1)
+        lse = jnp.broadcast_to(tops[0] + jnp.log(sums[0]), (BR, 128))
+        for h in range(1, heads):
+            div = jnp.where(lane == h, sums[h], div)
+            lse = jnp.where(col == h, tops[h] + jnp.log(sums[h]), lse)
+        ctx_ref[0, r, :] = (out / div).astype(BF)
+        lse_ref[0, :, r] = lse.T[0:8, :]
 
 
 def attn_bwd(scal, bounds, x_ref, wq_ref, wk_ref, wv_ref, bias_ref, bcol_ref, segc_ref, segr_ref,
@@ -150,7 +148,8 @@
             prod = dob.astype(F32) * ctx_ref[0, r, :].astype(F32)
             lane = head_of(prod.shape, 1)
             inner = [jnp.sum(jnp.where(lane == h, prod, 0.0), axis=1, keepdims=True) for h in range(heads)]
-            lses = [lse_ref[0, r, h : h + 1] for h in range(heads)]
+            stats = jnp.concatenate([lse_ref[0, :, r]] * 16, axis=0).T
+            lses = [stats[:, h : h + 1] for h in range(heads)]
             qts = [qt_s[h * HEAD_DIM : (h + 1) * HEAD_DIM, r] for h in range(heads)]
             dots = [dot_ref[0, h * HEAD_DIM : (h + 1) * HEAD_DIM, r] for h in range(heads)]
 
@@ -355,37 +354,40 @@
 
 def weight_specs(groups, feat, width):
     def one(kind):
-        return pl.BlockSpec((1, feat, width), lambda q, s, b: (kind * groups + jnp.minimum(q, s[0]), 0, 0))
+        return pl.BlockSpec((1, feat, width), lambda q, s, b: (jnp.minimum(q, s[0]), kind, 0))
 
     return [one(kind) for kind in range(3)]
 
 
-def run_fwd(scal, bounds, x, wqkv, bias, segc, segr):
-    groups, feat, width = wqkv.shape[0] // 3, wqkv.shape[1], wqkv.shape[2]
+def run_fwd(bounds, x, wqkv, bias, segc, segr):
+    feat, width = wqkv.shape[1:]
     tokens = x.shape[0]
     heads = feat // HEAD_DIM
-    at_quarter, whole = attn_specs(tokens, width, feat)
+
+    def part(shape, kind=0):
+        return pl.BlockSpec(shape, lambda i, b: (kind,) + (0,) * (len(shape) - 1))
+
     sds = jax.ShapeDtypeStruct
     return pl.pallas_call(
         attn_fwd,
         name="attn_fwd",
-        cost_estimate=pl.CostEstimate(flops=int(40e9), bytes_accessed=int(30e6), transcendentals=0),
-        out_shape=(sds((groups, tokens, feat), BF), sds((groups, tokens, 128), F32)),
+        cost_estimate=pl.CostEstimate(flops=int(10e9), bytes_accessed=int(10e6), transcendentals=0),
+        out_shape=(sds((1, tokens, feat), BF), sds((1, 8, tokens), F32)),
         grid_spec=pltpu.PrefetchScalarGridSpec(
-            num_scalar_prefetch=2, grid=(groups,),
-            in_specs=[whole(tokens, width)] + weight_specs(groups, feat, width)
-            + [at_quarter(8, feat), whole(tokens, 128), whole(8, tokens)],
-            out_specs=(at_quarter(tokens, feat), at_quarter(tokens, 128)),
+            num_scalar_prefetch=1, grid=(1,),
+            in_specs=[part((tokens, width))] + [part((1, feat, width), n) for n in range(3)]
+            + [part((1, 8, feat)), part((tokens, 128)), part((8, tokens))],
+            out_specs=(part((1, tokens, feat)), part((1, 8, tokens))),
             scratch_shapes=[
                 pltpu.VMEM((tokens, feat), BF), pltpu.VMEM((heads, feat, tokens), BF),
                 pltpu.VMEM((heads, tokens, feat), BF), pltpu.VMEM((heads, BR, tokens), F32),
                 pltpu.VMEM((heads, BR, BC), F32)]),
-        compiler_params=pltpu.CompilerParams(vmem_limit_bytes=60 << 20),
-    )(scal, bounds, x, wqkv, wqkv, wqkv, bias, segc, segr)
+        compiler_params=pltpu.CompilerParams(vmem_limit_bytes=40 << 20),
+    )(bounds, x, wqkv, wqkv, wqkv, bias, segc, segr)
 
 
 def run_bwd(scal, bounds, x, wqkv, bias, bcol, segc, segr, ctx, lse, do, dot, s1g):
-    groups, feat, width = wqkv.shape[0] // 3, wqkv.shape[1], wqkv.shape[2]
+    groups, feat, width = wqkv.shape[0], bias.shape[2], wqkv.shape[2]
     tokens = x.shape[0]
     heads = feat // HEAD_DIM
     at_quarter, whole = attn_specs(tokens, width, feat)
@@ -400,7 +402,7 @@
             num_scalar_prefetch=2, grid=(groups,),
             in_specs=[whole(tokens, width)] + weight_specs(groups, feat, width)
             + [at_quarter(8, feat), at_quarter(feat, 128), whole(tokens, 128), whole(8, tokens),
-               at_quarter(tokens, feat), at_quarter(tokens, 128), at_quarter(tokens, feat),
+               at_quarter(tokens, feat), at_quarter(8, tokens), at_quarter(tokens, feat),
                at_quarter(feat, tokens), whole(tokens, width)],
             out_specs=(whole(tokens, width),) + (at_quarter(feat, width),) * 3 + (at_quarter(16, feat),),
             scratch_shapes=[
@@ -582,39 +584,109 @@
     )(terms.reshape((groups, 4, 2, count, width)))
 
 
-def gather_kernel(own_ref, line_ref, all_ref, lines_ref, own_sem, recv_sem, z_sem, y_sem, core_sem, x_sem):
+def shard_kernel(own_ref, line_ref, all_ref, lines_ref, own_sem, recv_sem, z_sem, y_sem):
     w = lax.axis_index("width")
     t = lax.axis_index("tok")
     y = lax.rem(t, 2)
     z = lax.div(t, 2)
-    mine = (pltpu.make_async_copy(own_ref, all_ref.at[:, w, t], own_sem.at[0]),
-            pltpu.make_async_copy(line_ref, lines_ref.at[w, t], own_sem.at[1]))
+    mine = (pltpu.make_async_copy(own_ref, all_ref.at[:, t], own_sem.at[0]),
+            pltpu.make_async_copy(line_ref, lines_ref.at[t], own_sem.at[1]))
     for copy in mine:
         copy.start()
     greet(w, t)
     for copy in mine:
         copy.wait()
 
-    def both(q, s, sems, **where):
-        return (peer_copy(all_ref.at[:, q, s], all_ref.at[:, q, s], sems.at[0], recv_sem.at[0, q, s], **where),
-                peer_copy(lines_ref.at[q, s], lines_ref.at[q, s], sems.at[1], recv_sem.at[1, q, s], **where))
+    def both(s, sems, **where):
+        return (peer_copy(all_ref.at[:, s], all_ref.at[:, s], sems.at[0], recv_sem.at[0, s], **where),
+                peer_copy(lines_ref.at[s], lines_ref.at[s], sems.at[1], recv_sem.at[1, s], **where))
 
     def along(k):
-        return both(w, t, z_sem.at[k - 1], width=w, tok=lax.rem(t + 2 * k, 8))
+        return both(t, z_sem.at[k - 1], width=w, tok=lax.rem(t + 2 * k, 8))
 
     def beside(zz):
-        return both(w, 2 * zz + y, y_sem.at[zz], width=w, tok=t ^ 1)
-
-    def near(q, s):
-        return both(q, s, core_sem.at[q, s], width=w ^ 1, tok=t)
-
-    def across(s):
-        return both(w, s, x_sem.at[s], width=w ^ 2, tok=t)
+        return both(2 * zz + y, y_sem.at[zz], width=w, tok=t ^ 1)
 
     def start(pair):
         for copy in pair:
             copy.start()
 
+    def arrived(s):
+        for copy in both(s, y_sem.at[0], width=w, tok=t ^ 1):
+            copy.wait_recv()
+
+    def sent(pair):
+        for copy in pair:
+            copy.wait_send()
+
+    for k in range(1, 4):
+        start(along(k))
+    start(beside(z))
+    for k in range(1, 4):
+        zz = lax.rem(z + k, 4)
+        arrived(2 * zz + y)
+        start(beside(zz))
+
+    @pl.loop(0, 4)
+    def _(k):
+        s = 2 * lax.rem(z + k, 4) + (1 - y)
+        arrived(s)
+
+    for k in range(1, 4):
+        sent(along(k))
+
+    @pl.loop(0, 4)
+    def _(zz):
+        sent(beside(zz))
+
+
+def gather_kernel(own_ref, line_ref, ctx_ref, lse_ref, all_ref, lines_ref, ctxs_ref, lses_ref,
+                  own_sem, recv_sem, z_sem, y_sem, core_sem, x_sem,
+                  side_recv, side_core, side_x):
+    w = lax.axis_index("width")
+    t = lax.axis_index("tok")
+    y = lax.rem(t, 2)
+    z = lax.div(t, 2)
+    mine = (pltpu.make_async_copy(own_ref, all_ref.at[w, t], own_sem.at[0]),
+            pltpu.make_async_copy(line_ref, lines_ref.at[w, t], own_sem.at[1]),
+            pltpu.make_async_copy(ctx_ref.at[0], ctxs_ref.at[w], own_sem.at[2]),
+            pltpu.make_async_copy(lse_ref.at[0], lses_ref.at[w], own_sem.at[3]))
+    for copy in mine:
+        copy.start()
+    greet(w, t)
+    for copy in mine:
+        copy.wait()
+
+    def both(q, s, sems, **where):
+        return (peer_copy(all_ref.at[q, s], all_ref.at[q, s], sems.at[0], recv_sem.at[0, q, s], **where),
+                peer_copy(lines_ref.at[q, s], lines_ref.at[q, s], sems.at[1], recv_sem.at[1, q, s], **where))
+
+    def along(k):
+        return both(w, t, z_sem.at[k - 1], width=w, tok=lax.rem(t + 2 * k, 8))
+
+    def beside(zz):
+        return both(w, 2 * zz + y, y_sem.at[zz], width=w, tok=t ^ 1)
+
+    def near(q, s):
+        return both(q, s, core_sem.at[q, s], width=w ^ 1, tok=t)
+
+    def across(s):
+        return both(w, s, x_sem.at[s], width=w ^ 2, tok=t)
+
+    def side(q, sems, **where):
+        return (peer_copy(ctxs_ref.at[q], ctxs_ref.at[q], sems.at[0], side_recv.at[0, q], **where),
+                peer_copy(lses_ref.at[q], lses_ref.at[q], sems.at[1], side_recv.at[1, q], **where))
+
+    def side_near(q):
+        return side(q, side_core.at[q], width=w ^ 1, tok=t)
+
+    def side_across():
+        return side(w, side_x, width=w ^ 2, tok=t)
+
+    def start(pair):
+        for copy in pair:
+            copy.start()
+
     def arrived(q, s):
         for copy in near(q, s):
             copy.wait_recv()
@@ -631,6 +703,14 @@
         @pl.when((w == 0) | (w == 2))
         def _():
             start(near(w, s))
+
+    @pl.when(w <= 1)
+    def _():
+        start(side_across())
+
+    @pl.when((w == 0) | (w == 2))
+    def _():
+        start(side_near(w))
 
     for k in range(1, 4):
         start(along(k))
@@ -648,6 +728,12 @@
         arrived(w, s)
         outward(s)
 
+    @pl.when(w >= 2)
+    def _():
+        for copy in side_near(w - 2):
+            copy.wait_recv()
+        start(side_near(w - 2))
+
     @pl.loop(0, 8)
     def _(k):
         zz = lax.rem(z + lax.div(k, 2), 4)
@@ -693,22 +779,66 @@
         def _():
             sent(near(w - 2, s))
 
-
-def gather_fast(own, line):
-    kinds, owned, width = own.shape
+    @pl.when((w == 1) | (w == 3))
+    def _():
+        for copy in side_near(w - 1):
+            copy.wait_recv()
+
+    @pl.when(w == 3)
+    def _():
+        for copy in side_near(0):
+            copy.wait_recv()
+
+    @pl.when(w == 2)
+    def _():
+        for copy in side_near(1):
+            copy.wait_recv()
+
+    @pl.when(w <= 1)
+    def _():
+        sent(side_across())
+
+    @pl.when((w == 0) | (w == 2))
+    def _():
+        sent(side_near(w))
+
+    @pl.when(w >= 2)
+    def _():
+        sent(side_near(w - 2))
+
+
+def shard_fast(own, line):
     hbm = pl.BlockSpec(memory_space=pl.ANY)
     dma = pltpu.SemaphoreType.DMA
+    sds = jax.ShapeDtypeStruct
+    return pl.pallas_call(
+        shard_kernel,
+        name="shard_fast",
+        out_shape=(sds((own.shape[0], 8) + own.shape[1:], BF), sds((8,) + line.shape, BF)),
+        in_specs=[hbm] * 2,
+        out_specs=(hbm,) * 2,
+        scratch_shapes=[dma((2,)), dma((2, 8)), dma((3, 2)), dma((4, 2))],
+        compiler_params=pltpu.CompilerParams(collective_id=2, has_side_effects=True),
+        cost_estimate=pl.CostEstimate(flops=int(10e9), bytes_accessed=int(10e6), transcendentals=0),
+    )(own, line)
+
+
+def gather_fast(own, line, ctx, lse):
+    hbm = pl.BlockSpec(memory_space=pl.ANY)
+    dma = pltpu.SemaphoreType.DMA
+    sds = jax.ShapeDtypeStruct
     return pl.pallas_call(
         gather_kernel,
         name="gather_fast",
-        out_shape=(jax.ShapeDtypeStruct((kinds, 4, 8, owned, width), BF),
-                   jax.ShapeDtypeStruct((4, 8) + line.shape, BF)),
-        in_specs=[hbm, hbm],
-        out_specs=(hbm, hbm),
-        scratch_shapes=[dma((2,)), dma((2, 4, 8)), dma((3, 2)), dma((4, 2)), dma((4, 8, 2)), dma((8, 2))],
-        compiler_params=pltpu.CompilerParams(collective_id=2, has_side_effects=True),
+        out_shape=(sds((4, 8) + own.shape, BF), sds((4, 8) + line.shape, BF),
+                   sds((4,) + ctx.shape[1:], BF), sds((4,) + lse.shape[1:], F32)),
+        in_specs=[hbm] * 4,
+        out_specs=(hbm,) * 4,
+        scratch_shapes=[dma((4,)), dma((2, 4, 8)), dma((3, 2)), dma((4, 2)), dma((4, 8, 2)), dma((8, 2)),
+                        dma((2, 4)), dma((4, 2)), dma((2,))],
+        compiler_params=pltpu.CompilerParams(collective_id=3, has_side_effects=True),
         cost_estimate=pl.CostEstimate(flops=int(30e9), bytes_accessed=int(30e6), transcendentals=0),
-    )(own, line)
+    )(own, line, ctx, lse)
 
 
 def columns(array):
@@ -739,36 +869,20 @@
         line = jnp.concatenate(vectors)
         return jnp.pad(line, (0, width - line.shape[0]))[None, :]
 
-    late = gather_all(jnp.concatenate(weights[3:] + (flat(*biases[2:]),), axis=0))
+    fast = groups == 4 and shards == 8 and owned % 8 == 0
+    late = gather_all(jnp.concatenate([weights[4], flat(*biases[2:])], axis=0))
     late = late.reshape((groups, shards) + late.shape[1:])
     soon = jnp.stack(weights[:3])
     line = jnp.concatenate(biases[:2])
-    if groups == 4 and shards == 8 and owned % 8 == 0:
+    if fast:
         line = jnp.pad(line[None, :], ((0, 7), (0, 128 - line.shape[0])))
-        wqkv, line = gather_fast(soon, line)
-        line = line[:, :, 0, : 2 * owned]
+        own, line = shard_fast(soon, line)
+        line = line[:, 0, : 2 * owned]
     else:
-        got = gather_all(jnp.concatenate([soon.reshape(3 * owned, width), flat(line)], axis=0))
-        wqkv = jnp.swapaxes(got[:, : 3 * owned].reshape(groups * shards, 3, owned, width), 0, 1)
-        line = got[:, 3 * owned, : 2 * owned].reshape(groups, shards, 2 * owned)
-    wqkv = wqkv.reshape(3 * groups, feat, width)
-
-    def rows(lower, count):
-        return late[:, :, lower : lower + count].reshape(groups, count * shards, width)
-
-    wo = rows(0, owned)
-    we, ws = rows(owned, owned_ff), rows(owned + owned_ff, owned_ff)
-    row = late[:, :, owned + 2 * owned_ff]
-    sizes = [b.shape[0] for b in biases[2:]]
-    starts = [sum(sizes[:n]) for n in range(7)]
-    vecs = [row[:, :, a : a + n].reshape(groups, n * shards) for a, n in zip(starts, sizes)]
-    qb = line[:, :, :owned].reshape(groups, feat)
-    vb = line[:, :, owned:].reshape(groups, feat)
-    eb = jnp.pad(vecs[1][:, None, :].astype(F32), ((0, 0), (0, 7), (0, 0)))
-    vec = jnp.stack([v.reshape(-1) for v in [vecs[0], vecs[2]] + vecs[3:]]).astype(F32)
-    vec = jnp.pad(vec, ((2, 0), (0, 0)))
-    bias = jnp.pad(jnp.stack([qb, vb], axis=1).astype(F32), ((0, 0), (0, 6), (0, 0)))
-    bcol = jnp.pad(jnp.stack([qb, vb], axis=2), ((0, 0), (0, 0), (0, 126)))
+        own = lax.all_gather(soon, "tok", axis=1)
+        line = lax.all_gather(line, "tok", axis=0)
+    own = own.reshape(3, feat, width)
+    qv = jnp.stack([line[:, :owned].reshape(feat), line[:, owned:].reshape(feat)])
 
     ends = jnp.cumsum(seq_lengths[0])
     positions = jnp.arange(tokens, dtype=jnp.int32)
@@ -780,7 +894,33 @@
     segr = jnp.broadcast_to(segment[None, :], (8, tokens))
     scal = level[None].astype(jnp.int32)
 
-    ctx, lse = run_fwd(scal, bounds, tokens_in, wqkv, bias, segc, segr)
+    def as_bias(pair):
+        return jnp.pad(pair.astype(F32), ((0, 0), (0, 6), (0, 0)))
+
+    ctx, lse = run_fwd(bounds, tokens_in, own, as_bias(qv[None]), segc, segr)
+    if fast:
+        ws, wo, ctx, lse = gather_fast(weights[5], weights[3], ctx, lse)
+    else:
+        both = gather_all(jnp.concatenate([weights[5], weights[3]], axis=0))
+        both = both.reshape((groups, shards) + both.shape[1:])
+        ws, wo = both[:, :, :owned_ff], both[:, :, owned_ff:]
+        ctx, lse = (lax.all_gather(part[0], "width", axis=0) for part in (ctx, lse))
+    ws, wo = ws.reshape(groups, units, width), wo.reshape(groups, feat, width)
+    we = late[:, :, :owned_ff].reshape(groups, units, width)
+    row = late[:, :, owned_ff]
+    sizes = [b.shape[0] for b in biases[2:]]
+    starts = [sum(sizes[:n]) for n in range(7)]
+    vecs = [row[:, :, a : a + n].reshape(groups, n * shards) for a, n in zip(starts, sizes)]
+    eb = jnp.pad(vecs[1][:, None, :].astype(F32), ((0, 0), (0, 7), (0, 0)))
+    vec = jnp.stack([v.reshape(-1) for v in [vecs[0], vecs[2]] + vecs[3:]]).astype(F32)
+    vec = jnp.pad(vec, ((2, 0), (0, 0)))
+
+    qv = jnp.pad(qv, ((0, 6), (0, width - feat)))
+    wqkv = lax.all_gather(jnp.concatenate([own.reshape(3 * feat, width), qv], axis=0), "width", axis=0)
+    qv = wqkv[:, 3 * feat : 3 * feat + 2, :feat]
+    bias = as_bias(qv)
+    bcol = jnp.pad(jnp.swapaxes(qv, 1, 2), ((0, 0), (0, 0), (0, 126)))
+
     result, s1g, do, dot, dwo, vg, ebg, de, ds = run_middle(
         scal, tokens_in, ctx, wo, we, ws, vec, eb, out_grad[0])
     mine = jnp.arange(groups) <= level

time: 401 us -> 420 us (1.047)
  Pallas kernels: 284 us -> 349 us
  waiting for transfers between devices: 48 us -> 3.14 us
    pallas_call x1 -> x2, Pallas kernels: 38.5 us -> 112 us  [the longest x1 85.7 us: gather_fast(): pl.pallas_call(gather_kernel, name='gather_fast', out_shape=(sds((4, 8) +...]
    all_gather x1, waiting for transfers between devices: 38.4 us -> 0.02 us  [gather_all(): return lax.all_gather(pack, ('width', 'tok'), axis=0, tiled=False)]
    reduce_scatter x1, waiting for transfers between devices: 9.55 us -> 3.05 us  [scatter_all(): lax.psum_scatter(flat, ('width', 'tok'), scatter_dimension=0, tiled=True)[0]]
    pallas_call x1, Pallas kernels: 167 us -> 162 us  [reduce_fast(): pl.pallas_call(reduce_kernel, name='reduce_fast', out_shape=jax.ShapeDtyp...]
    slice x5, local copies, waits for them, and re-layouts: 12.3 us -> 7.36 us  [the longest x1 4.79 us: local(): we = late[:, :, :owned_ff].reshape(groups, units, width)]
    unnamed x4 -> x21, local copies, waits for them, and re-layouts: 0.17 us -> 4.56 us
  transfers between devices with their start and end apart: 2 -> 3, of which waited for: 2 -> 1; matrix products, arithmetic and copies ran while one was open for 4% -> 9% of each run, Pallas kernels for 63% -> 83%
where the time goes in v5:
time: 420 us; the launch traced here: 419 us
  Pallas kernels  349 us (83%)
  local copies, waits for them, and re-layouts  27 us (6%)
  other arithmetic  25.2 us (6%)
  between operations  14.1 us (3%)
    pallas_call x1, Pallas kernels, reduce_fast(): pl.pallas_call(reduce_kernel, name='reduce_fast', out_shape=jax.ShapeDtyp...  162 us
    pallas_call x1, Pallas kernels, gather_fast(): pl.pallas_call(gather_kernel, name='gather_fast', out_shape=(sds((4, 8) +...  85.7 us
    pallas_call x1, Pallas kernels, run_middle(): pl.pallas_call(middle, name='middle', cost_estimate=pl.CostEstimate(flops...  30.8 us
    pallas_call x1, Pallas kernels, run_bwd(): pl.pallas_call(attn_bwd, name='attn_bwd', cost_estimate=pl.CostEstimate(f...  30.1 us
    pallas_call x1, Pallas kernels, shard_fast(): pl.pallas_call(shard_kernel, name='shard_fast', out_shape=(sds((own.shape...  26.1 us
    pallas_call x1, Pallas kernels, run_fwd(): pl.pallas_call(attn_fwd, name='attn_fwd', cost_estimate=pl.CostEstimate(f...  14.3 us
    select_n x2, other arithmetic, only(): jnp.where(mine.reshape((groups,) + (1,) * (term.ndim - 1)), term, jnp.zer...  9.7 us
  transfers between devices with their start and end apart: 3, of which 1 were waited for; matrix products, arithmetic and copies ran while one was open for 9% of the time, Pallas kernels for 83%

profile of v5, /device:TPU:0, one launch (start us, length us, event | category | flops | bytes accessed | tf_op | source)
XLA Modules:
  0.0 418.8 jit_solution(6608494179810615224)
XLA Ops:
  7.2 4.8 %concatenate.40 = bf16[240]{0:T(256)(128)(2,1)S(1)} concatenate(bf16[24]{0:T(256)(128)(2,1)} %param.28, bf16[96]{0:T(256)(128)(2,1)} %param.29, bf16[24]{0:T(256)(128)(2,1)} %param.30, bf16[24]{0:T(256)(128)(2,1)} %param.31, bf16[24]{0:T(256)(128)(2,1)} %param.32, bf16[24]{0:T(256)(128)(2,1)} %param.33, bf16[24]{0:T(256)(128)(2,1)} %param.34), dimensions={0} | concatenate | bytes 960 | tf_op jit(solution)/shard_map/concatenate | solution.py:869
  12.0 1.6 maximum_bitcast_fusion
  13.7 0.8 maximum_bitcast_fusion.1
  14.4 0.6 pad.55.line_ref
  15.0 1.5 pad_maximum_fusion.1.own_ref
  16.5 26.1 %shard_fast.1 = (bf16[3,8,24,768]{3,2,1,0:T(8,128)(2,1)}, bf16[8,8,128]{2,1,0:T(8,128)(2,1)}) custom-call(bf16[3,24,768]{2,1,0:T(8,128)(2,1)} %pad_maximum_fusion.1.own_ref, bf16[8,128]{1,0:T(8,128)(2,1)} %pad.55.line_ref), custom_call_target="tpu_custom_call" | custom-call | flops 10000000000 | bytes 10000000 | tf_op jit(solution)/shard_map/shard_fast/pallas_call | solution.py:814
  42.5 0.7 slice.172
  43.5 2.1 pad_maximum_fusion
  45.9 0.1 reduce
  46.5 0.2 convert_reduce_fusion.2
  46.8 0.2 broadcast_in_dim.84.segc_ref
  47.0 1.4 copy-done
  48.4 1.4 copy-done.4
  49.8 14.3 %attn_fwd.1 = (bf16[1,1024,192]{2,1,0:T(8,128)(2,1)S(1)}, f32[1,8,1024]{2,1,0:T(8,128)S(1)}) custom-call(s32[2,8]{1,0:T(2,128)S(1)} %pad_add_fusion.bounds, bf16[1024,768]{1,0:T(8,128)(2,1)S(1)} %copy-done.4, bf16[3,192,768]{2,1,0:T(8,128)(2,1)S(1)} %bitcast.82, bf16[3,192,768]{2,1,0:T(8,128)(2,1)S(1)} %bitcast.83, bf16[3,192,768]{2,1,0:T(8,128)(2,1)S(1)} %bitcast.84, ...), custom_call_target="tpu_custom_call" | custom-call | flops 10000000000 | bytes 10000000 | tf_op jit(solution)/shard_map/attn_fwd/pallas_call | solution.py:371
  64.1 0.8 copy-done.5
  64.9 0.6 copy-done.6
  65.5 85.7 %gather_fast.1 = (bf16[4,8,96,768]{3,2,1,0:T(8,128)(2,1)}, bf16[4,8,24,768]{3,2,1,0:T(8,128)(2,1)}, bf16[4,1024,192]{2,1,0:T(8,128)(2,1)}, f32[4,8,1024]{2,1,0:T(8,128)}) custom-call(bf16[96,768]{1,0:T(8,128)(2,1)} %own_ref.1, bf16[24,768]{1,0:T(8,128)(2,1)} %line_ref.1, bf16[1,1024,192]{2,1,0:T(8,128)(2,1)} %copy-done.5, f32[1,8,1024]{2,1,0:T(8,128)} %copy-done.6), custom_call_target="tpu_custom_call" | custom-call | flops 30000001024 | bytes 30000000 | tf_op jit(solution)/shard_map/gather_fast/pallas_call | solution.py:830
  151.2 1.1 slice.222
  152.4 4.8 %slice.221 = bf16[4,8,96,768]{3,2,1,0:T(8,128)(2,1)} slice(bf16[4,8,97,768]{3,2,1,0:T(8,128)(2,1)} %bitcast.90), slice={[0:4], [0:8], [0:96], [0:768]} | slice | bytes 9437184 | tf_op jit(solution)/shard_map/slice | solution.py:909
  157.3 0.1 stack_reshape_reshape.19
  157.4 0.1 stack_reshape_reshape.20
  157.5 0.1 stack_reshape_reshape.21
  157.6 0.1 stack_reshape_reshape.22
  157.9 0.6 pad_convert_fusion.2.vec_ref
  158.6 0.7 pad_convert_fusion.1.eb_ref
  159.2 30.8 %middle.1 = (bf16[1024,768]{1,0:T(8,128)(2,1)}, f32[1024,768]{1,0:T(8,128)}, bf16[4,1024,192]{2,1,0:T(8,128)(2,1)}, bf16[4,192,1024]{2,1,0:T(8,128)(2,1)}, bf16[...) custom-call(s32[1]{0:T(128)} %bitcast.scal, ...), custom_call_target="tpu_custom_call" | custom-call | flops 49999998976 | bytes 30000000 | tf_op jit(solution)/shard_map/middle/pallas_call | solution.py:324
  190.1 0.7 convert.39
  191.5 0.9 slice_reduce_fusion
  192.6 0.1 concatenate.44
  192.8 7.3 %maximum_select_fusion = bf16[4,8,216,768]{3,2,1,0:T(8,128)(2,1)S(1)} fusion(bf16[4,8,96,768]{3,2,1,0:T(8,128)(2,1)} %bitcast.88, bf16[4,8,96,768]{3,2,1,0:T(8,128)(2,1)} %bitcast.87, bf16[4,8,24,768]{3,2,1,0:T(8,128)(2,1)} %bitcast.92, pred[4]{0:T(512)(128)(4,1)S(1)} %iota_compare_fusion.7), kind=kLoop, calls=%fused_computation.3 | loop fusion | flops 37158912 | bytes 21233668 | tf_op jit(solution)/shard_map/jit(_where)/select_n | solution.py:935
  200.0 5.3 %fusion.1 = bf16[4,8,224,768]{3,2,1,0:T(8,128)(2,1)} fusion(bf16[4,8,1,768]{3,2,1,0:T(2,128)(2,1)S(1)} %copy.72, bf16[4,8,216,768]{3,2,1,0:T(8,128)(2,1)S(1)} %maximum_select_fusion), kind=kLoop, calls=%fused_computation.2 | loop fusion | flops 33030144 | bytes 21676032 | tf_op jit(solution)/shard_map/concatenate | solution.py:946
  205.4 0.7 slice.230
  206.1 0.2 copy.71
  206.4 0.8 copy.67.bias_ref
  207.1 0.7 pad.66.bcol_ref
  207.9 30.1 %attn_bwd.1 = (f32[1024,768]{1,0:T(8,128)}, bf16[4,192,768]{2,1,0:T(8,128)(2,1)}, bf16[4,192,768]{2,1,0:T(8,128)(2,1)}, bf16[4,192,768]{2,1,0:T(8,128)(2,1)}, f32[4,16,192]{2,1,0:T(8,128)}) custom-call(s32[1]{0:T(128)} %bitcast.scal, s32[2,8]{1,0:T(2,128)} %copy-done.3, bf16[1024,768]{1,0:T(8,128)(2,1)} %x_ref.5, bf16[4,584,768]{2,1,0:T(8,128)(2,1)} %bitcast.104, ...), custom_call_target="tpu_custom_call" | custom-call | flops 89999998976 | bytes 30000000 | tf_op jit(solution)/shard_map/attn_bwd/pallas_call | solution.py:395
  238.0 0.8 slice_reduce_fusion.2
  239.3 2.4 maximum_select_fusion.1
  241.7 0.3 fusion.3
  242.1 162.2 %reduce_fast.1 = f32[80,768]{1,0:T(8,128)S(1)} custom-call(bf16[4,4,2,80,768]{4,3,2,1,0:T(8,128)(2,1)S(1)} %bitcast.80), custom_call_target="tpu_custom_call" | custom-call | tf_op jit(solution)/shard_map/reduce_fast/pallas_call | solution.py:570
  404.2 0.6 slice_bitcast_fusion.10
  404.8 0.7 fusion.18
  405.5 3.1 reduce-scatter.2.cloned.1.call-done
  408.6 1.1 convert_bitcast_fusion
  409.6 0.8 slice_bitcast_fusion
  410.5 0.6 slice_bitcast_fusion.2
  411.1 0.6 slice_bitcast_fusion.3
  411.7 0.5 slice_bitcast_fusion.8
  (63 shorter events, 3.0 us)
Async XLA Ops:
  7.2 144.0 %all-gather.8.cloned.1.call-start = ((), (), s32[]{:S(2)}) async-start(), calls=%async_computation.3 | async-start | bytes 5271552 | tf_op jit(solution)/shard_map/all_gather | solution.py:849
  13.6 191.8 %all-gather.6.cloned.1.call-start = ((), (), s32[]{:S(2)}) async-start(), calls=%async_computation.2 | async-start | bytes 4485120 | tf_op jit(solution)/shard_map/all_gather | solution.py:919
  16.5 29.3 %copy-start.7 = (s32[1,24]{1,0:T(1,128)S(1)}, s32[1,24]{1,0:T(1,128)}, u32[]{:S(2)}) copy-start(s32[1,24]{1,0:T(1,128)} %param.19) | copy-start | bytes 292
  45.7 362.8 %reduce-scatter.2.cloned.1.call-start = ((), (), s32[]{:S(2)}) async-start(), calls=%async_computation.1 | async-start | bytes 11354112 | tf_op jit(solution)/shard_map/reduce_scatter | solution.py:854
  46.8 17.3 %copy-start.3 = (s32[2,8]{1,0:T(2,128)}, s32[2,8]{1,0:T(2,128)S(1)}, u32[]{:S(2)}) copy-start(s32[2,8]{1,0:T(2,128)S(1)} %pad_add_fusion.bounds) | copy-start | bytes 196
  47.0 17.1 %copy-start.1 = (s32[1024,128]{1,0:T(8,128)}, s32[1024,128]{1,0:T(8,128)S(1)}, u32[]{:S(2)}) copy-start(s32[1024,128]{1,0:T(8,128)S(1)} %broadcast_in_dim.84.segc_ref) | copy-start | bytes 1572868
  47.0 17.1 %copy-start.2 = (s32[8,1024]{1,0:T(8,128)}, s32[8,1024]{1,0:T(8,128)S(1)}, u32[]{:S(2)}) copy-start(s32[8,1024]{1,0:T(8,128)S(1)} %lt.6.segr_ref) | copy-start | bytes 98308
  47.0 1.4 copy-start
  48.4 1.4 copy-start.4
  64.1 0.8 copy-start.5
  64.9 0.6 copy-start.6
Sparse Core Ops, SparseCore 0:
  13.8 71.9 all-gather.7
  87.3 45.1 all-gather.5
  205.5 203.0 reduce-scatter.1

commit v6 on v5

--- a/solution.py
+++ b/solution.py
@@ -104,7 +104,7 @@
 
 def attn_bwd(scal, bounds, x_ref, wq_ref, wk_ref, wv_ref, bias_ref, bcol_ref, segc_ref, segr_ref,
              ctx_ref, lse_ref, do_ref, dot_ref, s1g_ref,
-             ig_ref, dwq_ref, dwk_ref, dwv_ref, db_ref,
+             ig_ref, pack_ref,
              q_s, qt_s, k_s, kt_s, vt_s, dq_s, dkt_s, dvt_s, kt_f, vt_f):
     heads = q_s.shape[1] // HEAD_DIM
     tokens = x_ref.shape[0]
@@ -179,12 +179,16 @@
             ig_ref[r, :] += nn(dq_s[r, :], wq) + tn(dkt_s[:, r], wk) + tn(dvt_s[:, r], wv)
 
         x = x_ref[...]
-        dwq_ref[0] = tn(dq_s[...], x).astype(BF)
-        dwk_ref[0] = nn(dkt_s[...], x).astype(BF)
-        dwv_ref[0] = nn(dvt_s[...], x).astype(BF)
+        chunks = pack_ref.shape[1]
+        part = wq.shape[0] // chunks
+        terms = (tn(dq_s[...], x), nn(dkt_s[...], x), nn(dvt_s[...], x))
+        for n, term in enumerate(terms):
+            pack_ref[0, :, n * part : (n + 1) * part, :] = term.astype(BF).reshape(chunks, part, x.shape[1])
         ones = jnp.ones((8, tokens), BF)
-        db_ref[0, 0:8, :] = nn(ones, dq_s[...])
-        db_ref[0, 8:16, :] = nt(ones, dvt_s[...])
+        pack_ref[0, :, 3 * part :, :] = jnp.zeros((chunks, 8, x.shape[1]), BF)
+        for n, line in enumerate((nn(ones, dq_s[...]), nt(ones, dvt_s[...]))):
+            for k in range(chunks):
+                pack_ref[0, k, 3 * part :, n * 256 : n * 256 + part] = line[:, k * part : (k + 1) * part].astype(BF)
 
 
 def normal_parts(value):
@@ -193,11 +197,31 @@
     return cum, phi
 
 
-def middle(scal, x_ref, ctx_ref, wo_ref, e_ref, s_ref, vec_ref, eb_ref, c_ref,
-           lo_ref, s1g_ref, do_ref, dot_ref, dwo_ref, vg_ref, ebg_ref, de_hbm, ds_hbm,
-           nl_s, n1_s, r1_s, br_s, act_s, gp_s, ug_s, bg_s, stage, sems):
+def middle(scal, x_ref, ctx_ref, wo_ref, e_hbm, s_hbm, vec_ref, eb_ref, c_ref,
+           lo_ref, s1g_ref, do_ref, dot_ref, vg_ref, ebg_ref, pack_hbm,
+           nl_s, n1_s, r1_s, br_s, act_s, gp_s, ug_s, bg_s, stage, sems,
+           e_s, s_s, in_sem, dwo_s, dwo_sem, zero_sem):
     tokens, width = x_ref.shape
     used = scal[0] + 1
+    groups, chunks, each, _ = e_s.shape
+    feat = dwo_s.shape[2]
+    units = chunks * each
+
+    def loads(q):
+        return (pltpu.make_async_copy(e_hbm.at[q, :, 0:each, :], e_s.at[q], in_sem.at[0, q]),
+                pltpu.make_async_copy(s_hbm.at[q], s_s.at[q], in_sem.at[1, q]))
+
+    @pl.loop(0, used)
+    def _(q):
+        for copy in loads(q):
+            copy.start()
+
+    def e_at(q):
+        return e_s[q].reshape(units, width)
+
+    def s_at(q):
+        return s_s[q].reshape(units, width)
+
     tiles = tokens // RT
     ob, sb = vec_ref[2:3, :], vec_ref[3:4, :]
     g1, b1 = vec_ref[4:5, :], vec_ref[5:6, :]
@@ -223,15 +247,18 @@
 
     @pl.loop(0, used)
     def _(q):
+        for copy in loads(q):
+            copy.wait()
+
         @pl.loop(0, tiles)
         def _(i):
             r = rows_at(i, RT)
-            u = nt(nl_s[r, :], e_ref[q]) + eb_ref[q, 0:1, :]
+            u = nt(nl_s[r, :], e_at(q)) + eb_ref[q, 0:1, :]
             cum, phi = normal_parts(u)
             act = (u * cum).astype(BF)
             act_s[q, r, :] = act
             gp_s[q, r, :] = (cum + u * phi).astype(BF)
-            br_s[r, :] += nn(act, s_ref[q])
+            br_s[r, :] += nn(act, s_at(q))
 
     zero = jnp.zeros((1, width), F32)
 
@@ -257,32 +284,45 @@
     vg_ref[7:8, :] = b2g
     vg_ref[3:4, :] = sbg
 
-    def moved(kind, q, out_hbm):
-        return pltpu.make_async_copy(stage.at[kind], out_hbm.at[q], sems.at[kind])
+    def slot(kind):
+        return slice(feat + kind * each, feat + (kind + 1) * each)
+
+    def moved(kind, q):
+        return pltpu.make_async_copy(stage.at[kind], pack_hbm.at[q, :, slot(kind), :], sems.at[kind])
+
+    def put(kind, n, value):
+        count = value.shape[0]
+        value = value.astype(BF)
+        if chunks == 1:
+            stage[kind, 0, n * count : (n + 1) * count, :] = value
+        else:
+            some = count // each
+            stage[kind, n * some : (n + 1) * some] = value.reshape(some, each, width)
 
     @pl.loop(0, used)
     def _(q):
         def tile(i, total):
             r = rows_at(i, RT)
-            d = nt(bg_s[r, :], s_ref[q]) * gp_s[q, r, :].astype(F32)
+            d = nt(bg_s[r, :], s_at(q)) * gp_s[q, r, :].astype(F32)
             ug = d.astype(BF)
             ug_s[r, :] = ug
-            s1g_ref[r, :] += nn(ug, e_ref[q])
+            s1g_ref[r, :] += nn(ug, e_at(q))
             return total + jnp.sum(ug.astype(F32), axis=0, keepdims=True)
 
         ebg_ref[q, 0:1, :] = lax.fori_loop(0, tiles, tile, zero)
 
         @pl.when(q > 0)
         def _():
-            moved(0, q - 1, de_hbm).wait()
-            moved(1, q - 1, ds_hbm).wait()
-
-        for n in range(width // RT):
-            cols = slice(n * RT, (n + 1) * RT)
-            stage[0, cols, :] = tn(ug_s[:, cols], nl_s[...]).astype(BF)
-            stage[1, cols, :] = tn(act_s[q, :, cols], bg_s[...]).astype(BF)
-        moved(0, q, de_hbm).start()
-        moved(1, q, ds_hbm).start()
+            moved(0, q - 1).wait()
+            moved(1, q - 1).wait()
+
+        half = units // 2
+        for n in range(2):
+            cols = slice(n * half, (n + 1) * half)
+            put(0, n, tn(ug_s[:, cols], nl_s[...]))
+            put(1, n, tn(act_s[q, :, cols], bg_s[...]))
+        moved(0, q).start()
+        moved(1, q).start()
 
     def first_norm(i, sums):
         r = rows_at(i, RT)
@@ -308,19 +348,48 @@
     vg_ref[5:6, :] = b1g
     vg_ref[2:3, :] = obg
 
+    def moved_out(q):
+        return pltpu.make_async_copy(dwo_s.at[q], pack_hbm.at[q, :, 0:feat, :], dwo_sem.at[q])
+
     @pl.loop(0, used)
     def _(q):
-        dwo_ref[q] = tn(ctx_ref[q], ug_s[...]).astype(BF)
-
-    moved(0, used - 1, de_hbm).wait()
-    moved(1, used - 1, ds_hbm).wait()
+        dwo_s[q] = tn(ctx_ref[q], ug_s[...]).astype(BF).reshape(chunks, feat, width)
+        moved_out(q).start()
+
+    moved(0, used - 1).wait()
+    moved(1, used - 1).wait()
+    stage[0] = jnp.zeros_like(stage[0])
+
+    def cleared(q):
+        zeros = stage.at[0]
+        return (pltpu.make_async_copy(zeros.at[:, 0:feat, :], pack_hbm.at[q, :, 0:feat, :], zero_sem.at[0, q]),
+                pltpu.make_async_copy(zeros, pack_hbm.at[q, :, slot(0), :], zero_sem.at[1, q]),
+                pltpu.make_async_copy(zeros, pack_hbm.at[q, :, slot(1), :], zero_sem.at[2, q]))
+
+    @pl.loop(used, groups)
+    def _(q):
+        for copy in cleared(q):
+            copy.start()
+
+    @pl.loop(0, used)
+    def _(q):
+        moved_out(q).wait()
+
+    @pl.loop(used, groups)
+    def _(q):
+        for copy in cleared(q):
+            copy.wait()
 
 
 def run_middle(scal, x, ctx, wo, e, s, vec, eb, cot):
     groups, feat, width = wo.shape
+    chunks, each = s.shape[1:3]
     tokens = x.shape[0]
     vm = pl.BlockSpec(memory_space=pltpu.VMEM)
+    hbm = pl.BlockSpec(memory_space=pl.ANY)
+    dma = pltpu.SemaphoreType.DMA
     sds = jax.ShapeDtypeStruct
+    part = feat // chunks
     return pl.pallas_call(
         middle,
         name="middle",
@@ -328,16 +397,19 @@
         out_shape=(
             sds((tokens, width), BF), sds((tokens, width), F32),
             sds((groups, tokens, feat), BF), sds((groups, feat, tokens), BF),
-            sds((groups, feat, width), BF), sds((8, width), F32), sds((groups, 8, width), F32),
-            sds(e.shape, BF), sds(s.shape, BF)),
-        in_specs=[pl.BlockSpec(memory_space=pltpu.SMEM)] + [vm] * 8,
-        out_specs=(vm,) * 7 + (pl.BlockSpec(memory_space=pl.ANY),) * 2,
+            sds((8, width), F32), sds((groups, 8, width), F32),
+            sds((groups, chunks, part + 2 * each + 8, width), BF)),
+        in_specs=[pl.BlockSpec(memory_space=pltpu.SMEM)] + [vm] * 3 + [hbm] * 2 + [vm] * 3,
+        out_specs=(vm,) * 6 + (hbm,),
         scratch_shapes=[
             pltpu.VMEM((tokens, width), BF), pltpu.VMEM((tokens, width), F32),
             pltpu.VMEM((tokens, 128), F32), pltpu.VMEM((tokens, width), F32),
             pltpu.VMEM((groups, tokens, width), BF), pltpu.VMEM((groups, tokens, width), BF),
             pltpu.VMEM((tokens, width), BF), pltpu.VMEM((tokens, width), BF),
-            pltpu.VMEM((2, width, width), BF), pltpu.SemaphoreType.DMA((2,))],
+            pltpu.VMEM((2, chunks, each, width), BF), dma((2,)),
+            pltpu.VMEM((groups, chunks, each, width), BF), pltpu.VMEM((groups, chunks, each, width), BF),
+            dma((2, groups)), pltpu.VMEM((groups, chunks, part, width), BF), dma((groups,)),
+            dma((3, groups))],
         compiler_params=pltpu.CompilerParams(vmem_limit_bytes=62 << 20),
     )(scal, x, ctx, wo, e, s, vec, eb, cot)
 
@@ -386,8 +458,9 @@
     )(bounds, x, wqkv, wqkv, wqkv, bias, segc, segr)
 
 
-def run_bwd(scal, bounds, x, wqkv, bias, bcol, segc, segr, ctx, lse, do, dot, s1g):
+def run_bwd(chunks, scal, bounds, x, wqkv, bias, bcol, segc, segr, ctx, lse, do, dot, s1g):
     groups, feat, width = wqkv.shape[0], bias.shape[2], wqkv.shape[2]
+    part = feat // chunks
     tokens = x.shape[0]
     heads = feat // HEAD_DIM
     at_quarter, whole = attn_specs(tokens, width, feat)
@@ -396,15 +469,15 @@
         attn_bwd,
         name="attn_bwd",
         cost_estimate=pl.CostEstimate(flops=int(90e9), bytes_accessed=int(30e6), transcendentals=0),
-        out_shape=(sds((tokens, width), F32),) + (sds((groups, feat, width), BF),) * 3
-        + (sds((groups, 16, feat), F32),),
+        out_shape=(sds((tokens, width), F32), sds((groups, chunks, 3 * part + 8, width), BF)),
         grid_spec=pltpu.PrefetchScalarGridSpec(
             num_scalar_prefetch=2, grid=(groups,),
             in_specs=[whole(tokens, width)] + weight_specs(groups, feat, width)
             + [at_quarter(8, feat), at_quarter(feat, 128), whole(tokens, 128), whole(8, tokens),
                at_quarter(tokens, feat), at_quarter(8, tokens), at_quarter(tokens, feat),
                at_quarter(feat, tokens), whole(tokens, width)],
-            out_specs=(whole(tokens, width),) + (at_quarter(feat, width),) * 3 + (at_quarter(16, feat),),
+            out_specs=(whole(tokens, width), pl.BlockSpec(
+                (1, chunks, 3 * part + 8, width), lambda q, s, b: (jnp.minimum(q, s[0]), 0, 0, 0))),
             scratch_shapes=[
                 pltpu.VMEM((tokens, feat), BF), pltpu.VMEM((feat, tokens), BF),
                 pltpu.VMEM((heads, tokens, feat), BF), pltpu.VMEM((heads, feat, tokens), BF),
@@ -905,8 +978,10 @@
         both = both.reshape((groups, shards) + both.shape[1:])
         ws, wo = both[:, :, :owned_ff], both[:, :, owned_ff:]
         ctx, lse = (lax.all_gather(part[0], "width", axis=0) for part in (ctx, lse))
-    ws, wo = ws.reshape(groups, units, width), wo.reshape(groups, feat, width)
-    we = late[:, :, :owned_ff].reshape(groups, units, width)
+    wo = wo.reshape(groups, feat, width)
+    we, chunks = late, shards
+    if not fast:
+        we, ws, chunks = late[:, :, :owned_ff].reshape(groups, 1, units, width), ws.reshape(groups, 1, units, width), 1
     row = late[:, :, owned_ff]
     sizes = [b.shape[0] for b in biases[2:]]
     starts = [sum(sizes[:n]) for n in range(7)]
@@ -916,26 +991,30 @@
     vec = jnp.pad(vec, ((2, 0), (0, 0)))
 
     qv = jnp.pad(qv, ((0, 6), (0, width - feat)))
+    own, wo = lax.optimization_barrier((own, wo))
     wqkv = lax.all_gather(jnp.concatenate([own.reshape(3 * feat, width), qv], axis=0), "width", axis=0)
     qv = wqkv[:, 3 * feat : 3 * feat + 2, :feat]
     bias = as_bias(qv)
     bcol = jnp.pad(jnp.swapaxes(qv, 1, 2), ((0, 0), (0, 0), (0, 126)))
 
-    result, s1g, do, dot, dwo, vg, ebg, de, ds = run_middle(
+    result, s1g, do, dot, vg, ebg, first = run_middle(
         scal, tokens_in, ctx, wo, we, ws, vec, eb, out_grad[0])
     mine = jnp.arange(groups) <= level
 
-    def pieces(term):
-        return term.reshape((groups, shards, -1) + term.shape[2:])
-
     def split(line):
         return line.reshape(groups, shards, -1)
 
     def only(term):
         return jnp.where(mine.reshape((groups,) + (1,) * (term.ndim - 1)), term, jnp.zeros_like(term))
 
-    def packed(*terms):
-        return only(jnp.concatenate([pieces(t) for t in terms], axis=2))
+    def parted(term, sizes):
+        if fast:
+            return term
+        out, at = [], 0
+        for size in sizes:
+            out.append(term[:, 0, at : at + size * shards].reshape(groups, shards, size, width))
+            at = at + size * shards
+        return jnp.concatenate(out + [jnp.zeros((groups, shards, 8, width), BF)], axis=2)
 
     def lined(*lines):
         line = jnp.concatenate(lines, axis=2).astype(BF)
@@ -943,25 +1022,29 @@
         return jnp.pad(line[:, :, None, :], ((0, 0), (0, 0), (0, 7), (0, 0)))
 
     line = lined(only(split(ebg[:, 0])), *(split(vg[n]) for n in range(2, 8)))
-    first = jnp.concatenate([packed(dwo, de, ds), line], axis=2)
+    first = parted(first, (owned, owned_ff, owned_ff))
+    first = lax.dynamic_update_slice(first, line, (0, 0, first.shape[2] - 8, 0))
     first, s1g = lax.optimization_barrier((first, s1g))
     early = scatter_all(first)
-    input_grad, dwq, dwk, dwv, db = run_bwd(
-        scal, bounds, tokens_in, wqkv, bias, bcol, segc, segr, ctx, lse, do, dot, s1g)
-
-    line = lined(only(split(db[:, 0])), only(split(db[:, 8])))
-    second = jnp.concatenate([packed(dwq, dwk, dwv), line], axis=2)
-    if groups == 4 and shards == 8 and owned % 8 == 0:
+    input_grad, second = run_bwd(
+        chunks, scal, bounds, tokens_in, wqkv, bias, bcol, segc, segr, ctx, lse, do, dot, s1g)
+
+    if fast:
         final = reduce_fast(second)
+        late = [final[3 * owned, :owned], final[3 * owned, 256 : 256 + owned]]
     else:
+        line = only(jnp.concatenate([split(second[:, 0, 3 * feat, n : n + feat]) for n in (0, 256)], axis=2))
+        second = only(parted(second, (owned,) * 3))
+        line = jnp.pad(line, ((0, 0), (0, 0), (0, width - line.shape[2])))[:, :, None, :]
+        second = lax.dynamic_update_slice(second, line, (0, 0, 3 * owned, 0))
         final = scatter_all(second).astype(F32)
+        late = [final[3 * owned, :owned], final[3 * owned, owned : 2 * owned]]
     early = early.astype(F32)
     outs = [final[n * owned : (n + 1) * owned] for n in range(3)]
     outs += [early[:owned], early[owned : owned + owned_ff], early[owned + owned_ff : owned + 2 * owned_ff]]
-    late = final[3 * owned]
     soon = early[owned + 2 * owned_ff]
     vecs = [soon[owned_ff + n * owned : owned_ff + (n + 1) * owned] for n in range(6)]
-    outs += [late[:owned], late[owned : 2 * owned], vecs[0], soon[:owned_ff]] + vecs[1:]
+    outs += late + [vecs[0], soon[:owned_ff]] + vecs[1:]
     return (result[None], input_grad[None]) + tuple(outs)
 
 

time: 420 us -> 382 us (0.910)
  Pallas kernels: 349 us -> 327 us
  other arithmetic: 25.2 us -> 8.51 us
    pallas_call x1, Pallas kernels: 85.7 us -> 66.6 us  [gather_fast(): pl.pallas_call(gather_kernel, name='gather_fast', out_shape=(sds((4, 8) +...]
    select_n x2 -> x0, other arithmetic: 9.7 us -> none  [only(): jnp.where(mine.reshape((groups,) + (1,) * (term.ndim - 1)), term, jnp.zer...]
    slice x4 -> x1, local copies, waits for them, and re-layouts: 6.69 us -> 0.51 us  [local(): outs += late + [vecs[0], soon[:owned_ff]] + vecs[1:]]
    concatenate x2 -> x0, other arithmetic: 5.67 us -> none  [the longest x1 5.32 us: local(): first = jnp.concatenate([packed(dwo, de, ds), line], axis=2)]
  transfers between devices with their start and end apart: 3 -> 3, of which waited for: 1 -> 1; matrix products, arithmetic and copies ran while one was open for 9% -> 4% of each run, Pallas kernels for 83% -> 86%
where the time goes in v6:
time: 382 us; the launch traced here: 381 us
  Pallas kernels  327 us (86%)
  local copies, waits for them, and re-layouts  24.8 us (6%)
  between operations  14.1 us (4%)
  other arithmetic  8.51 us (2%)
  waiting for transfers between devices  6.55 us (2%)
    pallas_call x1, Pallas kernels, reduce_fast(): pl.pallas_call(reduce_kernel, name='reduce_fast', out_shape=jax.ShapeDtyp...  158 us
    pallas_call x1, Pallas kernels, gather_fast(): pl.pallas_call(gather_kernel, name='gather_fast', out_shape=(sds((4, 8) +...  66.6 us
    pallas_call x1, Pallas kernels, run_middle(): pl.pallas_call(middle, name='middle', cost_estimate=pl.CostEstimate(flops...  31.7 us
    pallas_call x1, Pallas kernels, run_bwd(): pl.pallas_call(attn_bwd, name='attn_bwd', cost_estimate=pl.CostEstimate(f...  30.1 us
    pallas_call x1, Pallas kernels, shard_fast(): pl.pallas_call(shard_kernel, name='shard_fast', out_shape=(sds((own.shape...  26.5 us
    pallas_call x1, Pallas kernels, run_fwd(): pl.pallas_call(attn_fwd, name='attn_fwd', cost_estimate=pl.CostEstimate(f...  14.3 us
  transfers between devices with their start and end apart: 3, of which 1 were waited for; matrix products, arithmetic and copies ran while one was open for 4% of the time, Pallas kernels for 86%

profile of v6, /device:TPU:0, one launch (start us, length us, event | category | flops | bytes accessed | tf_op | source)
XLA Modules:
  0.0 381.4 jit_solution(6378152528636089921)
XLA Ops:
  7.2 4.8 %concatenate.24 = bf16[240]{0:T(256)(128)(2,1)S(1)} concatenate(bf16[24]{0:T(256)(128)(2,1)} %param.28, bf16[96]{0:T(256)(128)(2,1)} %param.29, bf16[24]{0:T(256)(128)(2,1)} %param.30, bf16[24]{0:T(256)(128)(2,1)} %param.31, bf16[24]{0:T(256)(128)(2,1)} %param.32, bf16[24]{0:T(256)(128)(2,1)} %param.33, bf16[24]{0:T(256)(128)(2,1)} %param.34), dimensions={0} | concatenate | bytes 960 | tf_op jit(solution)/shard_map/concatenate | solution.py:942
  12.0 1.6 maximum_bitcast_fusion
  13.7 0.7 copy.55
  14.5 0.1 reduce
  14.9 0.8 maximum_bitcast_fusion.1
  15.6 0.6 pad.48.line_ref
  16.2 1.5 pad_maximum_fusion.1.own_ref
  17.7 26.5 %shard_fast.1 = (bf16[3,8,24,768]{3,2,1,0:T(8,128)(2,1)}, bf16[8,8,128]{2,1,0:T(8,128)(2,1)}) custom-call(bf16[3,24,768]{2,1,0:T(8,128)(2,1)} %pad_maximum_fusion.1.own_ref, bf16[8,128]{1,0:T(8,128)(2,1)} %pad.48.line_ref), custom_call_target="tpu_custom_call" | custom-call | flops 10000000000 | bytes 10000000 | tf_op jit(solution)/shard_map/shard_fast/pallas_call | solution.py:887
  44.2 0.7 slice.154
  45.1 0.1 stack.35
  45.3 0.2 convert_reduce_fusion.2
  45.6 0.2 broadcast_in_dim.26.segc_ref
  45.9 1.4 copy-done.1
  47.2 1.4 copy-done.6
  48.6 14.3 %attn_fwd.1 = (bf16[1,1024,192]{2,1,0:T(8,128)(2,1)S(1)}, f32[1,8,1024]{2,1,0:T(8,128)S(1)}) custom-call(s32[2,8]{1,0:T(2,128)S(1)} %pad_add_fusion.bounds, bf16[1024,768]{1,0:T(8,128)(2,1)S(1)} %copy-done.6, bf16[3,192,768]{2,1,0:T(8,128)(2,1)S(1)} %bitcast.71, bf16[3,192,768]{2,1,0:T(8,128)(2,1)S(1)} %bitcast.72, bf16[3,192,768]{2,1,0:T(8,128)(2,1)S(1)} %bitcast.73, ...), custom_call_target="tpu_custom_call" | custom-call | flops 10000000000 | bytes 10000000 | tf_op jit(solution)/shard_map/attn_fwd/pallas_call | solution.py:443
  63.0 0.8 copy-done.7
  63.8 0.6 copy-done.8
  64.4 66.6 %gather_fast.1 = (bf16[4,8,96,768]{3,2,1,0:T(8,128)(2,1)}, bf16[4,8,24,768]{3,2,1,0:T(8,128)(2,1)}, bf16[4,1024,192]{2,1,0:T(8,128)(2,1)}, f32[4,8,1024]{2,1,0:T(8,128)}) custom-call(bf16[96,768]{1,0:T(8,128)(2,1)} %own_ref.1, bf16[24,768]{1,0:T(8,128)(2,1)} %line_ref.1, bf16[1,1024,192]{2,1,0:T(8,128)(2,1)} %copy-done.7, f32[1,8,1024]{2,1,0:T(8,128)} %copy-done.8), custom_call_target="tpu_custom_call" | custom-call | flops 30000001024 | bytes 30000000 | tf_op jit(solution)/shard_map/gather_fast/pallas_call | solution.py:903
  131.0 1.0 pad_maximum_fusion
  132.1 1.1 slice.198
  133.3 0.1 stack_reshape_reshape.18
  133.4 0.1 stack_reshape_reshape.19
  133.5 0.1 stack_reshape_reshape.20
  133.6 0.1 stack_reshape_reshape.21
  133.7 0.1 stack_reshape_reshape.22
  134.0 0.7 pad_convert_fusion.1.eb_ref
  134.7 0.6 pad_convert_fusion.2.vec_ref
  135.3 31.7 %middle.1 = (bf16[1024,768]{1,0:T(8,128)(2,1)}, f32[1024,768]{1,0:T(8,128)}, bf16[4,1024,192]{2,1,0:T(8,128)(2,1)}, bf16[4,192,1024]{2,1,0:T(8,128)(2,1)}, f32[8...) custom-call(s32[1]{0:T(128)} %bitcast.scal, bf16[1024,768]{1,0:T(8,128)(2,1)} %x_ref.5, ...), custom_call_target="tpu_custom_call" | custom-call | flops 49999998976 | bytes 30000000 | tf_op jit(solution)/shard_map/middle/pallas_call | solution.py:393
  167.0 0.7 convert.33
  168.1 0.1 reshape_squeeze.31
  168.4 0.9 slice_reduce_fusion
  169.5 0.1 concatenate.27
  169.7 0.9 pad_dynamic-update-slice_fusion
  170.6 0.7 slice.206
  171.3 0.2 copy.62
  171.5 0.8 copy.59.bias_ref
  172.3 0.7 pad.59.bcol_ref
  173.0 30.1 %attn_bwd.1 = (f32[1024,768]{1,0:T(8,128)}, bf16[4,8,80,768]{3,2,1,0:T(8,128)(2,1)}) custom-call(s32[1]{0:T(128)} %bitcast.scal, s32[2,8]{1,0:T(2,128)} %copy-done.5, bf16[1024,768]{1,0:T(8,128)(2,1)} %x_ref.5, bf16[4,584,768]{2,1,0:T(8,128)(2,1)} %bitcast.87, bf16[4,584,768]{2,1,0:T(8,128)(2,1)} %bitcast.88, bf16[4,584,768]{2,1,0:T(8,128)(2,1)} %bitcast.89, ...), custom_call_target="tpu_custom_call" | custom-call | flops 89999998976 | bytes 30000000 | tf_op jit(solution)/shard_map/attn_bwd/pallas_call | solution.py:468
  203.1 2.1 copy-done
  205.2 158.3 %reduce_fast.1 = f32[80,768]{1,0:T(8,128)S(1)} custom-call(bf16[4,4,2,80,768]{4,3,2,1,0:T(8,128)(2,1)S(1)} %bitcast.70), custom_call_target="tpu_custom_call" | custom-call | tf_op jit(solution)/shard_map/reduce_fast/pallas_call | solution.py:643
  363.6 0.5 slice_bitcast_fusion.10
  364.1 0.7 fusion.10
  364.8 6.5 %reduce-scatter.2.cloned.1.call-done = bf16[1,224,768]{2,1,0:T(8,128)(2,1)} async-done(((bf16[32,224,768]{2,1,0:T(8,128)(2,1)}), bf16[1,224,768]{2,1,0:T(8,128)(2,1)}) %reduce-scatter.2.cloned.1.call-update) | async-done | bytes 344080 | tf_op jit(solution)/shard_map/reduce_scatter | solution.py:927
  371.2 1.1 convert_bitcast_fusion
  372.3 0.8 slice_bitcast_fusion
  373.2 0.6 slice_bitcast_fusion.2
  373.8 0.6 slice_bitcast_fusion.3
  374.4 0.5 slice_bitcast_fusion.8
  (55 shorter events, 2.2 us)
Async XLA Ops:
  7.2 124.9 %all-gather.8.cloned.1.call-start = ((), (), s32[]{:S(2)}) async-start(), calls=%async_computation.3 | async-start | bytes 5271552 | tf_op jit(solution)/shard_map/all_gather | solution.py:922
  13.6 156.9 %all-gather.6.cloned.1.call-start = ((), (), s32[]{:S(2)}) async-start(), calls=%async_computation.2 | async-start | bytes 4485120 | tf_op jit(solution)/shard_map/all_gather | solution.py:995
  45.6 17.4 %copy-start.5 = (s32[2,8]{1,0:T(2,128)}, s32[2,8]{1,0:T(2,128)S(1)}, u32[]{:S(2)}) copy-start(s32[2,8]{1,0:T(2,128)S(1)} %pad_add_fusion.bounds) | copy-start | bytes 196
  45.8 17.1 %copy-start.3 = (s32[1024,128]{1,0:T(8,128)}, s32[1024,128]{1,0:T(8,128)S(1)}, u32[]{:S(2)}) copy-start(s32[1024,128]{1,0:T(8,128)S(1)} %broadcast_in_dim.26.segc_ref) | copy-start | bytes 1572868
  45.8 17.1 %copy-start.4 = (s32[8,1024]{1,0:T(8,128)}, s32[8,1024]{1,0:T(8,128)S(1)}, u32[]{:S(2)}) copy-start(s32[8,1024]{1,0:T(8,128)S(1)} %lt.6.segr_ref) | copy-start | bytes 98308
  45.8 1.4 copy-start.1
  47.2 1.4 copy-start.6
  63.0 0.8 copy-start.7
  63.8 0.6 copy-start.8
  64.4 66.6 %copy-start.2 = (bf16[3,8,24,768]{3,2,1,0:T(8,128)(2,1)S(1)}, bf16[3,8,24,768]{3,2,1,0:T(8,128)(2,1)}, u32[]{:S(2)}) copy-start(bf16[3,8,24,768]{3,2,1,0:T(8,128)(2,1)} %get-tuple-element.38) | copy-start | bytes 2654212
  132.0 239.3 %reduce-scatter.2.cloned.1.call-start = ((), (), s32[]{:S(2)}) async-start(), calls=%async_computation.1 | async-start | bytes 11354112 | tf_op jit(solution)/shard_map/reduce_scatter | solution.py:927
  203.1 2.1 copy-start
Sparse Core Ops, SparseCore 0:
  13.8 72.1 all-gather.7
  132.1 37.5 all-gather.5
  175.6 195.5 reduce-scatter.1

commit v7 on v6

--- a/solution.py
+++ b/solution.py
@@ -13,8 +13,8 @@
 norm_eps = 1e-12
 BF = jnp.bfloat16
 F32 = jnp.float32
-BR = 128
-BC = 256
+BR = 256
+BC = 512
 RT = 256
 MASKED = -1e30
 
@@ -103,7 +103,7 @@
 
 
 def attn_bwd(scal, bounds, x_ref, wq_ref, wk_ref, wv_ref, bias_ref, bcol_ref, segc_ref, segr_ref,
-             ctx_ref, lse_ref, do_ref, dot_ref, s1g_ref,
+             ctx_ref, lse_ref, do_ref, dot_ref, s1g_ref, rest_ref,
              ig_ref, pack_ref,
              q_s, qt_s, k_s, kt_s, vt_s, dq_s, dkt_s, dvt_s, kt_f, vt_f):
     heads = q_s.shape[1] // HEAD_DIM
@@ -180,15 +180,16 @@
 
         x = x_ref[...]
         chunks = pack_ref.shape[1]
-        part = wq.shape[0] // chunks
+        part, extra = wq.shape[0] // chunks, rest_ref.shape[2]
+        pack_ref[0, :, 0:extra, :] = rest_ref[0]
         terms = (tn(dq_s[...], x), nn(dkt_s[...], x), nn(dvt_s[...], x))
         for n, term in enumerate(terms):
-            pack_ref[0, :, n * part : (n + 1) * part, :] = term.astype(BF).reshape(chunks, part, x.shape[1])
+            pack_ref[0, :, extra + n * part : extra + (n + 1) * part, :] = term.astype(BF).reshape(chunks, part, x.shape[1])
         ones = jnp.ones((8, tokens), BF)
-        pack_ref[0, :, 3 * part :, :] = jnp.zeros((chunks, 8, x.shape[1]), BF)
+        pack_ref[0, :, extra + 3 * part :, :] = jnp.zeros((chunks, 8, x.shape[1]), BF)
         for n, line in enumerate((nn(ones, dq_s[...]), nt(ones, dvt_s[...]))):
             for k in range(chunks):
-                pack_ref[0, k, 3 * part :, n * 256 : n * 256 + part] = line[:, k * part : (k + 1) * part].astype(BF)
+                pack_ref[0, k, extra + 3 * part :, n * 256 : n * 256 + part] = line[:, k * part : (k + 1) * part].astype(BF)
 
 
 def normal_parts(value):
@@ -198,7 +199,7 @@
 
 
 def middle(scal, x_ref, ctx_ref, wo_ref, e_hbm, s_hbm, vec_ref, eb_ref, c_ref,
-           lo_ref, s1g_ref, do_ref, dot_ref, vg_ref, ebg_ref, pack_hbm,
+           lo_ref, s1g_ref, do_ref, dot_ref, vg_ref, ebg_ref, pack_hbm, rest_hbm,
            nl_s, n1_s, r1_s, br_s, act_s, gp_s, ug_s, bg_s, stage, sems,
            e_s, s_s, in_sem, dwo_s, dwo_sem, zero_sem):
     tokens, width = x_ref.shape
@@ -287,8 +288,15 @@
     def slot(kind):
         return slice(feat + kind * each, feat + (kind + 1) * each)
 
+    cut = each // 3
+    head = slice(feat + each, feat + each + cut)
+
     def moved(kind, q):
-        return pltpu.make_async_copy(stage.at[kind], pack_hbm.at[q, :, slot(kind), :], sems.at[kind])
+        if kind == 0:
+            return pltpu.make_async_copy(stage.at[0], pack_hbm.at[q, :, slot(0), :], sems.at[0])
+        if kind == 1:
+            return pltpu.make_async_copy(stage.at[1, :, 0:cut, :], pack_hbm.at[q, :, head, :], sems.at[1])
+        return pltpu.make_async_copy(stage.at[1, :, cut:each, :], rest_hbm.at[q], sems.at[2])
 
     def put(kind, n, value):
         count = value.shape[0]
@@ -315,6 +323,7 @@
         def _():
             moved(0, q - 1).wait()
             moved(1, q - 1).wait()
+            moved(2, q - 1).wait()
 
         half = units // 2
         for n in range(2):
@@ -323,6 +332,7 @@
             put(1, n, tn(act_s[q, :, cols], bg_s[...]))
         moved(0, q).start()
         moved(1, q).start()
+        moved(2, q).start()
 
     def first_norm(i, sums):
         r = rows_at(i, RT)
@@ -358,13 +368,14 @@
 
     moved(0, used - 1).wait()
     moved(1, used - 1).wait()
+    moved(2, used - 1).wait()
     stage[0] = jnp.zeros_like(stage[0])
 
     def cleared(q):
         zeros = stage.at[0]
         return (pltpu.make_async_copy(zeros.at[:, 0:feat, :], pack_hbm.at[q, :, 0:feat, :], zero_sem.at[0, q]),
                 pltpu.make_async_copy(zeros, pack_hbm.at[q, :, slot(0), :], zero_sem.at[1, q]),
-                pltpu.make_async_copy(zeros, pack_hbm.at[q, :, slot(1), :], zero_sem.at[2, q]))
+                pltpu.make_async_copy(zeros.at[:, 0:cut, :], pack_hbm.at[q, :, head, :], zero_sem.at[2, q]))
 
     @pl.loop(used, groups)
     def _(q):
@@ -398,15 +409,16 @@
             sds((tokens, width), BF), sds((tokens, width), F32),
             sds((groups, tokens, feat), BF), sds((groups, feat, tokens), BF),
             sds((8, width), F32), sds((groups, 8, width), F32),
-            sds((groups, chunks, part + 2 * each + 8, width), BF)),
+            sds((groups, chunks, part + each + each // 3 + 8, width), BF),
+            sds((groups, chunks, each - each // 3, width), BF)),
         in_specs=[pl.BlockSpec(memory_space=pltpu.SMEM)] + [vm] * 3 + [hbm] * 2 + [vm] * 3,
-        out_specs=(vm,) * 6 + (hbm,),
+        out_specs=(vm,) * 6 + (hbm,) * 2,
         scratch_shapes=[
             pltpu.VMEM((tokens, width), BF), pltpu.VMEM((tokens, width), F32),
             pltpu.VMEM((tokens, 128), F32), pltpu.VMEM((tokens, width), F32),
             pltpu.VMEM((groups, tokens, width), BF), pltpu.VMEM((groups, tokens, width), BF),
             pltpu.VMEM((tokens, width), BF), pltpu.VMEM((tokens, width), BF),
-            pltpu.VMEM((2, chunks, each, width), BF), dma((2,)),
+            pltpu.VMEM((2, chunks, each, width), BF), dma((3,)),
             pltpu.VMEM((groups, chunks, each, width), BF), pltpu.VMEM((groups, chunks, each, width), BF),
             dma((2, groups)), pltpu.VMEM((groups, chunks, part, width), BF), dma((groups,)),
             dma((3, groups))],
@@ -458,9 +470,9 @@
     )(bounds, x, wqkv, wqkv, wqkv, bias, segc, segr)
 
 
-def run_bwd(chunks, scal, bounds, x, wqkv, bias, bcol, segc, segr, ctx, lse, do, dot, s1g):
+def run_bwd(chunks, scal, bounds, x, wqkv, bias, bcol, segc, segr, ctx, lse, do, dot, s1g, rest):
     groups, feat, width = wqkv.shape[0], bias.shape[2], wqkv.shape[2]
-    part = feat // chunks
+    part, extra = feat // chunks, rest.shape[2]
     tokens = x.shape[0]
     heads = feat // HEAD_DIM
     at_quarter, whole = attn_specs(tokens, width, feat)
@@ -469,15 +481,16 @@
         attn_bwd,
         name="attn_bwd",
         cost_estimate=pl.CostEstimate(flops=int(90e9), bytes_accessed=int(30e6), transcendentals=0),
-        out_shape=(sds((tokens, width), F32), sds((groups, chunks, 3 * part + 8, width), BF)),
+        out_shape=(sds((tokens, width), F32), sds((groups, chunks, extra + 3 * part + 8, width), BF)),
         grid_spec=pltpu.PrefetchScalarGridSpec(
             num_scalar_prefetch=2, grid=(groups,),
             in_specs=[whole(tokens, width)] + weight_specs(groups, feat, width)
             + [at_quarter(8, feat), at_quarter(feat, 128), whole(tokens, 128), whole(8, tokens),
                at_quarter(tokens, feat), at_quarter(8, tokens), at_quarter(tokens, feat),
-               at_quarter(feat, tokens), whole(tokens, width)],
+               at_quarter(feat, tokens), whole(tokens, width), pl.BlockSpec(
+                (1, chunks, extra, width), lambda q, s, b: (jnp.minimum(q, s[0]), 0, 0, 0))],
             out_specs=(whole(tokens, width), pl.BlockSpec(
-                (1, chunks, 3 * part + 8, width), lambda q, s, b: (jnp.minimum(q, s[0]), 0, 0, 0))),
+                (1, chunks, extra + 3 * part + 8, width), lambda q, s, b: (jnp.minimum(q, s[0]), 0, 0, 0))),
             scratch_shapes=[
                 pltpu.VMEM((tokens, feat), BF), pltpu.VMEM((feat, tokens), BF),
                 pltpu.VMEM((heads, tokens, feat), BF), pltpu.VMEM((heads, feat, tokens), BF),
@@ -485,7 +498,7 @@
                 pltpu.VMEM((feat, tokens), BF), pltpu.VMEM((feat, tokens), BF),
                 pltpu.VMEM((feat, tokens), F32), pltpu.VMEM((feat, tokens), F32)]),
         compiler_params=pltpu.CompilerParams(vmem_limit_bytes=60 << 20),
-    )(scal, bounds, x, wqkv, wqkv, wqkv, bias, bcol, segc, segr, ctx, lse, do, dot, s1g)
+    )(scal, bounds, x, wqkv, wqkv, wqkv, bias, bcol, segc, segr, ctx, lse, do, dot, s1g, rest)
 
 
 PART = 16
@@ -997,7 +1010,7 @@
     bias = as_bias(qv)
     bcol = jnp.pad(jnp.swapaxes(qv, 1, 2), ((0, 0), (0, 0), (0, 126)))
 
-    result, s1g, do, dot, vg, ebg, first = run_middle(
+    result, s1g, do, dot, vg, ebg, first, rest = run_middle(
         scal, tokens_in, ctx, wo, we, ws, vec, eb, out_grad[0])
     mine = jnp.arange(groups) <= level
 
@@ -1022,17 +1035,21 @@
         return jnp.pad(line[:, :, None, :], ((0, 0), (0, 0), (0, 7), (0, 0)))
 
     line = lined(only(split(ebg[:, 0])), *(split(vg[n]) for n in range(2, 8)))
-    first = parted(first, (owned, owned_ff, owned_ff))
+    if not fast:
+        first = jnp.concatenate([first[:, :, :-8], rest], axis=2)
+        first = parted(first, (owned, owned_ff, owned_ff))
     first = lax.dynamic_update_slice(first, line, (0, 0, first.shape[2] - 8, 0))
     first, s1g = lax.optimization_barrier((first, s1g))
     early = scatter_all(first)
     input_grad, second = run_bwd(
-        chunks, scal, bounds, tokens_in, wqkv, bias, bcol, segc, segr, ctx, lse, do, dot, s1g)
+        chunks, scal, bounds, tokens_in, wqkv, bias, bcol, segc, segr, ctx, lse, do, dot, s1g, rest)
 
     if fast:
         final = reduce_fast(second)
+        shrunk, final = final[: rest.shape[2]], final[rest.shape[2] :]
         late = [final[3 * owned, :owned], final[3 * owned, 256 : 256 + owned]]
     else:
+        second = second[:, :, rest.shape[2] :]
         line = only(jnp.concatenate([split(second[:, 0, 3 * feat, n : n + feat]) for n in (0, 256)], axis=2))
         second = only(parted(second, (owned,) * 3))
         line = jnp.pad(line, ((0, 0), (0, 0), (0, width - line.shape[2])))[:, :, None, :]
@@ -1041,8 +1058,11 @@
         late = [final[3 * owned, :owned], final[3 * owned, owned : 2 * owned]]
     early = early.astype(F32)
     outs = [final[n * owned : (n + 1) * owned] for n in range(3)]
-    outs += [early[:owned], early[owned : owned + owned_ff], early[owned + owned_ff : owned + 2 * owned_ff]]
-    soon = early[owned + 2 * owned_ff]
+    last = early[owned + owned_ff : early.shape[0] - 8]
+    if fast:
+        last = jnp.concatenate([last, shrunk], axis=0)
+    outs += [early[:owned], early[owned : owned + owned_ff], last]
+    soon = early[-8]
     vecs = [soon[owned_ff + n * owned : owned_ff + (n + 1) * owned] for n in range(6)]
     outs += late + [vecs[0], soon[:owned_ff]] + vecs[1:]
     return (result[None], input_grad[None]) + tuple(outs)

time: 382 us -> 379 us (level)
  waiting for transfers between devices: 6.55 us -> 0.3 us
    pallas_call x1, Pallas kernels: 158 us -> 170 us  [reduce_fast(): pl.pallas_call(reduce_kernel, name='reduce_fast', out_shape=jax.ShapeDtyp...]
    reduce_scatter x1, waiting for transfers between devices: 6.46 us -> 0.01 us  [scatter_all(): lax.psum_scatter(flat, ('width', 'tok'), scatter_dimension=0, tiled=True)[0]]
    pallas_call x1, Pallas kernels: 30.1 us -> 25 us  [run_bwd(): pl.pallas_call(attn_bwd, name='attn_bwd', cost_estimate=pl.CostEstimate(f...]
    pallas_call x1, Pallas kernels: 14.3 us -> 10.4 us  [run_fwd(): pl.pallas_call(attn_fwd, name='attn_fwd', cost_estimate=pl.CostEstimate(f...]
  transfers between devices with their start and end apart: 3 -> 3, of which waited for: 1 -> 1; matrix products, arithmetic and copies ran while one was open for 4% -> 4% of each run, Pallas kernels for 86% -> 87%
where the time goes in v7:
time: 379 us; the launch traced here: 378 us
  Pallas kernels  329 us (87%)
  local copies, waits for them, and re-layouts  25.6 us (7%)
  between operations  14.1 us (4%)
  other arithmetic  9.17 us (2%)
    pallas_call x1, Pallas kernels, reduce_fast(): pl.pallas_call(reduce_kernel, name='reduce_fast', out_shape=jax.ShapeDtyp...  170 us
    pallas_call x1, Pallas kernels, gather_fast(): pl.pallas_call(gather_kernel, name='gather_fast', out_shape=(sds((4, 8) +...  66.6 us
    pallas_call x1, Pallas kernels, run_middle(): pl.pallas_call(middle, name='middle', cost_estimate=pl.CostEstimate(flops...  30.4 us
    pallas_call x1, Pallas kernels, shard_fast(): pl.pallas_call(shard_kernel, name='shard_fast', out_shape=(sds((own.shape...  26.5 us
    pallas_call x1, Pallas kernels, run_bwd(): pl.pallas_call(attn_bwd, name='attn_bwd', cost_estimate=pl.CostEstimate(f...  25 us
    pallas_call x1, Pallas kernels, run_fwd(): pl.pallas_call(attn_fwd, name='attn_fwd', cost_estimate=pl.CostEstimate(f...  10.4 us
  transfers between devices with their start and end apart: 3, of which 1 were waited for; matrix products, arithmetic and copies ran while one was open for 4% of the time, Pallas kernels for 87%

profile of v7, /device:TPU:0, one launch (start us, length us, event | category | flops | bytes accessed | tf_op | source)
XLA Modules:
  0.0 378.2 jit_solution(16908037191507011745)
XLA Ops:
  7.2 4.8 %concatenate.27 = bf16[240]{0:T(256)(128)(2,1)S(1)} concatenate(bf16[24]{0:T(256)(128)(2,1)} %param.28, bf16[96]{0:T(256)(128)(2,1)} %param.29, bf16[24]{0:T(256)(128)(2,1)} %param.30, bf16[24]{0:T(256)(128)(2,1)} %param.31, bf16[24]{0:T(256)(128)(2,1)} %param.32, bf16[24]{0:T(256)(128)(2,1)} %param.33, bf16[24]{0:T(256)(128)(2,1)} %param.34), dimensions={0} | concatenate | bytes 960 | tf_op jit(solution)/shard_map/concatenate | solution.py:955
  12.0 1.6 maximum_bitcast_fusion
  13.7 0.7 copy.55
  14.5 0.1 reduce
  14.9 0.8 maximum_bitcast_fusion.1
  15.6 0.6 pad.48.line_ref
  16.2 1.5 pad_maximum_fusion.2.own_ref
  17.7 26.5 %shard_fast.1 = (bf16[3,8,24,768]{3,2,1,0:T(8,128)(2,1)}, bf16[8,8,128]{2,1,0:T(8,128)(2,1)}) custom-call(bf16[3,24,768]{2,1,0:T(8,128)(2,1)} %pad_maximum_fusion.2.own_ref, bf16[8,128]{1,0:T(8,128)(2,1)} %pad.48.line_ref), custom_call_target="tpu_custom_call" | custom-call | flops 10000000000 | bytes 10000000 | tf_op jit(solution)/shard_map/shard_fast/pallas_call | solution.py:900
  44.1 0.7 slice.163
  45.1 0.1 stack.34
  45.3 0.2 convert_reduce_fusion.2
  45.6 0.2 broadcast_in_dim.50.segc_ref
  45.8 1.4 copy-done.1
  47.2 1.4 copy-done.6
  48.6 10.4 %attn_fwd.1 = (bf16[1,1024,192]{2,1,0:T(8,128)(2,1)S(1)}, f32[1,8,1024]{2,1,0:T(8,128)S(1)}) custom-call(s32[2,4]{1,0:T(2,128)S(1)} %pad_add_fusion.bounds, bf16[1024,768]{1,0:T(8,128)(2,1)S(1)} %copy-done.6, bf16[3,192,768]{2,1,0:T(8,128)(2,1)S(1)} %bitcast.71, bf16[3,192,768]{2,1,0:T(8,128)(2,1)S(1)} %bitcast.72, bf16[3,192,768]{2,1,0:T(8,128)(2,1)S(1)} %bitcast.73, ...), custom_call_target="tpu_custom_call" | custom-call | flops 10000000000 | bytes 10000000 | tf_op jit(solution)/shard_map/attn_fwd/pallas_call | solution.py:455
  59.1 0.8 copy-done.7
  59.9 0.6 copy-done.8
  60.5 66.6 %gather_fast.1 = (bf16[4,8,96,768]{3,2,1,0:T(8,128)(2,1)}, bf16[4,8,24,768]{3,2,1,0:T(8,128)(2,1)}, bf16[4,1024,192]{2,1,0:T(8,128)(2,1)}, f32[4,8,1024]{2,1,0:T(8,128)}) custom-call(bf16[96,768]{1,0:T(8,128)(2,1)} %own_ref.1, bf16[24,768]{1,0:T(8,128)(2,1)} %line_ref.1, bf16[1,1024,192]{2,1,0:T(8,128)(2,1)} %copy-done.7, f32[1,8,1024]{2,1,0:T(8,128)} %copy-done.8), custom_call_target="tpu_custom_call" | custom-call | flops 30000001024 | bytes 30000000 | tf_op jit(solution)/shard_map/gather_fast/pallas_call | solution.py:916
  127.1 1.0 pad_maximum_fusion
  128.2 1.1 slice.208
  129.4 0.1 stack_reshape_reshape.18
  129.5 0.1 stack_reshape_reshape.19
  129.6 0.1 stack_reshape_reshape.20
  129.9 0.1 stack_reshape_reshape.23
  130.1 0.7 pad_convert_fusion.1.eb_ref
  130.8 0.6 pad_convert_fusion.2.vec_ref
  131.4 30.4 %middle.1 = (bf16[1024,768]{1,0:T(8,128)(2,1)}, f32[1024,768]{1,0:T(8,128)}, bf16[4,1024,192]{2,1,0:T(8,128)(2,1)}, bf16[4,192,1024]{2,1,0:T(8,128)(2,1)}, f32[8...) custom-call(s32[1]{0:T(128)} %bitcast.scal, ...), custom_call_target="tpu_custom_call" | custom-call | flops 49999998976 | bytes 30000000 | tf_op jit(solution)/shard_map/middle/pallas_call | solution.py:404
  161.9 0.9 slice_reduce_fusion
  162.9 0.7 convert.33
  164.2 0.1 reshape_squeeze.33
  164.4 0.1 concatenate.30
  164.6 0.9 pad_dynamic-update-slice_fusion
  165.5 0.2 all-gather.6.cloned.1.call-done
  165.7 0.7 slice.216
  166.5 0.2 copy.62
  166.7 0.8 copy.59.bias_ref
  167.5 0.7 pad.59.bcol_ref
  168.2 25.0 %attn_bwd.1 = (f32[1024,768]{1,0:T(8,128)}, bf16[4,8,144,768]{3,2,1,0:T(8,128)(2,1)}) custom-call(s32[1]{0:T(128)} %bitcast.scal, s32[2,4]{1,0:T(2,128)} %copy-done.5, bf16[1024,768]{1,0:T(8,128)(2,1)} %x_ref.5, bf16[4,584,768]{2,1,0:T(8,128)(2,1)} %bitcast.87, bf16[4,584,768]{2,1,0:T(8,128)(2,1)} %bitcast.88, bf16[4,584,768]{2,1,0:T(8,128)(2,1)} %bitcast.89, ...), custom_call_target="tpu_custom_call" | custom-call | flops 89999998976 | bytes 30000000 | tf_op jit(solution)/shard_map/attn_bwd/pallas_call | solution.py:480
  193.3 3.0 copy-done
  196.3 170.0 %reduce_fast.1 = f32[144,768]{1,0:T(8,128)S(1)} custom-call(bf16[4,4,2,144,768]{4,3,2,1,0:T(8,128)(2,1)S(1)} %bitcast.70), custom_call_target="tpu_custom_call" | custom-call | tf_op jit(solution)/shard_map/reduce_fast/pallas_call | solution.py:656
  366.3 0.5 slice_bitcast_fusion.10
  366.8 0.7 fusion.10
  367.5 1.0 convert_bitcast_fusion
  368.5 0.6 slice_bitcast_fusion.2
  369.1 0.7 slice_bitcast_fusion
  369.9 0.6 slice_bitcast_fusion.3
  370.5 0.5 slice_bitcast_fusion.8
  371.0 0.7 pad_maximum_fusion.1
  (58 shorter events, 2.2 us)
Async XLA Ops:
  7.2 121.0 %all-gather.8.cloned.1.call-start = ((), (), s32[]{:S(2)}) async-start(), calls=%async_computation.3 | async-start | bytes 5271552 | tf_op jit(solution)/shard_map/all_gather | solution.py:935
  13.6 152.1 %all-gather.6.cloned.1.call-start = ((), (), s32[]{:S(2)}) async-start(), calls=%async_computation.2 | async-start | bytes 4485120 | tf_op jit(solution)/shard_map/all_gather | solution.py:1008
  45.6 13.5 %copy-start.5 = (s32[2,4]{1,0:T(2,128)}, s32[2,4]{1,0:T(2,128)S(1)}, u32[]{:S(2)}) copy-start(s32[2,4]{1,0:T(2,128)S(1)} %pad_add_fusion.bounds) | copy-start | bytes 100
  45.8 13.3 %copy-start.3 = (s32[1024,128]{1,0:T(8,128)}, s32[1024,128]{1,0:T(8,128)S(1)}, u32[]{:S(2)}) copy-start(s32[1024,128]{1,0:T(8,128)S(1)} %broadcast_in_dim.50.segc_ref) | copy-start | bytes 1572868
  45.8 1.4 copy-start.1
  47.2 1.4 copy-start.6
  48.6 10.5 %copy-start.4 = (s32[8,1024]{1,0:T(8,128)}, s32[8,1024]{1,0:T(8,128)S(1)}, u32[]{:S(2)}) copy-start(s32[8,1024]{1,0:T(8,128)S(1)} %broadcast_in_dim.51.segr_ref) | copy-start | bytes 98308
  59.1 0.8 copy-start.7
  59.9 0.6 copy-start.8
  60.5 66.6 %copy-start.2 = (bf16[3,8,24,768]{3,2,1,0:T(8,128)(2,1)S(1)}, bf16[3,8,24,768]{3,2,1,0:T(8,128)(2,1)}, u32[]{:S(2)}) copy-start(bf16[3,8,24,768]{3,2,1,0:T(8,128)(2,1)} %get-tuple-element.39) | copy-start | bytes 2654212
  128.1 239.4 %reduce-scatter.2.cloned.1.call-start = ((), (), s32[]{:S(2)}) async-start(), calls=%async_computation.1 | async-start | bytes 8110080 | tf_op jit(solution)/shard_map/reduce_scatter | solution.py:940
  193.2 3.0 copy-start
Sparse Core Ops, SparseCore 0:
  13.8 72.3 all-gather.7
  128.2 37.4 all-gather.5
  171.4 174.6 reduce-scatter.1

commit v8 on v7

--- a/solution.py
+++ b/solution.py
@@ -13,9 +13,10 @@
 norm_eps = 1e-12
 BF = jnp.bfloat16
 F32 = jnp.float32
-BR = 256
+BR = 512
 BC = 512
-RT = 256
+RT = 512
+MT = 512
 MASKED = -1e30
 
 
@@ -223,7 +224,7 @@
     def s_at(q):
         return s_s[q].reshape(units, width)
 
-    tiles = tokens // RT
+    tiles = tokens // MT
     ob, sb = vec_ref[2:3, :], vec_ref[3:4, :]
     g1, b1 = vec_ref[4:5, :], vec_ref[5:6, :]
     g2, b2 = vec_ref[6:7, :], vec_ref[7:8, :]
@@ -233,15 +234,15 @@
 
     @pl.loop(0, tiles)
     def _(i):
-        r = rows_at(i, RT)
+        r = rows_at(i, MT)
         total = lax.fori_loop(
-            0, used, lambda q, t: t + nn(ctx_ref[q, r, :], wo_ref[q]), jnp.zeros((RT, width), F32))
+            0, used, lambda q, t: t + nn(ctx_ref[q, r, :], wo_ref[q]), jnp.zeros((MT, width), F32))
         v = x_ref[r, :].astype(F32) + (total + ob)
         v = v - mean(v)
         rstd = lax.rsqrt(mean(v * v) + norm_eps)
         n = v * rstd
         n1_s[r, :] = n
-        r1_s[r, :] = jnp.broadcast_to(rstd, (RT, 128))
+        r1_s[r, :] = jnp.broadcast_to(rstd, (MT, 128))
         normed = n * g1 + b1
         nl_s[r, :] = normed.astype(BF)
         br_s[r, :] = normed + sb
@@ -253,7 +254,7 @@
 
         @pl.loop(0, tiles)
         def _(i):
-            r = rows_at(i, RT)
+            r = rows_at(i, MT)
             u = nt(nl_s[r, :], e_at(q)) + eb_ref[q, 0:1, :]
             cum, phi = normal_parts(u)
             act = (u * cum).astype(BF)
@@ -264,7 +265,7 @@
     zero = jnp.zeros((1, width), F32)
 
     def second_norm(i, sums):
-        r = rows_at(i, RT)
+        r = rows_at(i, MT)
         v = br_s[r, :]
         v = v - mean(v)
         rstd = lax.rsqrt(mean(v * v) + norm_eps)
@@ -288,7 +289,7 @@
     def slot(kind):
         return slice(feat + kind * each, feat + (kind + 1) * each)
 
-    cut = each // 3
+    cut = each // 2
     head = slice(feat + each, feat + each + cut)
 
     def moved(kind, q):
@@ -310,7 +311,7 @@
     @pl.loop(0, used)
     def _(q):
         def tile(i, total):
-            r = rows_at(i, RT)
+            r = rows_at(i, MT)
             d = nt(bg_s[r, :], s_at(q)) * gp_s[q, r, :].astype(F32)
             ug = d.astype(BF)
             ug_s[r, :] = ug
@@ -335,7 +336,7 @@
         moved(2, q).start()
 
     def first_norm(i, sums):
-        r = rows_at(i, RT)
+        r = rows_at(i, MT)
         g = s1g_ref[r, :]
         n = n1_s[r, :]
         m = g * g1
@@ -409,8 +410,8 @@
             sds((tokens, width), BF), sds((tokens, width), F32),
             sds((groups, tokens, feat), BF), sds((groups, feat, tokens), BF),
             sds((8, width), F32), sds((groups, 8, width), F32),
-            sds((groups, chunks, part + each + each // 3 + 8, width), BF),
-            sds((groups, chunks, each - each // 3, width), BF)),
+            sds((groups, chunks, part + each + each // 2 + 8, width), BF),
+            sds((groups, chunks, each - each // 2, width), BF)),
         in_specs=[pl.BlockSpec(memory_space=pltpu.SMEM)] + [vm] * 3 + [hbm] * 2 + [vm] * 3,
         out_specs=(vm,) * 6 + (hbm,) * 2,
         scratch_shapes=[
@@ -422,7 +423,7 @@
             pltpu.VMEM((groups, chunks, each, width), BF), pltpu.VMEM((groups, chunks, each, width), BF),
             dma((2, groups)), pltpu.VMEM((groups, chunks, part, width), BF), dma((groups,)),
             dma((3, groups))],
-        compiler_params=pltpu.CompilerParams(vmem_limit_bytes=62 << 20),
+        compiler_params=pltpu.CompilerParams(vmem_limit_bytes=67043328),
     )(scal, x, ctx, wo, e, s, vec, eb, cot)
 
 

time: 379 us -> 363 us (0.958)
  Pallas kernels: 329 us -> 313 us
    pallas_call x1, Pallas kernels: 170 us -> 157 us  [reduce_fast(): pl.pallas_call(reduce_kernel, name='reduce_fast', out_shape=jax.ShapeDtyp...]
  transfers between devices with their start and end apart: 3 -> 3, of which waited for: 1 -> 1; matrix products, arithmetic and copies ran while one was open for 4% -> 5% of each run, Pallas kernels for 87% -> 86%
where the time goes in v8:
time: 363 us; the launch traced here: 362 us
  Pallas kernels  313 us (86%)
  local copies, waits for them, and re-layouts  23.9 us (7%)
  between operations  14.1 us (4%)
  other arithmetic  10.4 us (3%)
    pallas_call x1, Pallas kernels, reduce_fast(): pl.pallas_call(reduce_kernel, name='reduce_fast', out_shape=jax.ShapeDtyp...  157 us
    pallas_call x1, Pallas kernels, gather_fast(): pl.pallas_call(gather_kernel, name='gather_fast', out_shape=(sds((4, 8) +...  66.6 us
    pallas_call x1, Pallas kernels, run_middle(): pl.pallas_call(middle, name='middle', cost_estimate=pl.CostEstimate(flops...  29 us
    pallas_call x1, Pallas kernels, shard_fast(): pl.pallas_call(shard_kernel, name='shard_fast', out_shape=(sds((own.shape...  26.5 us
    pallas_call x1, Pallas kernels, run_bwd(): pl.pallas_call(attn_bwd, name='attn_bwd', cost_estimate=pl.CostEstimate(f...  23.5 us
    pallas_call x1, Pallas kernels, run_fwd(): pl.pallas_call(attn_fwd, name='attn_fwd', cost_estimate=pl.CostEstimate(f...  9.91 us
  transfers between devices with their start and end apart: 3, of which 1 were waited for; matrix products, arithmetic and copies ran while one was open for 5% of the time, Pallas kernels for 86%

profile of v8, /device:TPU:0, one launch (start us, length us, event | category | flops | bytes accessed | tf_op | source)
XLA Modules:
  0.0 362.1 jit_solution(9958195652622714147)
XLA Ops:
  7.2 4.8 %concatenate.27 = bf16[240]{0:T(256)(128)(2,1)S(1)} concatenate(bf16[24]{0:T(256)(128)(2,1)} %param.28, bf16[96]{0:T(256)(128)(2,1)} %param.29, bf16[24]{0:T(256)(128)(2,1)} %param.30, bf16[24]{0:T(256)(128)(2,1)} %param.31, bf16[24]{0:T(256)(128)(2,1)} %param.32, bf16[24]{0:T(256)(128)(2,1)} %param.33, bf16[24]{0:T(256)(128)(2,1)} %param.34), dimensions={0} | concatenate | bytes 960 | tf_op jit(solution)/shard_map/concatenate | solution.py:956
  12.0 1.6 maximum_bitcast_fusion
  13.7 0.7 copy.55
  14.5 0.1 reduce
  14.9 0.7 maximum_bitcast_fusion.1
  15.6 0.6 pad.48.line_ref
  16.2 1.5 pad_maximum_fusion.2.own_ref
  17.7 26.5 %shard_fast.1 = (bf16[3,8,24,768]{3,2,1,0:T(8,128)(2,1)}, bf16[8,8,128]{2,1,0:T(8,128)(2,1)}) custom-call(bf16[3,24,768]{2,1,0:T(8,128)(2,1)} %pad_maximum_fusion.2.own_ref, bf16[8,128]{1,0:T(8,128)(2,1)} %pad.48.line_ref), custom_call_target="tpu_custom_call" | custom-call | flops 10000000000 | bytes 10000000 | tf_op jit(solution)/shard_map/shard_fast/pallas_call | solution.py:901
  44.1 0.7 slice.163
  45.1 0.1 stack.34
  45.3 0.2 fusion.6
  45.6 0.2 broadcast_in_dim.50.segc_ref
  45.8 1.3 copy-done.1
  47.2 9.9 %attn_fwd.1 = (bf16[1,1024,192]{2,1,0:T(8,128)(2,1)S(1)}, f32[1,8,1024]{2,1,0:T(8,128)S(1)}) custom-call(s32[2,2]{1,0:T(2,128)S(1)} %pad_add_fusion.bounds, bf16[1024,768]{1,0:T(8,128)(2,1)S(1)} %copy-done.6, bf16[3,192,768]{2,1,0:T(8,128)(2,1)S(1)} %bitcast.71, bf16[3,192,768]{2,1,0:T(8,128)(2,1)S(1)} %bitcast.72, bf16[3,192,768]{2,1,0:T(8,128)(2,1)S(1)} %bitcast.73, ...), custom_call_target="tpu_custom_call" | custom-call | flops 10000000000 | bytes 10000000 | tf_op jit(solution)/shard_map/attn_fwd/pallas_call | solution.py:456
  57.2 0.8 copy-done.7
  57.9 0.6 copy-done.8
  58.6 66.6 %gather_fast.1 = (bf16[4,8,96,768]{3,2,1,0:T(8,128)(2,1)}, bf16[4,8,24,768]{3,2,1,0:T(8,128)(2,1)}, bf16[4,1024,192]{2,1,0:T(8,128)(2,1)}, f32[4,8,1024]{2,1,0:T(8,128)}) custom-call(bf16[96,768]{1,0:T(8,128)(2,1)} %own_ref.1, bf16[24,768]{1,0:T(8,128)(2,1)} %line_ref.1, bf16[1,1024,192]{2,1,0:T(8,128)(2,1)} %copy-done.7, f32[1,8,1024]{2,1,0:T(8,128)} %copy-done.8), custom_call_target="tpu_custom_call" | custom-call | flops 30000001024 | bytes 30000000 | tf_op jit(solution)/shard_map/gather_fast/pallas_call | solution.py:917
  125.2 1.0 pad_maximum_fusion
  126.2 0.5 iota_compare_fusion.4
  126.7 1.0 slice.208
  128.0 0.1 stack_reshape_reshape.18
  128.1 0.1 stack_reshape_reshape.19
  128.2 0.1 stack_reshape_reshape.20
  128.3 0.1 stack_reshape_reshape.21
  128.6 0.7 pad_convert_fusion.1.eb_ref
  129.4 0.6 pad_convert_fusion.2.vec_ref
  130.0 29.0 %middle.1 = (bf16[1024,768]{1,0:T(8,128)(2,1)}, f32[1024,768]{1,0:T(8,128)}, bf16[4,1024,192]{2,1,0:T(8,128)(2,1)}, bf16[4,192,1024]{2,1,0:T(8,128)(2,1)}, f32[8...) custom-call(s32[1]{0:T(128)} %bitcast.scal, ...), custom_call_target="tpu_custom_call" | custom-call | flops 49999998976 | bytes 30000000 | tf_op jit(solution)/shard_map/middle/pallas_call | solution.py:405
  159.0 0.9 slice_reduce_fusion
  160.0 0.7 convert.33
  161.4 0.7 select_convert_fusion
  162.1 0.1 concatenate.30
  162.3 0.9 pad_dynamic-update-slice_fusion
  163.2 0.6 all-gather.6.cloned.1.call-done
  163.8 0.7 slice.216
  164.5 0.2 copy.62
  164.8 0.8 copy.59.bias_ref
  165.6 0.7 pad.59.bcol_ref
  166.3 23.5 %attn_bwd.1 = (f32[1024,768]{1,0:T(8,128)}, bf16[4,8,128,768]{3,2,1,0:T(8,128)(2,1)}) custom-call(s32[1]{0:T(128)} %bitcast.scal, s32[2,2]{1,0:T(2,128)} %copy-done.5, bf16[1024,768]{1,0:T(8,128)(2,1)} %x_ref.5, bf16[4,584,768]{2,1,0:T(8,128)(2,1)} %bitcast.87, bf16[4,584,768]{2,1,0:T(8,128)(2,1)} %bitcast.88, bf16[4,584,768]{2,1,0:T(8,128)(2,1)} %bitcast.89, ...), custom_call_target="tpu_custom_call" | custom-call | flops 89999998976 | bytes 30000000 | tf_op jit(solution)/shard_map/attn_bwd/pallas_call | solution.py:481
  189.8 2.8 copy-done
  192.6 157.5 %reduce_fast.1 = f32[128,768]{1,0:T(8,128)S(1)} custom-call(bf16[4,4,2,128,768]{4,3,2,1,0:T(8,128)(2,1)S(1)} %bitcast.70), custom_call_target="tpu_custom_call" | custom-call | tf_op jit(solution)/shard_map/reduce_fast/pallas_call | solution.py:657
  350.1 0.5 slice_bitcast_fusion.10
  350.6 0.7 fusion.12
  351.3 1.0 convert_bitcast_fusion
  352.3 0.6 slice_bitcast_fusion.2
  352.9 0.7 slice_bitcast_fusion
  353.7 0.6 slice_bitcast_fusion.3
  354.3 0.5 slice_bitcast_fusion.8
  354.8 0.7 pad_maximum_fusion.1
  (58 shorter events, 2.2 us)
Async XLA Ops:
  7.2 119.5 %all-gather.8.cloned.1.call-start = ((), (), s32[]{:S(2)}) async-start(), calls=%async_computation.3 | async-start | bytes 5271552 | tf_op jit(solution)/shard_map/all_gather | solution.py:936
  13.6 150.2 %all-gather.6.cloned.1.call-start = ((), (), s32[]{:S(2)}) async-start(), calls=%async_computation.2 | async-start | bytes 4485120 | tf_op jit(solution)/shard_map/all_gather | solution.py:1009
  17.6 28.2 %copy-start.6 = (bf16[1024,768]{1,0:T(8,128)(2,1)S(1)}, bf16[1024,768]{1,0:T(8,128)(2,1)}, u32[]{:S(2)}) copy-start(bf16[1024,768]{1,0:T(8,128)(2,1)} %x_ref.5) | copy-start | bytes 4718596
  45.6 11.5 %copy-start.5 = (s32[2,2]{1,0:T(2,128)}, s32[2,2]{1,0:T(2,128)S(1)}, u32[]{:S(2)}) copy-start(s32[2,2]{1,0:T(2,128)S(1)} %pad_add_fusion.bounds) | copy-start | bytes 52
  45.8 11.3 %copy-start.3 = (s32[1024,128]{1,0:T(8,128)}, s32[1024,128]{1,0:T(8,128)S(1)}, u32[]{:S(2)}) copy-start(s32[1024,128]{1,0:T(8,128)S(1)} %broadcast_in_dim.50.segc_ref) | copy-start | bytes 1572868
  45.8 1.4 copy-start.1
  47.2 9.9 %copy-start.4 = (s32[8,1024]{1,0:T(8,128)}, s32[8,1024]{1,0:T(8,128)S(1)}, u32[]{:S(2)}) copy-start(s32[8,1024]{1,0:T(8,128)S(1)} %broadcast_in_dim.51.segr_ref) | copy-start | bytes 98308
  57.1 0.8 copy-start.7
  57.9 0.6 copy-start.8
  58.6 66.6 %copy-start.2 = (bf16[3,8,24,768]{3,2,1,0:T(8,128)(2,1)S(1)}, bf16[3,8,24,768]{3,2,1,0:T(8,128)(2,1)}, u32[]{:S(2)}) copy-start(bf16[3,8,24,768]{3,2,1,0:T(8,128)(2,1)} %get-tuple-element.39) | copy-start | bytes 2654212
  126.2 225.1 %reduce-scatter.2.cloned.1.call-start = ((), (), s32[]{:S(2)}) async-start(), calls=%async_computation.1 | async-start | bytes 8921088 | tf_op jit(solution)/shard_map/reduce_scatter | solution.py:941
  189.8 2.8 copy-start
Sparse Core Ops, SparseCore 0:
  13.8 72.1 all-gather.7
  126.3 37.4 all-gather.5
  169.7 177.0 reduce-scatter.1
